TPU v7x, 32 devices: a whole 2x2x4 slice. The times are simulated.
32 devices in a mesh: rows: 8 (over z, core), seq: 4 (over y, x).
Axes of the slice: x: 2, y: 2, z: 4, core: 2. Of those that a mesh axis runs over, the one named last changes fastest.
Arguments:
- tokens: bfloat16 [16, 2048, 1152], P('rows', 'seq'), may hold values from -6 to 6
- picture_ids: int32 [16, 2048], P('rows'), may hold values from -1 to 19, as said below
- attn_gain: bfloat16 [1152], P('rows'), may hold values from 0.099609375 to 1.8984375
- attn_shift: bfloat16 [1152], P('rows'), may hold values from -3 to 3
- query_weight: bfloat16 [1152, 1152], P('rows'), may hold values from -0.1875 to 0.1875
- query_bias: bfloat16 [1152], P('rows'), may hold values from -3 to 3
- key_weight: bfloat16 [1152, 1152], P('rows'), may hold values from -0.1875 to 0.1875
- value_weight: bfloat16 [1152, 1152], P('rows'), may hold values from -0.1875 to 0.1875
- value_bias: bfloat16 [1152], P('rows'), may hold values from -3 to 3
- output_weight: bfloat16 [1152, 1152], P('rows'), may hold values from -2 to 2
- output_bias: bfloat16 [1152], P('rows'), may hold values from -3 to 3
- mlp_gain: bfloat16 [1152], P('rows'), may hold values from 0.099609375 to 1.8984375
- mlp_shift: bfloat16 [1152], P('rows'), may hold values from -3 to 3
- up_weight: bfloat16 [1152, 4304], P('rows'), may hold values from -0.1875 to 0.1875
- up_bias: bfloat16 [4304], P('rows'), may hold values from -3 to 3
- down_weight: bfloat16 [4304, 1152], P(None, 'rows'), may hold values from -0.09375 to 0.09375
- down_bias: bfloat16 [1152], P('rows'), may hold values from -3 to 3
- cotangent: bfloat16 [16, 2048, 1152], P('rows', 'seq'), may hold values from -6 to 6
Outputs:
- activations: float32 [16, 2048, 1152], P('rows', 'seq')
- token_grad: float32 [16, 2048, 1152], P('rows', 'seq')
- grad_attn_gain: float32 [1152], P('rows')
- grad_attn_shift: float32 [1152], P('rows')
- grad_query_weight: float32 [1152, 1152], P('rows')
- grad_query_bias: float32 [1152], P('rows')
- grad_key_weight: float32 [1152, 1152], P('rows')
- grad_value_weight: float32 [1152, 1152], P('rows')
- grad_value_bias: float32 [1152], P('rows')
- grad_output_weight: float32 [1152, 1152], P('rows')
- grad_output_bias: float32 [1152], P('rows')
- grad_mlp_gain: float32 [1152], P('rows')
- grad_mlp_shift: float32 [1152], P('rows')
- grad_up_weight: float32 [1152, 4304], P('rows')
- grad_up_bias: float32 [4304], P('rows')
- grad_down_weight: float32 [4304, 1152], P(None, 'rows')
- grad_down_bias: float32 [1152], P('rows')
Inputs may be any that keep to these rules, and one draw needn't show every extreme that they name: `picture_ids`: each row of 2048 slots holds whole pictures of 100 to 1024 patches, numbered 0, 1, 2, ... from the row's start, then pad slots numbered -1 to the row's end. The first row begins with a picture of exactly 1024 patches; the last row holds 20 pictures of exactly 100 patches, then pads.
All inputs are finite; a program needn't handle non-finite values.
Results may differ from a plain program's by a relative error of at most 0.019.
Values may be sent and summed in bfloat16 or wider, within the bound.
A program may use at most 256 MiB of HBM per device.

v0:
```python
import jax
import jax.numpy as jnp
from jax import lax
from jax.sharding import PartitionSpec as P

ATTENTION_HEADS = 16
HEAD_SIZE = 72
MICRO = 2
ROWS_MB = 1


EPS = 1e-06
NEGATIVE = -1e30


def norm_apply(value_rows, gain, shift):
    center = value_rows - jnp.mean(value_rows, axis=-1, keepdims=True)
    spread = jnp.mean(center * center, axis=-1, keepdims=True)
    return center * lax.rsqrt(spread + EPS) * gain + shift


def gelu_tanh(value_rows):
    return jax.nn.gelu(value_rows, approximate=True)


def split_heads(packed):
    return (
        packed[..., :HEAD_SIZE],
        packed[..., HEAD_SIZE : 2 * HEAD_SIZE],
        packed[..., 2 * HEAD_SIZE :],
    )


def block_scores(query_block, id_block, key_rows, picture_of_row):
    scores = jnp.einsum(
        "qhd,khd->hqk", query_block, key_rows, preferred_element_type=jnp.float32
    ) * HEAD_SIZE ** (-0.5)
    allowed = (id_block[:, None] == picture_of_row[None, :])[None]
    return jnp.where(allowed, scores, NEGATIVE)


def attend_row(packed, picture_of_row):
    query_rows, key_rows, value_rows = split_heads(packed)
    length = packed.shape[0]
    tile_block = min(512, length)

    def one_block(start):
        query_block = lax.dynamic_slice_in_dim(query_rows, start, tile_block, 0)
        id_block = lax.dynamic_slice_in_dim(picture_of_row, start, tile_block, 0)
        scores = block_scores(query_block, id_block, key_rows, picture_of_row)
        highest = jnp.max(scores, axis=-1, keepdims=True)
        expo = jnp.exp(scores - highest)
        total = jnp.sum(expo, axis=-1, keepdims=True)
        probs = (expo / total).astype(jnp.bfloat16)
        mixed_heads = jnp.einsum(
            "hqk,khd->qhd", probs, value_rows, preferred_element_type=jnp.float32
        )
        return (mixed_heads.astype(jnp.bfloat16), (highest + jnp.log(total))[..., 0])

    starts = jnp.arange(length // tile_block, dtype=jnp.int32) * tile_block
    mixed_heads, logsum = lax.map(one_block, starts)
    return (mixed_heads.reshape(length, mixed_heads.shape[2], mixed_heads.shape[3]), logsum)


def attend_back(packed, grad_mixed, logsum, picture_of_row):
    query_rows, key_rows, value_rows = split_heads(packed)
    length = packed.shape[0]
    tile_block = min(512, length)
    factor = HEAD_SIZE ** (-0.5)

    def one_block(carry, inputs):
        grad_keys, grad_values = carry
        start, logsum_block = inputs
        query_block = lax.dynamic_slice_in_dim(query_rows, start, tile_block, 0)
        id_block = lax.dynamic_slice_in_dim(picture_of_row, start, tile_block, 0)
        grad_block = lax.dynamic_slice_in_dim(grad_mixed, start, tile_block, 0)
        scores = block_scores(query_block, id_block, key_rows, picture_of_row)
        probs = jnp.exp(scores - logsum_block[..., None])
        grad_probs = jnp.einsum(
            "qhd,khd->hqk", grad_block, value_rows, preferred_element_type=jnp.float32
        )
        inner = jnp.sum(probs * grad_probs, axis=-1, keepdims=True)
        grad_scores = (probs * (grad_probs - inner)).astype(jnp.bfloat16)
        grad_query = (
            jnp.einsum("hqk,khd->qhd", grad_scores, key_rows, preferred_element_type=jnp.float32)
            * factor
        )
        grad_keys = (
            grad_keys
            + jnp.einsum(
                "hqk,qhd->khd", grad_scores, query_block, preferred_element_type=jnp.float32
            )
            * factor
        )
        grad_values = grad_values + jnp.einsum(
            "hqk,qhd->khd",
            probs.astype(jnp.bfloat16),
            grad_block,
            preferred_element_type=jnp.float32,
        )
        return ((grad_keys, grad_values), grad_query.astype(jnp.bfloat16))

    zeros = jnp.zeros(key_rows.shape, jnp.float32)
    starts = jnp.arange(length // tile_block, dtype=jnp.int32) * tile_block
    (grad_keys, grad_values), grad_queries = lax.scan(one_block, (zeros, zeros), (starts, logsum))
    grad_queries = grad_queries.reshape(key_rows.shape)
    return jnp.concatenate(
        [grad_queries, grad_keys.astype(jnp.bfloat16), grad_values.astype(jnp.bfloat16)], axis=-1
    )


def forward_micro(token_rows, id_rows, whole):
    (
        first_gain,
        first_shift,
        query_matrix,
        query_offset,
        key_matrix,
        value_matrix,
        value_offset,
        output_matrix,
        output_offset,
        second_gain,
        second_shift,
        up_matrix,
        up_offset,
        down_matrix,
        down_offset,
    ) = whole
    count, piece, width = token_rows.shape
    inputs = token_rows.astype(jnp.float32)
    attn_input = norm_apply(
        inputs, first_gain.astype(jnp.float32), first_shift.astype(jnp.float32)
    ).astype(jnp.bfloat16)
    query_rows = (
        jnp.einsum("rpd,de->rpe", attn_input, query_matrix, preferred_element_type=jnp.float32)
        + query_offset.astype(jnp.float32)
    ).astype(jnp.bfloat16)
    key_rows = jnp.einsum(
        "rpd,de->rpe", attn_input, key_matrix, preferred_element_type=jnp.float32
    ).astype(jnp.bfloat16)
    value_rows = (
        jnp.einsum("rpd,de->rpe", attn_input, value_matrix, preferred_element_type=jnp.float32)
        + value_offset.astype(jnp.float32)
    ).astype(jnp.bfloat16)
    packed = jnp.concatenate(
        [
            query_rows.reshape(count, piece, ATTENTION_HEADS, HEAD_SIZE),
            key_rows.reshape(count, piece, ATTENTION_HEADS, HEAD_SIZE),
            value_rows.reshape(count, piece, ATTENTION_HEADS, HEAD_SIZE),
        ],
        axis=3,
    )
    by_heads = lax.all_to_all(packed, "seq", split_axis=2, concat_axis=1, tiled=True)
    mixed_heads, logsum = lax.map(
        lambda member: attend_row(member[0], member[1]), (by_heads, id_rows)
    )
    mixed_back = lax.all_to_all(
        mixed_heads, "seq", split_axis=1, concat_axis=2, tiled=True
    ).reshape(count, piece, width)
    attn_out = jnp.einsum(
        "rpe,ed->rpd", mixed_back, output_matrix, preferred_element_type=jnp.float32
    ) + output_offset.astype(jnp.float32)
    resid = inputs + attn_out
    mlp_input = norm_apply(
        resid, second_gain.astype(jnp.float32), second_shift.astype(jnp.float32)
    ).astype(jnp.bfloat16)
    hidden = jnp.einsum(
        "rpd,df->rpf", mlp_input, up_matrix, preferred_element_type=jnp.float32
    ) + up_offset.astype(jnp.float32)
    gelu_out = gelu_tanh(hidden).astype(jnp.bfloat16)
    result = (
        resid
        + jnp.einsum("rpf,fd->rpd", gelu_out, down_matrix, preferred_element_type=jnp.float32)
        + down_offset.astype(jnp.float32)
    )
    return (result, (attn_input, by_heads, logsum, mixed_back, resid, mlp_input, hidden, gelu_out))


def backward_micro(token_rows, id_rows, cot_rows, kept_entries, whole):
    (
        first_gain,
        first_shift,
        query_matrix,
        query_offset,
        key_matrix,
        value_matrix,
        value_offset,
        output_matrix,
        output_offset,
        second_gain,
        second_shift,
        up_matrix,
        up_offset,
        down_matrix,
        down_offset,
    ) = whole
    attn_input, by_heads, logsum, mixed_back, resid, mlp_input, hidden, gelu_out = kept_entries
    count, piece, width = token_rows.shape
    cot_float = cot_rows.astype(jnp.float32)
    grad_down = jnp.einsum("rpf,rpd->fd", gelu_out, cot_rows, preferred_element_type=jnp.float32)
    grad_down_off = jnp.sum(cot_float, axis=(0, 1))
    grad_gelu = jnp.einsum("rpd,fd->rpf", cot_rows, down_matrix, preferred_element_type=jnp.float32)
    gelu_pull = jax.vjp(gelu_tanh, hidden)[1]
    grad_hidden = gelu_pull(grad_gelu)[0].astype(jnp.bfloat16)
    grad_up = jnp.einsum("rpd,rpf->df", mlp_input, grad_hidden, preferred_element_type=jnp.float32)
    grad_up_off = jnp.sum(grad_hidden.astype(jnp.float32), axis=(0, 1))
    grad_mlp_input = jnp.einsum(
        "rpf,df->rpd", grad_hidden, up_matrix, preferred_element_type=jnp.float32
    )
    second_pull = jax.vjp(
        norm_apply, resid, second_gain.astype(jnp.float32), second_shift.astype(jnp.float32)
    )[1]
    grad_resid_norm, grad_second_gain, grad_second_shift = second_pull(grad_mlp_input)
    grad_resid = cot_float + grad_resid_norm
    grad_attn = grad_resid.astype(jnp.bfloat16)
    grad_output = jnp.einsum(
        "rpe,rpd->ed", mixed_back, grad_attn, preferred_element_type=jnp.float32
    )
    grad_output_off = jnp.sum(grad_attn.astype(jnp.float32), axis=(0, 1))
    grad_mixed = jnp.einsum(
        "rpd,ed->rpe", grad_attn, output_matrix, preferred_element_type=jnp.float32
    )
    grad_mixed = grad_mixed.astype(jnp.bfloat16).reshape(count, piece, ATTENTION_HEADS, HEAD_SIZE)
    grad_heads = lax.all_to_all(grad_mixed, "seq", split_axis=2, concat_axis=1, tiled=True)
    grad_packed = lax.map(
        lambda member: attend_back(member[0], member[1], member[2], member[3]),
        (by_heads, grad_heads, logsum, id_rows),
    )
    grad_local = lax.all_to_all(grad_packed, "seq", split_axis=1, concat_axis=2, tiled=True)
    grad_queries = grad_local[..., :HEAD_SIZE].reshape(count, piece, width)
    grad_keys = grad_local[..., HEAD_SIZE : 2 * HEAD_SIZE].reshape(count, piece, width)
    grad_values = grad_local[..., 2 * HEAD_SIZE :].reshape(count, piece, width)
    grad_query = jnp.einsum(
        "rpd,rpe->de", attn_input, grad_queries, preferred_element_type=jnp.float32
    )
    grad_key = jnp.einsum("rpd,rpe->de", attn_input, grad_keys, preferred_element_type=jnp.float32)
    grad_value = jnp.einsum(
        "rpd,rpe->de", attn_input, grad_values, preferred_element_type=jnp.float32
    )
    grad_query_off = jnp.sum(grad_queries.astype(jnp.float32), axis=(0, 1))
    grad_value_off = jnp.sum(grad_values.astype(jnp.float32), axis=(0, 1))
    grad_attn_input = (
        jnp.einsum("rpe,de->rpd", grad_queries, query_matrix, preferred_element_type=jnp.float32)
        + jnp.einsum("rpe,de->rpd", grad_keys, key_matrix, preferred_element_type=jnp.float32)
        + jnp.einsum("rpe,de->rpd", grad_values, value_matrix, preferred_element_type=jnp.float32)
    )
    first_pull = jax.vjp(
        norm_apply,
        token_rows.astype(jnp.float32),
        first_gain.astype(jnp.float32),
        first_shift.astype(jnp.float32),
    )[1]
    grad_inputs_norm, grad_first_gain, grad_first_shift = first_pull(grad_attn_input)
    token_grad = grad_resid + grad_inputs_norm
    grads = (
        grad_first_gain,
        grad_first_shift,
        grad_query,
        grad_query_off,
        grad_key,
        grad_value,
        grad_value_off,
        grad_output,
        grad_output_off,
        grad_second_gain,
        grad_second_shift,
        grad_up,
        grad_up_off,
        grad_down,
        grad_down_off,
    )
    return (grads, token_grad)


def seq_total(shares):
    return lax.psum(
        (
            shares[0],
            shares[1],
            shares[2],
            shares[3],
            shares[4],
            shares[5],
            shares[6],
            shares[7],
            shares[8],
            shares[9],
            shares[10],
            shares[11],
            shares[12],
            shares[13],
            shares[14],
        ),
        "seq",
    )


def per_device(
    tokens,
    picture_ids,
    attn_gain,
    attn_shift,
    query_weight,
    query_bias,
    key_weight,
    value_weight,
    value_bias,
    output_weight,
    output_bias,
    mlp_gain,
    mlp_shift,
    up_weight,
    up_bias,
    down_weight,
    down_bias,
    cotangent,
):
    whole = (
        lax.all_gather(attn_gain, "rows", axis=0, tiled=True),
        lax.all_gather(attn_shift, "rows", axis=0, tiled=True),
        lax.all_gather(query_weight, "rows", axis=0, tiled=True),
        lax.all_gather(query_bias, "rows", axis=0, tiled=True),
        lax.all_gather(key_weight, "rows", axis=0, tiled=True),
        lax.all_gather(value_weight, "rows", axis=0, tiled=True),
        lax.all_gather(value_bias, "rows", axis=0, tiled=True),
        lax.all_gather(output_weight, "rows", axis=0, tiled=True),
        lax.all_gather(output_bias, "rows", axis=0, tiled=True),
        lax.all_gather(mlp_gain, "rows", axis=0, tiled=True),
        lax.all_gather(mlp_shift, "rows", axis=0, tiled=True),
        lax.all_gather(up_weight, "rows", axis=0, tiled=True),
        lax.all_gather(up_bias, "rows", axis=0, tiled=True),
        lax.all_gather(down_weight, "rows", axis=1, tiled=True),
        lax.all_gather(down_bias, "rows", axis=0, tiled=True),
    )
    results = []
    kept_all = []
    for micro in range(MICRO):
        lower = micro * ROWS_MB
        result, kept_entries = forward_micro(
            tokens[lower : lower + ROWS_MB], picture_ids[lower : lower + ROWS_MB], whole
        )
        results.append(result)
        kept_all.append(kept_entries)
    again = (
        lax.all_gather(attn_gain, "rows", axis=0, tiled=True),
        lax.all_gather(attn_shift, "rows", axis=0, tiled=True),
        lax.all_gather(query_weight, "rows", axis=0, tiled=True),
        lax.all_gather(query_bias, "rows", axis=0, tiled=True),
        lax.all_gather(key_weight, "rows", axis=0, tiled=True),
        lax.all_gather(value_weight, "rows", axis=0, tiled=True),
        lax.all_gather(value_bias, "rows", axis=0, tiled=True),
        lax.all_gather(output_weight, "rows", axis=0, tiled=True),
        lax.all_gather(output_bias, "rows", axis=0, tiled=True),
        lax.all_gather(mlp_gain, "rows", axis=0, tiled=True),
        lax.all_gather(mlp_shift, "rows", axis=0, tiled=True),
        lax.all_gather(up_weight, "rows", axis=0, tiled=True),
        lax.all_gather(up_bias, "rows", axis=0, tiled=True),
        lax.all_gather(down_weight, "rows", axis=1, tiled=True),
        lax.all_gather(down_bias, "rows", axis=0, tiled=True),
    )
    token_grads = []
    shares = None
    totals = None
    for micro in range(MICRO):
        lower = micro * ROWS_MB
        grads, token_grad = backward_micro(
            tokens[lower : lower + ROWS_MB],
            picture_ids[lower : lower + ROWS_MB],
            cotangent[lower : lower + ROWS_MB],
            kept_all[micro],
            again,
        )
        token_grads.append(token_grad)
        totals = grads if totals is None else jax.tree.map(jnp.add, totals, grads)
    shares = (
        lax.psum_scatter(
            totals[0].astype(jnp.bfloat16), "rows", scatter_dimension=0, tiled=True
        ).astype(jnp.float32),
        lax.psum_scatter(
            totals[1].astype(jnp.bfloat16), "rows", scatter_dimension=0, tiled=True
        ).astype(jnp.float32),
        lax.psum_scatter(
            totals[2].astype(jnp.bfloat16), "rows", scatter_dimension=0, tiled=True
        ).astype(jnp.float32),
        lax.psum_scatter(
            totals[3].astype(jnp.bfloat16), "rows", scatter_dimension=0, tiled=True
        ).astype(jnp.float32),
        lax.psum_scatter(
            totals[4].astype(jnp.bfloat16), "rows", scatter_dimension=0, tiled=True
        ).astype(jnp.float32),
        lax.psum_scatter(
            totals[5].astype(jnp.bfloat16), "rows", scatter_dimension=0, tiled=True
        ).astype(jnp.float32),
        lax.psum_scatter(
            totals[6].astype(jnp.bfloat16), "rows", scatter_dimension=0, tiled=True
        ).astype(jnp.float32),
        lax.psum_scatter(
            totals[7].astype(jnp.bfloat16), "rows", scatter_dimension=0, tiled=True
        ).astype(jnp.float32),
        lax.psum_scatter(
            totals[8].astype(jnp.bfloat16), "rows", scatter_dimension=0, tiled=True
        ).astype(jnp.float32),
        lax.psum_scatter(
            totals[9].astype(jnp.bfloat16), "rows", scatter_dimension=0, tiled=True
        ).astype(jnp.float32),
        lax.psum_scatter(
            totals[10].astype(jnp.bfloat16), "rows", scatter_dimension=0, tiled=True
        ).astype(jnp.float32),
        lax.psum_scatter(
            totals[11].astype(jnp.bfloat16), "rows", scatter_dimension=0, tiled=True
        ).astype(jnp.float32),
        lax.psum_scatter(
            totals[12].astype(jnp.bfloat16), "rows", scatter_dimension=0, tiled=True
        ).astype(jnp.float32),
        lax.psum_scatter(
            totals[13].astype(jnp.bfloat16), "rows", scatter_dimension=1, tiled=True
        ).astype(jnp.float32),
        lax.psum_scatter(
            totals[14].astype(jnp.bfloat16), "rows", scatter_dimension=0, tiled=True
        ).astype(jnp.float32),
    )
    final = seq_total(shares)
    return (
        jnp.concatenate(results, axis=0),
        jnp.concatenate(token_grads, axis=0),
        final[0],
        final[1],
        final[2],
        final[3],
        final[4],
        final[5],
        final[6],
        final[7],
        final[8],
        final[9],
        final[10],
        final[11],
        final[12],
        final[13],
        final[14],
    )


def solution(mesh):
    placed = (
        P("rows", "seq", None),
        P("rows", None),
        P("rows"),
        P("rows"),
        P("rows", None),
        P("rows"),
        P("rows", None),
        P("rows", None),
        P("rows"),
        P("rows", None),
        P("rows"),
        P("rows"),
        P("rows"),
        P("rows", None),
        P("rows"),
        P(None, "rows"),
        P("rows"),
        P("rows", "seq", None),
    )
    return jax.shard_map(
        per_device,
        mesh=mesh,
        in_specs=placed,
        out_specs=(
            P("rows", "seq", None),
            P("rows", "seq", None),
            P("rows"),
            P("rows"),
            P("rows", None),
            P("rows"),
            P("rows", None),
            P("rows", None),
            P("rows"),
            P("rows", None),
            P("rows"),
            P("rows"),
            P("rows"),
            P("rows", None),
            P("rows"),
            P(None, "rows"),
            P("rows"),
        ),
        check_vma=False,
    )
```

profile of v0, /device:TPU:16, one launch (start us, length us, event | category | flops | bytes accessed | tf_op | source)
XLA Modules:
  0.0 1753.8 jit_solution(2007251089235493237)
XLA Ops:
  14.6 25.4 %all-reduce.20 = (bf16[1152]{0:T(1024)(128)(2,1)S(1)}, bf16[1152]{0:T(1024)(128)(2,1)S(1)}, bf16[1152]{0:T(1024)(128)(2,1)S(1)}, bf16[1152]{0:T(1024)(128)(2,1)S...) all-reduce(bf16[1152]{0:T(1024)(128)(2,1)S(1)} %dynamic-update-slic, ...), channel_id=1, replica_groups=mesh['rows'=8,'seq'=4] {'rows'}, use_global_device_ids=true, to_apply=%add.3 | all-reduce | flops 12368 | bytes 49472
  51.3 28.5 %all-gather.11.cloned.1.call-done = bf16[1152,1152]{1,0:T(8,128)(2,1)} async-done(((bf16[144,1152]{1,0:T(8,128)(2,1)}), bf16[1152,1152]{1,0:T(8,128)(2,1)}) %all-gather.11.cloned.1.call-update) | async-done | bytes 2654224 | tf_op jit(solution)/shard_map/all_gather | solution.py:325
  86.9 27.7 %all-gather.9.cloned.1.call-done = bf16[1152,1152]{1,0:T(8,128)(2,1)} async-done(((bf16[144,1152]{1,0:T(8,128)(2,1)}), bf16[1152,1152]{1,0:T(8,128)(2,1)}) %all-gather.9.cloned.1.call-update) | async-done | bytes 2654224 | tf_op jit(solution)/shard_map/all_gather | solution.py:324
  153.4 17.5 all-to-all-done
  189.1 71.9 %while.90 = (s32[]{:T(128)}, bf16[4,512,4,72]{1,3,2,0:T(8,128)(2,1)}, f32[4,4,512]{2,1,0:T(4,128)}, s32[4]{0:T(128)S(1)}, s32[2048]{0:T(1024)S(1)}, /*index=5*/b...) while((s32[]{:T(128)}, ...), condition=%wide.region_5.6_spmd, body=%wide.region_2.5_spmd.sunk | while | flops 1259485184 | bytes 57556128 | solution.py:61
  282.9 71.9 %while.91 = (s32[]{:T(128)}, bf16[4,512,4,72]{1,3,2,0:T(8,128)(2,1)}, f32[4,4,512]{2,1,0:T(4,128)}, s32[4]{0:T(128)S(1)}, s32[2048]{0:T(1024)S(1)}, /*index=5*/b...) while((s32[]{:T(128)}, ...), condition=%wide.region_13.14_spmd, body=%wide.region_10.13_spmd.sunk | while | flops 1259485184 | bytes 57556128 | solution.py:61
  372.6 16.6 all-to-all-done.3
  405.4 12.2 convolution_add_fusion.6
  417.7 17.1 convert_reduce_fusion
  434.9 13.9 fusion.128
  460.6 18.1 %convert_reduce_fusion.1 = (f32[4304]{0:T(1024)}, bf16[512,4304]{0,1:T(8,128)(2,1)}) fusion(f32[512,4304]{0,1:T(8,128)} %convolution_add_fusion.7, bf16[4304,1152]{0,1:T(8,128)(2,1)} %all-gather.17.cloned.1.call-done, bf16[2,512,1152]{2,1,0:T(8,128)(2,1)S(1)} %copy-done.30), kind=kOutput, calls=%fused_computation.117 | convolution fusion | flops 5125681152 | bytes 24335168 | tf_op jit(solution)/shard_map/rpd,fd->rpf/dot_general | solution.py:203
  478.7 14.4 fusion.186
  538.8 256.9 %while.92 = (s32[]{:T(128)}, f32[2048,4,72]{0,2,1:T(8,128)}, f32[2048,4,72]{0,2,1:T(8,128)}, bf16[4,512,4,72]{1,3,2,0:T(8,128)(2,1)}, s32[4]{0:T(128)S(1)}, /*in...) while((s32[]{:T(128)}, f32[2048,4,72]{0,2,1:T(8,128)}, ...), condition=%wide.region_20.21_spmd.clone, body=%wide.region_18.20_spmd.clone.sunk | while | flops 3087104000 | bytes 178100992 | solution.py:105
  552.3 12.9 multiply_reduce_fusion.6
  565.1 15.0 multiply_convert_fusion.10
  615.5 12.9 multiply_reduce_fusion.6
  628.3 15.0 multiply_convert_fusion.10
  654.1 12.6 fusion.314
  680.0 12.9 multiply_reduce_fusion.6
  692.8 15.0 multiply_convert_fusion.10
  718.6 12.6 fusion.314
  744.5 12.8 multiply_reduce_fusion.6
  757.3 15.0 multiply_convert_fusion.10
  783.1 12.6 fusion.314
  818.1 257.5 %while.93 = (s32[]{:T(128)}, f32[2048,4,72]{0,2,1:T(8,128)}, f32[2048,4,72]{0,2,1:T(8,128)}, bf16[4,512,4,72]{1,3,2,0:T(8,128)(2,1)}, s32[4]{0:T(128)S(1)}, /*in...) while((s32[]{:T(128)}, f32[2048,4,72]{0,2,1:T(8,128)}, ...), condition=%wide.region_27.28_spmd.clone, body=%wide.region_25.27_spmd.clone.sunk | while | flops 3087104000 | bytes 178100992 | solution.py:105
  831.8 12.9 multiply_reduce_fusion.7
  844.6 15.0 multiply_convert_fusion.11
  869.7 12.0 fusion.327
  895.0 12.9 multiply_reduce_fusion.7
  907.9 15.0 multiply_convert_fusion.11
  933.6 12.7 fusion.327
  959.6 12.9 multiply_reduce_fusion.7
  972.5 15.0 multiply_convert_fusion.11
  998.2 12.7 fusion.327
  1024.2 12.8 multiply_reduce_fusion.7
  1037.0 15.0 multiply_convert_fusion.11
  1062.7 12.7 fusion.327
  1100.6 36.1 %all-to-all-done.7 = bf16[1,2048,4,216]{3,2,0,1:T(4,128)(2,1)} async-done(((bf16[1,2048,4,216]{3,2,0,1:T(4,128)(2,1)}), bf16[1,2048,4,216]{3,2,0,1:T(4,128)(2,1)}, u32[]{:S(2)}, u32[]{:S(2)}) %all-to-all-start.7) | async-done | bytes 3538976 | tf_op jit(solution)/shard_map/all_to_all | solution.py:230
  1172.8 12.8 fusion.166
  1185.6 14.5 fusion.76
  1200.1 12.8 fusion.148
  1212.9 15.9 fusion.77
  1277.3 23.3 %all-reduce.19 = (bf16[1152]{0:T(1024)(128)(2,1)S(1)}, bf16[1152]{0:T(1024)(128)(2,1)S(1)}, bf16[1152]{0:T(1024)(128)(2,1)S(1)}, bf16[1152]{0:T(1024)(128)(2,1)S...) all-reduce(bf16[1152]{0:T(1024)(128)(2,1)S(1)} %copy-done.87, ...), channel_id=1, replica_groups=mesh['rows'=8,'seq'=4] {'rows'}, use_global_device_ids=true, to_apply=%add.8 | all-reduce | flops 14672 | bytes 58688
  1309.7 12.3 fusion.107
  1322.1 12.1 fusion.105
  1336.7 42.7 %reduce-scatter.15.cloned.1.call-done = bf16[144,4304]{1,0:T(8,128)(2,1)} async-done(((bf16[1152,4304]{1,0:T(8,128)(2,1)}), bf16[144,4304]{1,0:T(8,128)(2,1)}) %reduce-scatter.15.cloned.1.call-update) | async-done | bytes 1239568 | tf_op jit(solution)/shard_map/reduce_scatter | solution.py:410
  1379.4 105.6 %reduce-scatter.17.cloned.1.call-done = bf16[4304,144]{0,1:T(8,128)(2,1)} async-done(((bf16[4304,1152]{0,1:T(8,128)(2,1)}), bf16[4304,144]{0,1:T(8,128)(2,1)}) %reduce-scatter.17.cloned.1.call-update) | async-done | bytes 1239568 | tf_op jit(solution)/shard_map/reduce_scatter | solution.py:416
  1485.0 261.6 %all-reduce.22 = (f32[144]{0:T(256)}, f32[144]{0:T(256)}, f32[144,1152]{1,0:T(8,128)}, f32[144]{0:T(256)}, f32[144,1152]{1,0:T(8,128)}, /*index=5*/f32[144,1152]...) all-reduce(f32[144]{0:T(256)S(1)} %dynamic-slice_convert_fusion.8, ...), channel_id=1, replica_groups=mesh['rows'=8,'seq'=4] {'seq'}, use_global_device_ids=true, to_apply=%region_33.34 | all-reduce | flops 1904794 | bytes 11432144 | tf_op jit(solution)/shard_map/psum | solution.py:277
  (573 shorter events, 651.5 us)
Async XLA Ops:
  7.3 33.3 %copy-start.8 = (bf16[2,512,1152]{2,1,0:T(8,128)(2,1)S(1)}, bf16[2,512,1152]{2,1,0:T(8,128)(2,1)}, u32[]{:S(2)}) copy-start(bf16[2,512,1152]{2,1,0:T(8,128)(2,1)} %param.26) | copy-start | bytes 7077892
  7.3 37.6 %all-gather.7.cloned.1.call-start = ((), (), s32[]{:S(2)}) async-start(), calls=%async_computation.14 | async-start | bytes 2985984 | tf_op jit(solution)/shard_map/all_gather | solution.py:322
  8.0 71.8 %all-gather.11.cloned.1.call-start = ((), (), s32[]{:S(2)}) async-start(), calls=%async_computation.16 | async-start | bytes 2985984 | tf_op jit(solution)/shard_map/all_gather | solution.py:325
  8.8 105.8 %all-gather.9.cloned.1.call-start = ((), (), s32[]{:S(2)}) async-start(), calls=%async_computation.15 | async-start | bytes 2985984 | tf_op jit(solution)/shard_map/all_gather | solution.py:324
  9.5 385.7 %all-gather.13.cloned.1.call-start = ((), (), s32[]{:S(2)}) async-start(), calls=%async_computation.17 | async-start | bytes 2985984 | tf_op jit(solution)/shard_map/all_gather | solution.py:327
  10.1 394.7 %all-gather.15.cloned.1.call-start = ((), (), s32[]{:S(2)}) async-start(), calls=%async_computation.18 | async-start | bytes 11280384 | tf_op jit(solution)/shard_map/all_gather | solution.py:331
  40.0 105.0 %copy-start.48 = (f32[1152]{0:T(1024)}, f32[1152]{0:T(1024)S(1)}, u32[]{:S(2)}) copy-start(f32[1152]{0:T(1024)S(1)} %convert_element_type.313) | copy-start | bytes 13828
  41.0 73.6 %copy-start.63 = (f32[512]{0:T(512)}, f32[512]{0:T(512)S(1)}, u32[]{:S(2)}) copy-start(f32[512]{0:T(512)S(1)} %get-tuple-element.554) | copy-start | bytes 6148
  42.4 72.2 %copy-start.51 = (f32[512]{0:T(512)}, f32[512]{0:T(512)S(1)}, u32[]{:S(2)}) copy-start(f32[512]{0:T(512)S(1)} %fusion.158) | copy-start | bytes 6148
  124.9 45.9 %all-to-all-start = ((bf16[1,512,16,216]{1,3,0,2:T(8,128)(2,1)}), bf16[1,512,16,216]{1,3,0,2:T(8,128)(2,1)}, u32[]{:S(2)}, u32[]{:S(2)}) async-start(bf16[1,512,16,216]{1,3,0,2:T(8,128)(2,1)} %maximum_bitcast_fusion), calls=%async_computation | async-start | bytes 7077888 | tf_op jit(solution)/shard_map/all_to_all | solution.py:154
  129.8 287.8 %all-gather.17.cloned.1.call-start = ((), (), s32[]{:S(2)}) async-start(), calls=%async_computation.19 | async-start | bytes 11280384 | tf_op jit(solution)/shard_map/all_gather | solution.py:333
  170.9 94.4 %all-to-all-start.2 = ((bf16[1,512,16,216]{1,3,0,2:T(8,128)(2,1)}), bf16[1,512,16,216]{1,3,0,2:T(8,128)(2,1)}, u32[]{:S(2)}, u32[]{:S(2)}) async-start(bf16[1,512,16,216]{1,3,0,2:T(8,128)(2,1)} %maximum_bitcast_fusion.1), calls=%async_computation.2 | async-start | bytes 7077888 | tf_op jit(solution)/shard_map/all_to_all | solution.py:154
  265.3 94.3 %all-to-all-start.1 = ((bf16[1,2048,4,72]{3,2,0,1:T(4,128)(2,1)}), bf16[1,2048,4,72]{3,2,0,1:T(4,128)(2,1)}, u32[]{:S(2)}, u32[]{:S(2)}) async-start(bf16[1,2048,4,72]{3,2,0,1:T(4,128)(2,1)} %bitcast.361), calls=%async_computation.1 | async-start | bytes 4194304 | tf_op jit(solution)/shard_map/all_to_all | solution.py:158
  359.6 29.6 %all-to-all-start.3 = ((bf16[1,2048,4,72]{3,2,0,1:T(4,128)(2,1)}), bf16[1,2048,4,72]{3,2,0,1:T(4,128)(2,1)}, u32[]{:S(2)}, u32[]{:S(2)}) async-start(bf16[1,2048,4,72]{3,2,0,1:T(4,128)(2,1)} %bitcast.362), calls=%async_computation.3 | async-start | bytes 4194304 | tf_op jit(solution)/shard_map/all_to_all | solution.py:158
  365.2 127.9 %copy-start.55 = (f32[1152]{0:T(1024)}, f32[1152]{0:T(1024)S(1)}, u32[]{:S(2)}) copy-start(f32[1152]{0:T(1024)S(1)} %convert_element_type.322) | copy-start | bytes 13828
  402.5 15.1 copy-start.89
  417.6 17.2 copy-start.28
  417.7 17.1 copy-start.90
  417.7 17.1 copy-start.106
  434.8 13.9 copy-start.122
  434.8 13.9 copy-start.20
  434.8 13.9 copy-start.68
  434.8 13.9 copy-start.74
  434.8 13.9 copy-start.91
  434.9 13.9 copy-start.98
  448.8 11.8 copy-start.30
  460.6 18.1 %copy-start.107 = (f32[512]{0:T(512)S(1)}, f32[512]{0:T(512)}, u32[]{:S(2)}) copy-start(f32[512]{0:T(512)} %copy-done.105) | copy-start | bytes 6148
  478.7 14.4 copy-start.80
  507.3 19.0 %all-to-all-start.4 = ((bf16[1,512,16,72]{1,3,0,2:T(8,128)(2,1)}), bf16[1,512,16,72]{1,3,0,2:T(8,128)(2,1)}, u32[]{:S(2)}, u32[]{:S(2)}) async-start(bf16[1,512,16,72]{1,3,0,2:T(8,128)(2,1)} %bitcast.45), calls=%async_computation.4 | async-start | bytes 2359296 | tf_op jit(solution)/shard_map/all_to_all | solution.py:225
  511.6 825.1 %reduce-scatter.13.cloned.1.call-start = ((), (), s32[]{:S(2)}) async-start(), calls=%async_computation.23 | async-start | bytes 2985984 | tf_op jit(solution)/shard_map/reduce_scatter | solution.py:398
  526.3 278.8 %all-to-all-start.6 = ((bf16[1,512,16,72]{1,3,0,2:T(8,128)(2,1)}), bf16[1,512,16,72]{1,3,0,2:T(8,128)(2,1)}, u32[]{:S(2)}, u32[]{:S(2)}) async-start(bf16[1,512,16,72]{1,3,0,2:T(8,128)(2,1)} %bitcast.62), calls=%async_computation.6 | async-start | bytes 2359296 | tf_op jit(solution)/shard_map/all_to_all | solution.py:225
  643.3 7.4 copy-start
  707.8 7.4 copy-start
  772.3 7.4 copy-start
  805.0 279.9 %all-to-all-start.5 = ((bf16[1,2048,4,216]{3,2,0,1:T(4,128)(2,1)}), bf16[1,2048,4,216]{3,2,0,1:T(4,128)(2,1)}, u32[]{:S(2)}, u32[]{:S(2)}) async-start(bf16[1,2048,4,216]{3,2,0,1:T(4,128)(2,1)} %copy.123), calls=%async_computation.5 | async-start | bytes 8388608 | tf_op jit(solution)/shard_map/all_to_all | solution.py:230
  922.8 7.4 copy-start.1
  987.4 7.4 copy-start.1
  1052.0 7.4 copy-start.1
  1084.9 51.7 %all-to-all-start.7 = ((bf16[1,2048,4,216]{3,2,0,1:T(4,128)(2,1)}), bf16[1,2048,4,216]{3,2,0,1:T(4,128)(2,1)}, u32[]{:S(2)}, u32[]{:S(2)}) async-start(bf16[1,2048,4,216]{3,2,0,1:T(4,128)(2,1)} %copy.130), calls=%async_computation.7 | async-start | bytes 8388608 | tf_op jit(solution)/shard_map/all_to_all | solution.py:230
  1089.8 246.9 %reduce-scatter.11.cloned.1.call-start = ((), (), s32[]{:S(2)}) async-start(), calls=%async_computation.22 | async-start | bytes 2985984 | tf_op jit(solution)/shard_map/reduce_scatter | solution.py:392
  1100.6 46.8 %copy-start.17 = (bf16[1,512,4,4,216]{1,4,3,2,0:T(8,128)(2,1)}, bf16[1,512,4,4,216]{1,4,3,2,0:T(8,128)(2,1)S(1)}, u32[]{:S(2)}) copy-start(bf16[1,512,4,4,216]{1,4,3,2,0:T(8,128)(2,1)S(1)} %copy.125) | copy-start | bytes 10616836
  1158.0 178.6 %reduce-scatter.9.cloned.1.call-start = ((), (), s32[]{:S(2)}) async-start(), calls=%async_computation.21 | async-start | bytes 2985984 | tf_op jit(solution)/shard_map/reduce_scatter | solution.py:389
  1165.2 171.5 %reduce-scatter.7.cloned.1.call-start = ((), (), s32[]{:S(2)}) async-start(), calls=%async_computation.20 | async-start | bytes 2985984 | tf_op jit(solution)/shard_map/reduce_scatter | solution.py:383
  1172.7 206.7 %reduce-scatter.15.cloned.1.call-start = ((), (), s32[]{:S(2)}) async-start(), calls=%async_computation.24 | async-start | bytes 11280384 | tf_op jit(solution)/shard_map/reduce_scatter | solution.py:410
  1200.1 284.9 %reduce-scatter.17.cloned.1.call-start = ((), (), s32[]{:S(2)}) async-start(), calls=%async_computation.25 | async-start | bytes 11280384 | tf_op jit(solution)/shard_map/reduce_scatter | solution.py:416
  1273.4 28.0 %copy-start.70 = (f32[512]{0:T(512)S(1)}, f32[512]{0:T(512)}, u32[]{:S(2)}) copy-start(f32[512]{0:T(512)} %copy-done.69) | copy-start | bytes 6148
  1273.4 28.0 %copy-start.72 = (f32[512]{0:T(512)S(1)}, f32[512]{0:T(512)}, u32[]{:S(2)}) copy-start(f32[512]{0:T(512)} %copy-done.71) | copy-start | bytes 6148
  1309.7 12.3 copy-start.29
  (101 other events, 382.4 us)
Sparse Core Ops, SparseCore 0:
  9.7 35.1 all-gather.6
  46.6 33.1 all-gather.10
  81.5 33.0 all-gather.8
  116.1 33.0 all-gather.12
  150.7 93.9 all-gather.14
  246.2 94.0 all-gather.16
  517.5 33.0 reduce-scatter.12
  1158.2 31.7 reduce-scatter.10
  1192.3 37.0 reduce-scatter.8
  1231.5 37.2 reduce-scatter.6
  1271.2 108.2 reduce-scatter.14
  1381.6 103.3 reduce-scatter.16
where the time goes:
time: 1770 us; the launch traced here: 1750 us
  matrix products  695 us (39%)
  blocking collectives  310 us (18%)
  waiting for transfers between devices  281 us (16%)
  other arithmetic  228 us (13%)
  local copies, waits for them, and re-layouts  150 us (8%)
  starting transfers between devices  38.9 us (2%)
  loops' own time  32.1 us (2%)
  between operations  18.7 us (1%)
    psum x1, blocking collectives, seq_total(): lax.psum((shares[0], shares[1], shares[2], shares[3], shares[4], shares[5...  262 us
    convert_element_type x8, other arithmetic, one_block(): grad_scores = (probs * (grad_probs - inner)).astype(jnp.bfloat16)  120 us
    reduce_scatter x1, waiting for transfers between devices, per_device(): lax.psum_scatter(totals[13].astype(jnp.bfloat16), 'rows', scatter_dimensi...  106 us
    dot_general x16, matrix products, block_scores(): jnp.einsum('qhd,khd->hqk', query_block, key_rows, preferred_element_type=...  105 us
    dot_general x8, matrix products, one_block(): jnp.einsum('qhd,khd->hqk', grad_block, value_rows, preferred_element_type...  103 us
    dot_general x8, matrix products, one_block(): jnp.einsum('hqk,qhd->khd', probs.astype(jnp.bfloat16), grad_block, prefer...  99.8 us
    dot_general x8, matrix products, one_block(): jnp.einsum('hqk,qhd->khd', grad_scores, query_block, preferred_element_ty...  57.7 us
    unnamed x2, blocking collectives  48.7 us
  transfers between devices with their start and end apart: 20, of which 9 were waited for; matrix products, arithmetic and copies ran while one was open for 56% of the time, Pallas kernels for 0%

commit v1 on v0

v1 whole, which is shorter than its diff:
```python
import functools
import jax
import jax.numpy as jnp
from jax import lax
from jax.experimental import pallas as pl
from jax.experimental.pallas import tpu as pltpu
from jax.sharding import PartitionSpec as P

HEAD_SIZE = 72
EPS = 1e-06
NEGATIVE = -1e30
LOG2E = 1.4426950408889634
PAD = 128
ROWS = 80


def split_refs(source, count, block):
    wide = source.astype(jnp.float32)
    return [wide[HEAD_SIZE * h : HEAD_SIZE * (h + 1)] for h in range(count)]


def grow_rows(value, rows):
    return jnp.concatenate([value, jnp.zeros((rows - value.shape[0], value.shape[1]), value.dtype)], axis=0)


def same_picture(kid_ref, qid_ref, key_start, query_start, block):
    key_ids = kid_ref[pl.ds(key_start, block), :]
    key_ids = jnp.concatenate([key_ids] * (block // 128), axis=1)
    return key_ids == qid_ref[0:1, pl.ds(query_start, block)]


def attend_kernel(low_ref, high_ref, qkv_ref, kid_ref, qid_ref, out_ref, log_ref, q_t, k_n, v_t, kept, top, total, acc, *, count, block):
    step = pl.program_id(0)
    length = qkv_ref.shape[2]
    factor = HEAD_SIZE ** (-0.5) * LOG2E

    @pl.when(step == 0)
    def _():
        @pl.loop(0, length // block)
        def _(part):
            at = pl.ds(pl.multiple_of(part * block, block), block)
            for h, value in enumerate(split_refs(qkv_ref[0, :, at], count, block)):
                q_t[h, :, at] = grow_rows(value, PAD).astype(jnp.bfloat16)
            for h, value in enumerate(split_refs(qkv_ref[1, :, at], count, block)):
                k_n[h, at, :] = grow_rows(value, PAD).T.astype(jnp.bfloat16)
            for h, value in enumerate(split_refs(qkv_ref[2, :, at], count, block)):
                v_t[h, :, at] = grow_rows(value, ROWS).astype(jnp.bfloat16)

    top[...] = jnp.full(top.shape, NEGATIVE, jnp.float32)
    total[...] = jnp.zeros(total.shape, jnp.float32)
    acc[...] = jnp.zeros(acc.shape, jnp.float32)
    query_start = pl.multiple_of(step * block, block)
    queries = pl.ds(query_start, block)

    def first(index, _):
        key_start = pl.multiple_of(index * block, block)
        mask = same_picture(kid_ref, qid_ref, key_start, query_start, block)
        for h in range(count):
            scores = jnp.dot(
                k_n[h, pl.ds(key_start, block), :], q_t[h, :, queries], preferred_element_type=jnp.float32
            )
            scores = jnp.where(mask, scores * factor, NEGATIVE)
            kept[h, pl.ds(key_start, block), :] = scores
            top[h] = jnp.maximum(top[h], jnp.max(scores.reshape(block // 8, 8, block), axis=0))
        return 0

    lax.fori_loop(low_ref[step], high_ref[step], first, 0)
    highest = [jnp.max(top[h], axis=0, keepdims=True) for h in range(count)]

    def second(index, _):
        keys = pl.ds(pl.multiple_of(index * block, block), block)
        for h in range(count):
            probs = jnp.exp2(kept[h, keys, :] - highest[h])
            total[h] += jnp.sum(probs.reshape(block // 8, 8, block), axis=0)
            acc[h] += jnp.dot(v_t[h, :, keys], probs.astype(jnp.bfloat16), preferred_element_type=jnp.float32)
        return 0

    lax.fori_loop(low_ref[step], high_ref[step], second, 0)
    sums = [jnp.sum(total[h], axis=0, keepdims=True) for h in range(count)]
    for h in range(count):
        log_ref[h : h + 1, :] = highest[h] + jnp.log2(sums[h])
    out_ref[0] = jnp.concatenate([acc[h, :HEAD_SIZE] / sums[h] for h in range(count)], axis=0).astype(jnp.bfloat16)


def attend(qkv, low, high, key_ids, query_ids, chunk):
    _, width, length = qkv.shape
    count = width // HEAD_SIZE
    block = min(256, chunk)
    per = chunk // block
    whole = lambda *shape: pl.BlockSpec(shape, lambda i, *_: (0,) * len(shape))
    area = length * length * count // 2
    return pl.pallas_call(
        functools.partial(attend_kernel, count=count, block=block),
        name="attend",
        grid_spec=pltpu.PrefetchScalarGridSpec(
            num_scalar_prefetch=2,
            grid=(length // block,),
            in_specs=[whole(3, width, length), whole(length, 128), whole(8, length)],
            out_specs=[
                pl.BlockSpec((1, width, block), lambda i, *_: (i // per, 0, i % per)),
                pl.BlockSpec((max(8, count), block), lambda i, *_: (0, i)),
            ],
            scratch_shapes=[
                pltpu.VMEM((count, PAD, length), jnp.bfloat16),
                pltpu.VMEM((count, length, PAD), jnp.bfloat16),
                pltpu.VMEM((count, ROWS, length), jnp.bfloat16),
                pltpu.VMEM((count, length, block), jnp.float32),
                pltpu.VMEM((count, 8, block), jnp.float32),
                pltpu.VMEM((count, 8, block), jnp.float32),
                pltpu.VMEM((count, ROWS, block), jnp.float32),
            ],
        ),
        out_shape=[
            jax.ShapeDtypeStruct((length // chunk, width, chunk), jnp.bfloat16),
            jax.ShapeDtypeStruct((max(8, count), length), jnp.float32),
        ],
        compiler_params=pltpu.CompilerParams(vmem_limit_bytes=40 << 20),
        cost_estimate=pl.CostEstimate(flops=area * 800, transcendentals=area, bytes_accessed=8 * length * width),
    )(low, high, qkv, key_ids, query_ids)


def attend_back_kernel(
    low_ref, high_ref, qkv_ref, gm_ref, out_ref, log_ref, kid_ref, qid_ref, grad_ref,
    q_t, k_t, k_n, v_n, g_t, delta, gq, gk, gv, *, count, block,
):
    step = pl.program_id(0)
    length = qkv_ref.shape[2]
    chunk = gm_ref.shape[2]
    scale = HEAD_SIZE ** (-0.5)
    factor = scale * LOG2E

    @pl.when(step == 0)
    def _():
        gq[...] = jnp.zeros(gq.shape, jnp.float32)

        @pl.loop(0, length // block)
        def _(part):
            at = pl.ds(pl.multiple_of(part * block, block), block)
            for h, value in enumerate(split_refs(qkv_ref[0, :, at], count, block)):
                q_t[h, :, at] = grow_rows(value, PAD).astype(jnp.bfloat16)
            for h, value in enumerate(split_refs(qkv_ref[1, :, at], count, block)):
                value = grow_rows(value, PAD)
                k_t[h, :, at] = value[:ROWS].astype(jnp.bfloat16)
                k_n[h, at, :] = value.T.astype(jnp.bfloat16)
            for h, value in enumerate(split_refs(qkv_ref[2, :, at], count, block)):
                v_n[h, at, :] = grow_rows(value, PAD).T.astype(jnp.bfloat16)

        for piece in range(length // chunk):
            at = pl.ds(piece * chunk, chunk)
            grads = split_refs(gm_ref[piece], count, chunk)
            outs = split_refs(out_ref[piece], count, chunk)
            for h in range(count):
                g_t[h, :, at] = grow_rows(grads[h], PAD).astype(jnp.bfloat16)
                delta[h, :, at] = jnp.sum(grads[h] * outs[h], axis=0, keepdims=True)

    gk[...] = jnp.zeros(gk.shape, jnp.float32)
    gv[...] = jnp.zeros(gv.shape, jnp.float32)
    key_start = pl.multiple_of(step * block, block)
    keys = pl.ds(key_start, block)

    def one(index, _):
        query_start = pl.multiple_of(index * block, block)
        queries = pl.ds(query_start, block)
        mask = same_picture(kid_ref, qid_ref, key_start, query_start, block)
        for h in range(count):
            scores = jnp.dot(k_n[h, keys, :], q_t[h, :, queries], preferred_element_type=jnp.float32)
            probs = jnp.where(mask, jnp.exp2(scores * factor - log_ref[h : h + 1, queries]), 0.0)
            back = jnp.dot(v_n[h, keys, :], g_t[h, :, queries], preferred_element_type=jnp.float32)
            slope = (probs * (back - delta[h, :, queries])).astype(jnp.bfloat16)
            nt = (((1,), (1,)), ((), ()))
            gv[h] += lax.dot_general(
                g_t[h, :ROWS, queries], probs.astype(jnp.bfloat16), nt, preferred_element_type=jnp.float32
            )
            gk[h] += lax.dot_general(q_t[h, :ROWS, queries], slope, nt, preferred_element_type=jnp.float32)
            gq[h, :, queries] += jnp.dot(k_t[h, :, keys], slope, preferred_element_type=jnp.float32)
        return 0

    lax.fori_loop(low_ref[step], high_ref[step], one, 0)
    grad_ref[1, :, keys] = (jnp.concatenate([gk[h, :HEAD_SIZE] for h in range(count)], axis=0) * scale).astype(jnp.bfloat16)
    grad_ref[2, :, keys] = jnp.concatenate([gv[h, :HEAD_SIZE] for h in range(count)], axis=0).astype(jnp.bfloat16)

    @pl.when(step == pl.num_programs(0) - 1)
    def _():
        @pl.loop(0, length // block)
        def _(part):
            at = pl.ds(pl.multiple_of(part * block, block), block)
            grad_ref[0, :, at] = (
                jnp.concatenate([gq[h, :HEAD_SIZE, at] for h in range(count)], axis=0) * scale
            ).astype(jnp.bfloat16)


def attend_back(qkv, grad_mixed, mixed, logsum, low, high, key_ids, query_ids):
    _, width, length = qkv.shape
    chunk = mixed.shape[2]
    count = width // HEAD_SIZE
    block = min(256, chunk)
    whole = lambda *shape: pl.BlockSpec(shape, lambda i, *_: (0,) * len(shape))
    area = length * length * count // 2
    return pl.pallas_call(
        functools.partial(attend_back_kernel, count=count, block=block),
        name="attend_back",
        grid_spec=pltpu.PrefetchScalarGridSpec(
            num_scalar_prefetch=2,
            grid=(length // block,),
            in_specs=[
                whole(3, width, length),
                whole(*mixed.shape),
                whole(*mixed.shape),
                whole(max(8, count), length),
                whole(length, 128),
                whole(8, length),
            ],
            out_specs=whole(3, width, length),
            scratch_shapes=[
                pltpu.VMEM((count, PAD, length), jnp.bfloat16),
                pltpu.VMEM((count, ROWS, length), jnp.bfloat16),
                pltpu.VMEM((count, length, PAD), jnp.bfloat16),
                pltpu.VMEM((count, length, PAD), jnp.bfloat16),
                pltpu.VMEM((count, PAD, length), jnp.bfloat16),
                pltpu.VMEM((count, 1, length), jnp.float32),
                pltpu.VMEM((count, ROWS, length), jnp.float32),
                pltpu.VMEM((count, ROWS, block), jnp.float32),
                pltpu.VMEM((count, ROWS, block), jnp.float32),
            ],
        ),
        out_shape=jax.ShapeDtypeStruct((3, width, length), jnp.bfloat16),
        compiler_params=pltpu.CompilerParams(vmem_limit_bytes=60 << 20),
        cost_estimate=pl.CostEstimate(flops=area * 2000, transcendentals=area, bytes_accessed=16 * length * width),
    )(low, high, qkv, grad_mixed, mixed, logsum, key_ids, query_ids)


def block_ranges(ids, block):
    ids = jnp.where(ids < 0, 1 << 20, ids).reshape(-1, block)
    first, last = ids[:, 0], ids[:, -1]
    low = jnp.sum((last[None, :] < first[:, None]).astype(jnp.int32), axis=1)
    high = jnp.sum((first[None, :] <= last[:, None]).astype(jnp.int32), axis=1)
    return low, high


def norm_parts(value_rows):
    center = value_rows - jnp.mean(value_rows, axis=-1, keepdims=True)
    inverse = lax.rsqrt(jnp.mean(center * center, axis=-1, keepdims=True) + EPS)
    return center * inverse, inverse


def norm_back(grad, normed, inverse, gain):
    scaled = grad * gain
    flat = jnp.mean(scaled, axis=-1, keepdims=True)
    along = jnp.mean(scaled * normed, axis=-1, keepdims=True)
    return inverse * (scaled - flat - normed * along)


def contract(left, right, left_axis, right_axis):
    return lax.dot_general(left, right, (((left_axis,), (right_axis,)), ((), ())), preferred_element_type=jnp.float32)


def per_device(
    tokens, picture_ids, attn_gain, attn_shift, query_weight, query_bias, key_weight, value_weight, value_bias,
    output_weight, output_bias, mlp_gain, mlp_shift, up_weight, up_bias, down_weight, down_bias, cotangent,
    *, seq_count, row_count,
):
    count, chunk, width = tokens.shape
    length = chunk * seq_count
    part = width // seq_count
    place = lax.axis_index("seq")
    band = lax.axis_index("rows")
    block = min(256, chunk)
    f32, bf16 = jnp.float32, jnp.bfloat16

    def own_columns(weight):
        return lax.dynamic_slice_in_dim(weight, place * part, part, axis=1)

    heads_shard = jnp.concatenate([own_columns(query_weight), own_columns(key_weight), own_columns(value_weight)], axis=1)
    heads_weight = lax.all_gather(heads_shard, "rows", axis=0, tiled=True)
    small = [attn_gain, attn_shift, query_bias, value_bias, output_bias, mlp_gain, mlp_shift, down_bias, up_bias]
    sizes = [piece.shape[0] for piece in small]
    packed = jnp.concatenate(small)
    padded = -(-packed.shape[0] // 2048) * 2048
    packed = jnp.pad(packed, (0, padded - packed.shape[0])).reshape(padded // 128, 128)
    packed = lax.all_gather(packed, "rows", axis=0, tiled=False).reshape(row_count, padded).astype(f32)
    pieces, start = [], 0
    for size in sizes:
        pieces.append(packed[:, start : start + size].reshape(row_count * size))
        start += size
    gain1, shift1, query_off, value_off, output_off, gain2, shift2, down_off, up_off = pieces
    heads_off = jnp.concatenate(
        [
            lax.dynamic_slice_in_dim(query_off, place * part, part),
            jnp.zeros((part,), f32),
            lax.dynamic_slice_in_dim(value_off, place * part, part),
        ]
    )

    attn_inputs, packs, mixes, logs, tables, mixed_own = [], [], [], [], [], []
    for row in range(count):
        ids = picture_ids[row]
        low, high = block_ranges(ids, block)
        tables.append((low, high, jnp.broadcast_to(ids[:, None], (length, 128)), jnp.broadcast_to(ids[None], (8, length))))
        whole_row = lax.all_gather(tokens[row], "seq", axis=0, tiled=True)
        attn_input = (norm_parts(whole_row.astype(f32))[0] * gain1 + shift1).astype(bf16)
        pack = (contract(heads_weight, attn_input, 0, 1) + heads_off[:, None]).astype(bf16).reshape(3, part, length)
        mixed, logsum = attend(pack, *tables[row], chunk)
        attn_inputs.append(attn_input)
        packs.append(pack)
        mixes.append(mixed)
        logs.append(logsum)
        back = lax.all_to_all(mixed, "seq", split_axis=0, concat_axis=0, tiled=True)
        mixed_own.append(back.reshape(width, chunk))

    output_whole = lax.all_gather(output_weight, "rows", axis=0, tiled=True)
    up_whole = lax.all_gather(up_weight, "rows", axis=0, tiled=True)
    down_whole = lax.all_gather(down_weight.T, "rows", axis=0, tiled=True)

    resid = jnp.concatenate(
        [
            tokens[row].astype(f32) + (contract(mixed_own[row], output_whole, 0, 0) + output_off)
            for row in range(count)
        ],
        axis=0,
    )
    normed2, inverse2 = norm_parts(resid)
    mlp_input = (normed2 * gain2 + shift2).astype(bf16)
    hidden = contract(mlp_input, up_whole, 1, 0) + up_off
    gelu_out, pull = jax.vjp(lambda v: jax.nn.gelu(v, approximate=True), hidden)
    gelu_out = gelu_out.astype(bf16)
    slope = pull(jnp.ones_like(hidden))[0].astype(bf16)
    activations = resid + contract(gelu_out, down_whole, 1, 1) + down_off

    cot = cotangent.reshape(count * chunk, width)
    grad_down = contract(cot, gelu_out, 0, 0).astype(bf16)
    grad_hidden = (contract(cot, down_whole, 1, 0) * slope.astype(f32)).astype(bf16)
    grad_up = contract(mlp_input, grad_hidden, 0, 0).astype(bf16)
    grad_mlp_input = contract(grad_hidden, up_whole, 1, 1)
    down_share = lax.psum_scatter(grad_down, "rows", scatter_dimension=0, tiled=True)
    up_share = lax.psum_scatter(grad_up, "rows", scatter_dimension=0, tiled=True)
    grad_resid = cot.astype(f32) + norm_back(grad_mlp_input, normed2, inverse2, gain2)
    grad_attn = grad_resid.astype(bf16)

    grad_output = None
    for row in range(count):
        term = contract(mixed_own[row], grad_attn[row * chunk : (row + 1) * chunk], 1, 0)
        grad_output = term if grad_output is None else grad_output + term
    output_share = lax.psum_scatter(grad_output.astype(bf16), "rows", scatter_dimension=0, tiled=True)
    grad_heads, grad_query_off, grad_value_off, token_grads, normed1_all, grad_in_all = None, 0.0, 0.0, [], [], []
    for row in range(count):
        grad_mixed = contract(output_whole, grad_attn[row * chunk : (row + 1) * chunk], 1, 1).astype(bf16)
        grad_mixed = lax.all_to_all(
            grad_mixed.reshape(seq_count, part, chunk), "seq", split_axis=0, concat_axis=0, tiled=True
        )
        grad_pack = attend_back(packs[row], grad_mixed, mixes[row], logs[row], *tables[row])
        grad_query_off = grad_query_off + jnp.sum(grad_pack[0].astype(f32), axis=1)
        grad_value_off = grad_value_off + jnp.sum(grad_pack[2].astype(f32), axis=1)
        grad_pack = grad_pack.reshape(3 * part, length)
        grad_in = contract(grad_pack, heads_weight, 0, 1).astype(bf16).reshape(seq_count, chunk, width)
        grad_in = lax.all_to_all(grad_in, "seq", split_axis=0, concat_axis=0, tiled=True)
        grad_in_all.append(jnp.sum(grad_in.astype(f32), axis=0))
        term = contract(attn_inputs[row], grad_pack, 0, 1)
        grad_heads = term if grad_heads is None else grad_heads + term
    heads_share = lax.psum_scatter(grad_heads.astype(bf16), "rows", scatter_dimension=0, tiled=True)

    grad_attn_input = jnp.concatenate(grad_in_all, axis=0)
    normed1, inverse1 = norm_parts(tokens.reshape(count * chunk, width).astype(f32))
    token_grad = grad_resid + norm_back(grad_attn_input, normed1, inverse1, gain1)

    def placed(value):
        return lax.dynamic_update_slice_in_dim(jnp.zeros((width,), f32), value, place * part, axis=0)

    grads = [
        jnp.sum(grad_attn_input * normed1, axis=0),
        jnp.sum(grad_attn_input, axis=0),
        placed(grad_query_off),
        placed(grad_value_off),
        jnp.sum(grad_attn.astype(f32), axis=0),
        jnp.sum(grad_mlp_input * normed2, axis=0),
        jnp.sum(grad_mlp_input, axis=0),
        jnp.sum(cot.astype(f32), axis=0),
        jnp.sum(grad_hidden.astype(f32), axis=0),
    ]
    together = jnp.concatenate([value.reshape(row_count, -1) for value in grads], axis=1)
    together = lax.psum(together, ("rows", "seq"))
    mine = lax.dynamic_index_in_dim(together, band, axis=0, keepdims=False)
    vectors, start = [], 0
    for size in sizes:
        vectors.append(mine[start : start + size])
        start += size

    def seq_sum(share):
        return jnp.sum(lax.all_gather(share, "seq", axis=0, tiled=False).astype(f32), axis=0)

    heads_all = lax.all_gather(heads_share, "seq", axis=0, tiled=False).astype(f32)

    def take(which):
        piece = heads_all[:, :, which * part : (which + 1) * part]
        return piece.transpose(1, 0, 2).reshape(heads_share.shape[0], width)

    return (
        activations.reshape(count, chunk, width),
        token_grad.reshape(count, chunk, width),
        vectors[0],
        vectors[1],
        take(0),
        vectors[2],
        take(1),
        take(2),
        vectors[3],
        seq_sum(output_share),
        vectors[4],
        vectors[5],
        vectors[6],
        seq_sum(up_share),
        vectors[8],
        seq_sum(down_share).T,
        vectors[7],
    )


def solution(mesh):
    matrix, vector, batch = P("rows", None), P("rows"), P("rows", "seq", None)
    columns = P(None, "rows")
    return jax.shard_map(
        functools.partial(per_device, seq_count=mesh.shape["seq"], row_count=mesh.shape["rows"]),
        mesh=mesh,
        in_specs=(
            batch, matrix, vector, vector, matrix, vector, matrix, matrix, vector, matrix, vector, vector, vector, matrix,
            vector, columns, vector, batch,
        ),
        out_specs=(
            batch, batch, vector, vector, matrix, vector, matrix, matrix, vector, matrix, vector, vector, vector, matrix,
            vector, columns, vector,
        ),
        check_vma=False,
    )
```

time: 1770 us -> 956 us (0.54)
  matrix products: 695 us -> 223 us
  blocking collectives: 310 us -> 71.9 us
  other arithmetic: 228 us -> 56.9 us
  Pallas kernels: 0 us -> 143 us
  local copies, waits for them, and re-layouts: 150 us -> 45.9 us
  waiting for transfers between devices: 281 us -> 361 us
  loops' own time: 32.1 us -> 0 us
    dot_general x92 -> x18, matrix products: 695 us -> 223 us  [contract(): lax.dot_general(left, right, (((left_axis,), (right_axis,)), ((), ())), p...]
    all_gather x6 -> x9, waiting for transfers between devices: 58.8 us -> 280 us  [the longest x1 76.3 us: per_device(): down_whole = lax.all_gather(down_weight.T, 'rows', axis=0, tiled=True)]
    psum x1, blocking collectives: 262 us -> 45.4 us  [per_device(): together = lax.psum(together, ('rows', 'seq'))]
    pallas_call x0 -> x4, Pallas kernels: none -> 143 us  [the longest x2 95.4 us: attend_back(): pl.pallas_call(functools.partial(attend_back_kernel, count=count, block=b...]
    reduce_scatter x6 -> x4, waiting for transfers between devices: 148 us -> 10.5 us  [the longest x1 10.5 us: per_device(): lax.psum_scatter(grad_down, 'rows', scatter_dimension=0, tiled=True)]
    convert_element_type x39 -> x1, other arithmetic: 137 us -> 0.15 us  [per_device(): lax.all_gather(heads_share, 'seq', axis=0, tiled=False).astype(f32)]
    unnamed x2 -> x0, blocking collectives: 48.7 us -> none
    all_to_all x12 -> x0, local copies, waits for them, and re-layouts: 48.2 us -> none  [the longest x4 21.5 us: backward_micro(): lax.all_to_all(grad_packed, 'seq', split_axis=1, concat_axis=2, tiled=True)]
  transfers between devices with their start and end apart: 20 -> 19, of which waited for: 9 -> 11; matrix products, arithmetic and copies ran while one was open for 56% -> 25% of each run, Pallas kernels for 0% -> 15%
where the time goes in v1:
time: 956 us; the launch traced here: 945 us
  waiting for transfers between devices  361 us (38%)
  matrix products  223 us (23%)
  Pallas kernels  143 us (15%)
  blocking collectives  71.9 us (8%)
  other arithmetic  56.9 us (6%)
  local copies, waits for them, and re-layouts  45.9 us (5%)
  starting transfers between devices  27.5 us (3%)
  between operations  15.6 us (2%)
    dot_general x18, matrix products, contract(): lax.dot_general(left, right, (((left_axis,), (right_axis,)), ((), ())), p...  223 us
    pallas_call x2, Pallas kernels, attend_back(): pl.pallas_call(functools.partial(attend_back_kernel, count=count, block=b...  95.4 us
    all_gather x1, waiting for transfers between devices, per_device(): down_whole = lax.all_gather(down_weight.T, 'rows', axis=0, tiled=True)  76.3 us
    all_gather x2, waiting for transfers between devices, per_device(): whole_row = lax.all_gather(tokens[row], 'seq', axis=0, tiled=True)  71.7 us
    all_gather x1, waiting for transfers between devices, per_device(): up_whole = lax.all_gather(up_weight, 'rows', axis=0, tiled=True)  66.7 us
    all_to_all x2, waiting for transfers between devices, per_device(): lax.all_to_all(grad_in, 'seq', split_axis=0, concat_axis=0, tiled=True)  50 us
    pallas_call x2, Pallas kernels, attend(): pl.pallas_call(functools.partial(attend_kernel, count=count, block=block)...  47.5 us
    psum x1, blocking collectives, per_device(): together = lax.psum(together, ('rows', 'seq'))  45.4 us
  transfers between devices with their start and end apart: 19, of which 11 were waited for; matrix products, arithmetic and copies ran while one was open for 25% of the time, Pallas kernels for 15%

profile of v1, /device:TPU:16, one launch (start us, length us, event | category | flops | bytes accessed | tf_op | source)
XLA Modules:
  0.0 945.3 jit_solution(4357229946844506203)
XLA Ops:
  15.5 12.3 %all_gather.47 = bf16[8,16,128]{2,1,0:T(8,128)(2,1)S(1)} all-gather(bf16[1,16,128]{2,1,0:T(8,128)(2,1)S(1)} %pad_bitcast_fusion), channel_id=1, replica_groups=mesh['rows'=8,'seq'=4] {'rows'}, dimensions={0}, use_global_device_ids=true | all-gather | bytes 36864 | tf_op jit(solution)/shard_map/all_gather | solution.py:280
  30.0 38.8 %all-gather.26.cloned.1.call-done = bf16[1,2048,1152]{2,1,0:T(8,128)(2,1)} async-done(((bf16[1,512,1152]{2,1,0:T(8,128)(2,1)}), bf16[1,2048,1152]{2,1,0:T(8,128)(2,1)}) %all-gather.26.cloned.1.call-update) | async-done | bytes 4718608 | tf_op jit(solution)/shard_map/all_gather | solution.py:299
  74.0 25.4 %all-gather.16.cloned.1.call-done = bf16[1152,864]{1,0:T(8,128)(2,1)} async-done(((bf16[144,864]{1,0:T(8,128)(2,1)}), bf16[1152,864]{1,0:T(8,128)(2,1)}) %all-gather.16.cloned.1.call-update) | async-done | bytes 1990672 | tf_op jit(solution)/shard_map/all_gather | solution.py:274
  99.3 8.0 add_convert_fusion
  107.8 25.6 %attend.3 = (bf16[4,288,512]{2,1,0:T(8,128)(2,1)}, f32[8,2048]{1,0:T(8,128)S(1)}) custom-call(s32[8]{0:T(128)S(1)} %get-tuple-element.44.low_ref, s32[8]{0:T(128)S(1)} %get-tuple-element.43.high_ref, bf16[3,288,2048]{2,1,0:T(8,128)(2,1)S(1)} %bitcast.152, s32[2048,128]{1,0:T(8,128)S(1)} %broadcast_in_dim.25.kid_ref, s32[8,2048]{1,0:T(8,128)S(1)} %broadcast_in_dim.26.qid_ref), custom_call_target="tpu_custom_call" | custom-call | flops 6710886400 | bytes 4718592 | tf_op jit(solution)/shard_map/attend/pallas_call | solution.py:92
  134.0 4.5 all-to-all-start.1
  138.5 32.9 %all-gather.24.cloned.1.call-done = bf16[1,2048,1152]{2,1,0:T(8,128)(2,1)} async-done(((bf16[1,512,1152]{2,1,0:T(8,128)(2,1)}), bf16[1,2048,1152]{2,1,0:T(8,128)(2,1)}) %all-gather.24.cloned.1.call-update) | async-done | bytes 4718608 | tf_op jit(solution)/shard_map/all_gather | solution.py:299
  176.6 5.9 add_convert_fusion.1
  182.8 21.9 %attend.2 = (bf16[4,288,512]{2,1,0:T(8,128)(2,1)}, f32[8,2048]{1,0:T(8,128)S(1)}) custom-call(s32[8]{0:T(128)S(1)} %get-tuple-element.42.low_ref, s32[8]{0:T(128)S(1)} %get-tuple-element.41.high_ref, bf16[3,288,2048]{2,1,0:T(8,128)(2,1)S(1)} %bitcast.154, s32[2048,128]{1,0:T(8,128)S(1)} %broadcast_in_dim.22.kid_ref, s32[8,2048]{1,0:T(8,128)S(1)} %broadcast_in_dim.23.qid_ref), custom_call_target="tpu_custom_call" | custom-call | flops 6710886400 | bytes 4718592 | tf_op jit(solution)/shard_map/attend/pallas_call | solution.py:92
  208.8 4.3 all-to-all-start
  213.7 5.8 fusion.30
  219.6 8.7 all-to-all-done
  228.2 4.2 fusion.31
  233.8 66.7 %all-gather.20.cloned.1.call-done = bf16[1152,4304]{1,0:T(8,128)(2,1)} async-done(((bf16[144,4304]{1,0:T(8,128)(2,1)}), bf16[1152,4304]{1,0:T(8,128)(2,1)}) %all-gather.20.cloned.1.call-update) | async-done | bytes 9916432 | tf_op jit(solution)/shard_map/all_gather | solution.py:311
  300.6 19.2 %fusion.47 = f32[1024,4304]{0,1:T(8,128)} fusion(bf16[1152,4304]{1,0:T(8,128)(2,1)} %all-gather.20.cloned.1.call-done, f32[1152]{0:T(1024)S(1)} %add.186, f32[1152]{0:T(1024)S(1)} %mul.202, f32[1024]{0:T(1024)S(1)} %add_rsqrt_fusion.3, f32[1024]{0:T(1024)S(1)} %broadcast_multiply_fusion.6, f32[512,1152]{1,0:T(8,128)S(1)} %copy-done.17, ...), kind=kOutput, calls=%fused_computation.132 | convolution fusion | flops 10161487872 | bytes 32281600 | tf_op jit(solution)/shard_map/dot_general | solution.py:254
  319.7 76.3 %all-gather.22.cloned.1.call-done = bf16[1152,4304]{1,0:T(8,128)(2,1)} async-done(((bf16[144,4304]{1,0:T(8,128)(2,1)}), bf16[1152,4304]{1,0:T(8,128)(2,1)}) %all-gather.22.cloned.1.call-update) | async-done | bytes 9916432 | tf_op jit(solution)/shard_map/all_gather | solution.py:312
  396.1 31.9 %convert_reduce_fusion = (f32[4304]{0:T(1024)}, bf16[1024,4304]{0,1:T(8,128)(2,1)}) fusion(f32[1024,4304]{0,1:T(8,128)} %fusion.47, f32[4304]{0:T(1024)S(1)} %add.189, bf16[1024,1152]{1,0:T(8,128)(2,1)} %bitcast.157, bf16[1152,4304]{1,0:T(8,128)(2,1)} %all-gather.22.cloned.1.call-done), kind=kOutput, calls=%fused_computation.11 | convolution fusion | flops 10260180992 | bytes 38753920 | tf_op jit(solution)/shard_map/dot_general | solution.py:254
  427.9 22.1 %multiply_reduce_fusion = (f32[1152]{0:T(1024)}, f32[1024]{0:T(1024)S(1)}, f32[1024]{0:T(1024)S(1)}, f32[1152]{0:T(1024)}, f32[1024,1152]{1,0:T(8,128)}) fusion(f32[1024]{0:T(1024)S(1)} %add_rsqrt_fusion.3, f32[1024]{0:T(1024)S(1)} %broadcast_multiply_fusion.6, f32[512,1152]{1,0:T(8,128)S(1)} %copy-done.17, f32[512,1152]{1,0:T(8,128)} %copy-done.18, ...), kind=kOutput, calls=%fused_computation.56 | convolution fusion | flops 10166202368 | bytes 28198400 | tf_op jit(solution)/shard_map/dot_general | solution.py:254
  450.1 7.2 convert_reduce_fusion.10
  457.3 3.8 fusion.36
  461.1 4.6 fusion.22
  465.8 18.3 %convolution_convert_fusion.1 = bf16[1152,4304]{1,0:T(8,128)(2,1)} fusion(bf16[1024,4304]{0,1:T(8,128)(2,1)} %get-tuple-element.83, f32[1152]{0:T(1024)S(1)} %add.186, f32[1152]{0:T(1024)S(1)} %mul.202, f32[1024]{0:T(1024)S(1)} %add_rsqrt_fusion.3, f32[1024]{0:T(1024)S(1)} %broadcast_multiply_fusion.6, f32[512,1152]{1,0:T(8,128)S(1)} %copy-done.17, ...), kind=kOutput, calls=%fused_computation.3 | convolution fusion | flops 10166446080 | bytes 23467008 | tf_op jit(solution)/shard_map/dot_general | solution.py:254
  485.8 22.8 %fusion.7 = bf16[1152,4304]{0,1:T(8,128)(2,1)} fusion(bf16[1024,1152]{1,0:T(8,128)(2,1)S(1)} %bitcast.158, f32[1024,4304]{0,1:T(8,128)} %fusion.47, f32[4304]{0:T(1024)S(1)} %add.189), kind=kOutput, calls=%fused_computation.14 | convolution fusion | flops 10203441152 | bytes 29922112 | tf_op jit(solution)/shard_map/dot_general | solution.py:254
  508.7 14.2 %copy.74 = bf16[1152,4304]{1,0:T(8,128)(2,1)} copy(bf16[1152,4304]{0,1:T(8,128)(2,1)} %fusion.7) | data formatting | bytes 19832832
  524.6 4.2 fusion.32
  531.3 4.3 all-to-all-start.2
  535.6 4.2 fusion.33
  542.2 9.1 all-to-all-done.2.gm_ref
  554.9 44.4 %attend_back.2 = bf16[3,288,2048]{2,1,0:T(8,128)(2,1)} custom-call(s32[8]{0:T(128)} %copy-done.9, s32[8]{0:T(128)} %copy-done.8, bf16[3,288,2048]{2,1,0:T(8,128)(2,1)} %bitcast.155, bf16[4,288,512]{2,1,0:T(8,128)(2,1)} %all-to-all-done.2.gm_ref, bf16[4,288,512]{2,1,0:T(8,128)(2,1)} %get-tuple-element.21.out_ref, f32[8,2048]{1,0:T(8,128)} %copy-done.13, ...), custom_call_target="tpu_custom_call" | custom-call | flops 16777216000 | bytes 9437184 | tf_op jit(solution)/shard_map/attend_back/pallas_call | solution.py:199
  599.3 11.3 %fusion.44 = f32[1152,864]{1,0:T(8,128)} fusion(bf16[864,2048]{1,0:T(8,128)(2,1)} %bitcast.167, bf16[1,2048,1152]{2,1,0:T(8,128)(2,1)} %all-gather.24.cloned.1.call-done, f32[1152]{0:T(1024)S(1)} %copy-done.41, f32[1152]{0:T(1024)S(1)} %copy-done.29, f32[2048]{0:T(1024)S(1)} %copy-done.45, f32[2048]{0:T(1024)S(1)} %copy-done.34), kind=kOutput, calls=%fused_computation.131 | convolution fusion | flops 4091019264 | bytes 12264448 | tf_op jit(solution)/shard_map/dot_general | solution.py:254
  611.6 51.0 %attend_back.3 = bf16[3,288,2048]{2,1,0:T(8,128)(2,1)} custom-call(s32[8]{0:T(128)} %copy-done.7, s32[8]{0:T(128)} %copy-done.6, bf16[3,288,2048]{2,1,0:T(8,128)(2,1)} %bitcast.153, bf16[4,288,512]{2,1,0:T(8,128)(2,1)} %copy-done.27, bf16[4,288,512]{2,1,0:T(8,128)(2,1)} %get-tuple-element.22.out_ref, f32[8,2048]{1,0:T(8,128)} %copy-done.12, ...), custom_call_target="tpu_custom_call" | custom-call | flops 16777216000 | bytes 9437184 | tf_op jit(solution)/shard_map/attend_back/pallas_call | solution.py:199
  662.7 12.0 %fusion.29 = bf16[1152,864]{1,0:T(8,128)(2,1)} fusion(f32[1152,864]{1,0:T(8,128)} %fusion.44, bf16[864,2048]{1,0:T(8,128)(2,1)} %bitcast.169, bf16[1,2048,1152]{2,1,0:T(8,128)(2,1)} %all-gather.26.cloned.1.call-done, f32[2048]{0:T(1024)S(1)} %copy-done.43, f32[2048]{0:T(1024)S(1)} %copy-done.32, f32[1152]{0:T(1024)S(1)} %copy-done.41, f32[1152]{0:T(1024)S(1)} %copy-done.29), kind=kOutput, calls=%fused_computation.70 | convolution fusion | flops 4093009920 | bytes 14255104 | tf_op jit(solution)/shard_map/dot_general | solution.py:254
  676.0 10.1 %convolution_convert_fusion.2 = bf16[2048,1152]{1,0:T(8,128)(2,1)} fusion(bf16[864,2048]{1,0:T(8,128)(2,1)} %bitcast.170, bf16[1152,864]{1,0:T(8,128)(2,1)S(1)} %copy-done.56), kind=kOutput, calls=%fused_computation.40 | convolution fusion | flops 4079222784 | bytes 10248192 | tf_op jit(solution)/shard_map/dot_general | solution.py:254
  686.1 5.2 all-to-all-start.5
  693.6 9.6 %convolution_convert_fusion.3 = bf16[2048,1152]{1,0:T(8,128)(2,1)} fusion(bf16[864,2048]{1,0:T(8,128)(2,1)} %bitcast.168, bf16[1152,864]{1,0:T(8,128)(2,1)} %all-gather.16.cloned.1.call-done), kind=kOutput, calls=%fused_computation.41 | convolution fusion | flops 4079222784 | bytes 10248192 | tf_op jit(solution)/shard_map/dot_general | solution.py:254
  703.2 10.5 %reduce-scatter.13.cloned.1.call-done = bf16[144,4304]{1,0:T(8,128)(2,1)} async-done(((bf16[1152,4304]{1,0:T(8,128)(2,1)}), bf16[144,4304]{1,0:T(8,128)(2,1)}) %reduce-scatter.13.cloned.1.call-update) | async-done | bytes 1239568 | tf_op jit(solution)/shard_map/reduce_scatter | solution.py:334
  713.7 23.4 %all-to-all-done.5 = bf16[4,512,1152]{2,1,0:T(8,128)(2,1)} async-done(((bf16[4,512,1152]{2,1,0:T(8,128)(2,1)}), bf16[4,512,1152]{2,1,0:T(8,128)(2,1)}, u32[]{:S(2)}, u32[]{:S(2)}) %all-to-all-start.5) | async-done | bytes 4718624 | tf_op jit(solution)/shard_map/all_to_all | solution.py:355
  737.1 5.0 all-to-all-start.3
  742.1 25.3 %fusion.23 = f32[1024,1152]{1,0:T(8,128)} fusion(bf16[1152,4304]{1,0:T(8,128)(2,1)} %all-gather.22.cloned.1.call-done, f32[1152]{0:T(1024)S(1)} %add.195, f32[512,1152]{1,0:T(8,128)} %fusion.30, f32[512,1152]{1,0:T(8,128)} %copy-done.18, f32[1024,4304]{0,1:T(8,128)} %fusion.47, f32[4304]{0:T(1024)S(1)} %add.189), kind=kOutput, calls=%fused_computation.46 | convolution fusion | flops 10202021888 | bytes 37004608 | tf_op jit(solution)/shard_map/dot_general | solution.py:254
  772.5 6.1 convert_reduce_fusion.3
  778.7 26.6 %all-to-all-done.3 = bf16[4,512,1152]{2,1,0:T(8,128)(2,1)} async-done(((bf16[4,512,1152]{2,1,0:T(8,128)(2,1)}), bf16[4,512,1152]{2,1,0:T(8,128)(2,1)}, u32[]{:S(2)}, u32[]{:S(2)}) %all-to-all-start.3) | async-done | bytes 4718624 | tf_op jit(solution)/shard_map/all_to_all | solution.py:355
  805.3 4.9 convert_reduce_fusion.5
  814.1 45.4 %psum.7 = f32[8,1690]{1,0:T(8,128)S(1)} all-reduce(f32[8,1690]{1,0:T(8,128)S(1)} %concatenate.26), channel_id=1, replica_groups=mesh['rows'=8,'seq'=4] {'rows','seq'}, use_global_device_ids=true, to_apply=%region_30.31 | all-reduce | flops 13520 | bytes 108160 | tf_op jit(solution)/shard_map/psum | solution.py:380
  860.8 6.3 fusion.28
  867.1 14.2 %all-gather.2 = bf16[576,864]{1,0:T(8,128)(2,1)S(1)} all-gather(bf16[144,864]{1,0:T(8,128)(2,1)} %reduce-scatter.7.cloned.1.call-done), channel_id=4, replica_groups=mesh['rows'=8,'seq'=4] {'seq'}, dimensions={0}, use_global_device_ids=true | all-gather | bytes 1244160 | tf_op jit(solution)/shard_map/all_gather | solution.py:390
  889.2 4.8 convert_reduce_fusion.8
  894.1 39.3 %all-gather.32.cloned.1.call-done = bf16[576,4304]{1,0:T(8,128)(2,1)} async-done(((bf16[144,4304]{1,0:T(8,128)(2,1)}), bf16[576,4304]{1,0:T(8,128)(2,1)}) %all-gather.32.cloned.1.call-update) | async-done | bytes 4958224 | tf_op jit(solution)/shard_map/all_gather | solution.py:388
  933.4 4.8 convert_reduce_fusion.7
  (243 shorter events, 62.4 us)
Async XLA Ops:
  7.2 8.1 copy-start.47
  7.2 8.1 copy-start.48
  7.2 8.1 copy-start.49
  7.3 20.5 %copy-start.37 = (s32[2,2048]{1,0:T(2,128)S(1)}, s32[2,2048]{1,0:T(2,128)}, u32[]{:S(2)}) copy-start(s32[2,2048]{1,0:T(2,128)} %param.19) | copy-start | bytes 49156
  7.3 61.5 %all-gather.26.cloned.1.call-start = ((), (), s32[]{:S(2)}) async-start(), calls=%async_computation.18 | async-start | bytes 5898240 | tf_op jit(solution)/shard_map/all_gather | solution.py:299
  10.7 88.7 %all-gather.16.cloned.1.call-start = ((), (), s32[]{:S(2)}) async-start(), calls=%async_computation.10 | async-start | bytes 2322432 | tf_op jit(solution)/shard_map/all_gather | solution.py:274
  12.8 158.6 %all-gather.24.cloned.1.call-start = ((), (), s32[]{:S(2)}) async-start(), calls=%async_computation.17 | async-start | bytes 5898240 | tf_op jit(solution)/shard_map/all_gather | solution.py:299
  13.6 200.2 %all-gather.18.cloned.1.call-start = ((), (), s32[]{:S(2)}) async-start(), calls=%async_computation.11 | async-start | bytes 2985984 | tf_op jit(solution)/shard_map/all_gather | solution.py:310
  14.1 286.4 %all-gather.20.cloned.1.call-start = ((), (), s32[]{:S(2)}) async-start(), calls=%async_computation.12 | async-start | bytes 11280384 | tf_op jit(solution)/shard_map/all_gather | solution.py:311
  14.7 381.3 %all-gather.22.cloned.1.call-start = ((), (), s32[]{:S(2)}) async-start(), calls=%async_computation.13 | async-start | bytes 11280384 | tf_op jit(solution)/shard_map/all_gather | solution.py:312
  29.1 147.4 %copy-start.40 = (f32[1152]{0:T(1024)}, f32[1152]{0:T(1024)S(1)}, u32[]{:S(2)}) copy-start(f32[1152]{0:T(1024)S(1)} %add.171) | copy-start | bytes 13828
  29.2 147.3 %copy-start.28 = (f32[1152]{0:T(1024)}, f32[1152]{0:T(1024)S(1)}, u32[]{:S(2)}) copy-start(f32[1152]{0:T(1024)S(1)} %mul.192) | copy-start | bytes 13828
  29.7 78.0 %copy-start.6 = (s32[8]{0:T(128)}, s32[8]{0:T(128)S(1)}, u32[]{:S(2)}) copy-start(s32[8]{0:T(128)S(1)} %get-tuple-element.43.high_ref) | copy-start | bytes 100
  29.7 78.0 %copy-start.7 = (s32[8]{0:T(128)}, s32[8]{0:T(128)S(1)}, u32[]{:S(2)}) copy-start(s32[8]{0:T(128)S(1)} %get-tuple-element.44.low_ref) | copy-start | bytes 100
  30.0 152.8 %copy-start.8 = (s32[8]{0:T(128)}, s32[8]{0:T(128)S(1)}, u32[]{:S(2)}) copy-start(s32[8]{0:T(128)S(1)} %get-tuple-element.41.high_ref) | copy-start | bytes 100
  30.0 152.8 %copy-start.9 = (s32[8]{0:T(128)}, s32[8]{0:T(128)S(1)}, u32[]{:S(2)}) copy-start(s32[8]{0:T(128)S(1)} %get-tuple-element.42.low_ref) | copy-start | bytes 100
  72.6 34.8 %copy-start.31 = (f32[2048]{0:T(1024)}, f32[2048]{0:T(1024)S(1)}, u32[]{:S(2)}) copy-start(f32[2048]{0:T(1024)S(1)} %broadcast_multiply_fusion) | copy-start | bytes 24580
  74.0 33.4 %copy-start.42 = (f32[2048]{0:T(1024)}, f32[2048]{0:T(1024)S(1)}, u32[]{:S(2)}) copy-start(f32[2048]{0:T(1024)S(1)} %add_rsqrt_fusion) | copy-start | bytes 24580
  107.4 26.0 %copy-start.10 = (bf16[864,2048]{1,0:T(8,128)(2,1)}, bf16[864,2048]{1,0:T(8,128)(2,1)S(1)}, u32[]{:S(2)}) copy-start(bf16[864,2048]{1,0:T(8,128)(2,1)S(1)} %add_convert_fusion) | copy-start | bytes 10616836
  107.7 25.6 %copy-start.2 = (s32[2048,128]{1,0:T(8,128)}, s32[2048,128]{1,0:T(8,128)S(1)}, u32[]{:S(2)}) copy-start(s32[2048,128]{1,0:T(8,128)S(1)} %broadcast_in_dim.25.kid_ref) | copy-start | bytes 3145732
  107.8 25.6 %copy-start.4 = (s32[8,2048]{1,0:T(8,128)}, s32[8,2048]{1,0:T(8,128)S(1)}, u32[]{:S(2)}) copy-start(s32[8,2048]{1,0:T(8,128)S(1)} %broadcast_in_dim.26.qid_ref) | copy-start | bytes 196612
  134.0 74.8 %all-to-all-start.1 = ((bf16[4,288,512]{2,1,0:T(8,128)(2,1)}), bf16[4,288,512]{2,1,0:T(8,128)(2,1)}, u32[]{:S(2)}, u32[]{:S(2)}) async-start(bf16[4,288,512]{2,1,0:T(8,128)(2,1)} %get-tuple-element.22.out_ref), calls=%async_computation.1 | async-start | bytes 2359296 | tf_op jit(solution)/shard_map/all_to_all | solution.py:307
  182.8 30.9 %copy-start.14 = (bf16[2,512,1152]{2,1,0:T(8,128)(2,1)S(1)}, bf16[2,512,1152]{2,1,0:T(8,128)(2,1)}, u32[]{:S(2)}) copy-start(bf16[2,512,1152]{2,1,0:T(8,128)(2,1)} %param.18) | copy-start | bytes 7077892
  208.8 19.4 %all-to-all-start = ((bf16[4,288,512]{2,1,0:T(8,128)(2,1)}), bf16[4,288,512]{2,1,0:T(8,128)(2,1)}, u32[]{:S(2)}, u32[]{:S(2)}) async-start(bf16[4,288,512]{2,1,0:T(8,128)(2,1)} %get-tuple-element.21.out_ref), calls=%async_computation | async-start | bytes 2359296 | tf_op jit(solution)/shard_map/all_to_all | solution.py:307
  213.1 461.6 %reduce-scatter.9.cloned.1.call-start = ((), (), s32[]{:S(2)}) async-start(), calls=%async_computation.15 | async-start | bytes 2985984 | tf_op jit(solution)/shard_map/reduce_scatter | solution.py:343
  232.4 68.1 %copy-start.17 = (f32[512,1152]{1,0:T(8,128)S(1)}, f32[512,1152]{1,0:T(8,128)}, u32[]{:S(2)}) copy-start(f32[512,1152]{1,0:T(8,128)} %fusion.30) | copy-start | bytes 7077892
  465.7 209.7 %reduce-scatter.11.cloned.1.call-start = ((), (), s32[]{:S(2)}) async-start(), calls=%async_computation.16 | async-start | bytes 11280384 | tf_op jit(solution)/shard_map/reduce_scatter | solution.py:335
  484.1 229.6 %reduce-scatter.13.cloned.1.call-start = ((), (), s32[]{:S(2)}) async-start(), calls=%async_computation.22 | async-start | bytes 11280384 | tf_op jit(solution)/shard_map/reduce_scatter | solution.py:334
  531.3 20.0 %all-to-all-start.2 = ((bf16[4,288,512]{2,1,0:T(8,128)(2,1)}), bf16[4,288,512]{2,1,0:T(8,128)(2,1)}, u32[]{:S(2)}, u32[]{:S(2)}) async-start(bf16[4,288,512]{2,1,0:T(8,128)(2,1)} %bitcast.163), calls=%async_computation.2 | async-start | bytes 2359296 | tf_op jit(solution)/shard_map/all_to_all | solution.py:347
  551.3 59.3 %all-to-all-start.4 = ((bf16[4,288,512]{2,1,0:T(8,128)(2,1)}), bf16[4,288,512]{2,1,0:T(8,128)(2,1)S(1)}, u32[]{:S(2)}, u32[]{:S(2)}) async-start(bf16[4,288,512]{2,1,0:T(8,128)(2,1)} %bitcast.23), calls=%async_computation.4 | async-start | bytes 2359296 | tf_op jit(solution)/shard_map/all_to_all | solution.py:347
  554.8 312.3 %reduce-scatter.7.cloned.1.call-start = ((), (), s32[]{:S(2)}) async-start(), calls=%async_computation.14 | async-start | bytes 2322432 | tf_op jit(solution)/shard_map/reduce_scatter | solution.py:359
  554.9 44.4 %copy-start.29 = (f32[1152]{0:T(1024)S(1)}, f32[1152]{0:T(1024)}, u32[]{:S(2)}) copy-start(f32[1152]{0:T(1024)} %copy-done.28) | copy-start | bytes 13828
  554.9 44.4 %copy-start.34 = (f32[2048]{0:T(1024)S(1)}, f32[2048]{0:T(1024)}, u32[]{:S(2)}) copy-start(f32[2048]{0:T(1024)} %copy-done.33) | copy-start | bytes 24580
  554.9 44.4 %copy-start.41 = (f32[1152]{0:T(1024)S(1)}, f32[1152]{0:T(1024)}, u32[]{:S(2)}) copy-start(f32[1152]{0:T(1024)} %copy-done.40) | copy-start | bytes 13828
  554.9 44.4 %copy-start.45 = (f32[2048]{0:T(1024)S(1)}, f32[2048]{0:T(1024)}, u32[]{:S(2)}) copy-start(f32[2048]{0:T(1024)} %copy-done.44) | copy-start | bytes 24580
  611.6 51.0 %copy-start.32 = (f32[2048]{0:T(1024)S(1)}, f32[2048]{0:T(1024)}, u32[]{:S(2)}) copy-start(f32[2048]{0:T(1024)} %copy-done.31) | copy-start | bytes 24580
  611.6 51.0 %copy-start.43 = (f32[2048]{0:T(1024)S(1)}, f32[2048]{0:T(1024)}, u32[]{:S(2)}) copy-start(f32[2048]{0:T(1024)} %copy-done.42) | copy-start | bytes 24580
  662.7 13.3 %copy-start.56 = (bf16[1152,864]{1,0:T(8,128)(2,1)S(1)}, bf16[1152,864]{1,0:T(8,128)(2,1)}, u32[]{:S(2)}) copy-start(bf16[1152,864]{1,0:T(8,128)(2,1)} %all-gather.16.cloned.1.call-done) | copy-start | bytes 5971972
  674.6 212.2 %all-gather.28.cloned.1.call-start = ((), (), s32[]{:S(2)}) async-start(), calls=%async_computation.19 | async-start | bytes 1658880 | tf_op jit(solution)/shard_map/all_gather | solution.py:388
  675.4 213.9 %all-gather.30.cloned.1.call-start = ((), (), s32[]{:S(2)}) async-start(), calls=%async_computation.20 | async-start | bytes 6266880 | tf_op jit(solution)/shard_map/all_gather | solution.py:388
  686.1 51.0 %all-to-all-start.5 = ((bf16[4,512,1152]{2,1,0:T(8,128)(2,1)}), bf16[4,512,1152]{2,1,0:T(8,128)(2,1)}, u32[]{:S(2)}, u32[]{:S(2)}) async-start(bf16[4,512,1152]{2,1,0:T(8,128)(2,1)} %bitcast.161), calls=%async_computation.5 | async-start | bytes 9437184 | tf_op jit(solution)/shard_map/all_to_all | solution.py:355
  691.3 242.1 %all-gather.32.cloned.1.call-start = ((), (), s32[]{:S(2)}) async-start(), calls=%async_computation.21 | async-start | bytes 6266880 | tf_op jit(solution)/shard_map/all_gather | solution.py:388
  737.1 68.2 %all-to-all-start.3 = ((bf16[4,512,1152]{2,1,0:T(8,128)(2,1)}), bf16[4,512,1152]{2,1,0:T(8,128)(2,1)}, u32[]{:S(2)}, u32[]{:S(2)}) async-start(bf16[4,512,1152]{2,1,0:T(8,128)(2,1)} %bitcast.162), calls=%async_computation.3 | async-start | bytes 9437184 | tf_op jit(solution)/shard_map/all_to_all | solution.py:355
  742.1 25.4 %copy-start.30 = (f32[1152]{0:T(1024)S(1)}, f32[1152]{0:T(1024)}, u32[]{:S(2)}) copy-start(f32[1152]{0:T(1024)} %get-tuple-element.45) | copy-start | bytes 13828
  742.1 25.4 %copy-start.39 = (f32[1152]{0:T(1024)S(1)}, f32[1152]{0:T(1024)}, u32[]{:S(2)}) copy-start(f32[1152]{0:T(1024)} %get-tuple-element.25) | copy-start | bytes 13828
  742.1 25.5 %copy-start.38 = (f32[1152]{0:T(1024)S(1)}, f32[1152]{0:T(1024)}, u32[]{:S(2)}) copy-start(f32[1152]{0:T(1024)} %get-tuple-element.28) | copy-start | bytes 13828
  742.1 25.6 %copy-start.36 = (f32[4304]{0:T(1024)S(1)}, f32[4304]{0:T(1024)}, u32[]{:S(2)}) copy-start(f32[4304]{0:T(1024)} %get-tuple-element.82) | copy-start | bytes 51652
  889.2 49.0 %copy-start.1 = (bf16[144,1152]{1,0:T(8,128)(2,1)S(1)}, bf16[144,1152]{1,0:T(8,128)(2,1)}, u32[]{:S(2)}) copy-start(bf16[144,1152]{1,0:T(8,128)(2,1)} %param.22) | copy-start | bytes 995332
  (28 other events, 115.1 us)
Sparse Core Ops, SparseCore 0:
  10.8 57.9 all-gather.25
  71.0 28.2 all-gather.15
  101.8 69.5 all-gather.23
  172.9 32.1 all-gather.17
  206.6 93.9 all-gather.19
  302.1 93.9 all-gather.21
  465.8 32.4 reduce-scatter.8
  500.7 107.1 reduce-scatter.10
  610.2 103.4 reduce-scatter.12
  715.9 30.2 reduce-scatter.6
  748.0 54.3 all-gather.27
  804.0 67.2 all-gather.29
  873.2 60.1 all-gather.31

commit v2 on v1

v2 whole, which is shorter than its diff:
```python
import functools
import jax
import jax.numpy as jnp
from jax import lax
from jax.experimental import pallas as pl
from jax.experimental.pallas import tpu as pltpu
from jax.sharding import PartitionSpec as P


HEAD_SIZE = 72
EPS = 1e-06
NEGATIVE = -1e30
LOG2E = 1.4426950408889634
PAD = 128
ROWS = 80


def split_refs(source, count):
    wide = source.astype(jnp.float32)
    return [wide[HEAD_SIZE * h : HEAD_SIZE * (h + 1)] for h in range(count)]


def grow_rows(value, rows):
    return jnp.concatenate([value, jnp.zeros((rows - value.shape[0], value.shape[1]), value.dtype)], axis=0)


def swap_chunk(part, per, place):
    return lax.bitwise_xor(part // per, place) * per + part % per


def same_picture(kid_ref, qid_ref, key_start, query_start, block):
    key_ids = kid_ref[pl.ds(key_start, block), :]
    key_ids = jnp.concatenate([key_ids] * (block // 128), axis=1)
    return key_ids == qid_ref[0:1, pl.ds(query_start, block)]


def attend_kernel(low_ref, high_ref, place_ref, qkv_ref, kid_ref, qid_ref, out_ref, log_ref, q_t, k_n, v_t, kept, top, total, acc, *, count, block, chunk):
    step = pl.program_id(0)
    length = qkv_ref.shape[2]
    per = chunk // block
    factor = HEAD_SIZE ** (-0.5) * LOG2E

    @pl.when(step == 0)
    def _():
        @pl.loop(0, length // block)
        def _(part):
            near = pl.ds(pl.multiple_of(part * block, block), block)
            at = pl.ds(pl.multiple_of(swap_chunk(part, per, place_ref[0]) * block, block), block)
            for h, value in enumerate(split_refs(qkv_ref[0, :, near], count)):
                q_t[h, :, at] = grow_rows(value, PAD).astype(jnp.bfloat16)
            for h, value in enumerate(split_refs(qkv_ref[1, :, near], count)):
                k_n[h, at, :] = grow_rows(value, PAD).T.astype(jnp.bfloat16)
            for h, value in enumerate(split_refs(qkv_ref[2, :, near], count)):
                v_t[h, :, at] = grow_rows(value, ROWS).astype(jnp.bfloat16)

    top[...] = jnp.full(top.shape, NEGATIVE, jnp.float32)
    total[...] = jnp.zeros(total.shape, jnp.float32)
    acc[...] = jnp.zeros(acc.shape, jnp.float32)
    query_start = pl.multiple_of(step * block, block)
    queries = pl.ds(query_start, block)

    def first(index, _):
        key_start = pl.multiple_of(index * block, block)
        mask = same_picture(kid_ref, qid_ref, key_start, query_start, block)
        for h in range(count):
            scores = jnp.dot(
                k_n[h, pl.ds(key_start, block), :], q_t[h, :, queries], preferred_element_type=jnp.float32
            )
            scores = jnp.where(mask, scores * factor, NEGATIVE)
            kept[h, pl.ds(key_start, block), :] = scores
            top[h] = jnp.maximum(top[h], jnp.max(scores.reshape(block // 8, 8, block), axis=0))
        return 0

    lax.fori_loop(low_ref[step], high_ref[step], first, 0)
    highest = [jnp.max(top[h], axis=0, keepdims=True) for h in range(count)]

    def second(index, _):
        keys = pl.ds(pl.multiple_of(index * block, block), block)
        for h in range(count):
            probs = jnp.exp2(kept[h, keys, :] - highest[h])
            total[h] += jnp.sum(probs.reshape(block // 8, 8, block), axis=0)
            acc[h] += jnp.dot(v_t[h, :, keys], probs.astype(jnp.bfloat16), preferred_element_type=jnp.float32)
        return 0

    lax.fori_loop(low_ref[step], high_ref[step], second, 0)
    sums = [jnp.sum(total[h], axis=0, keepdims=True) for h in range(count)]
    for h in range(count):
        log_ref[h : h + 1, :] = highest[h] + jnp.log2(sums[h])
    out_ref[0] = jnp.concatenate([acc[h, :HEAD_SIZE] / sums[h] for h in range(count)], axis=0).astype(jnp.bfloat16)


def attend(qkv, low, high, key_ids, query_ids, place, chunk):
    _, width, length = qkv.shape
    count = width // HEAD_SIZE
    block = min(256, chunk)
    per = chunk // block
    whole = lambda *shape: pl.BlockSpec(shape, lambda i, *_: (0,) * len(shape))
    area = length * length * count // 2
    return pl.pallas_call(
        functools.partial(attend_kernel, count=count, block=block, chunk=chunk),
        name="attend",
        grid_spec=pltpu.PrefetchScalarGridSpec(
            num_scalar_prefetch=3,
            grid=(length // block,),
            in_specs=[whole(3, width, length), whole(length, 128), whole(8, length)],
            out_specs=[
                pl.BlockSpec((1, width, block), lambda i, low, high, place: (lax.bitwise_xor(i // per, place[0]), 0, i % per)),
                pl.BlockSpec((max(8, count), block), lambda i, *_: (0, i)),
            ],
            scratch_shapes=[
                pltpu.VMEM((count, PAD, length), jnp.bfloat16),
                pltpu.VMEM((count, length, PAD), jnp.bfloat16),
                pltpu.VMEM((count, ROWS, length), jnp.bfloat16),
                pltpu.VMEM((count, length, block), jnp.float32),
                pltpu.VMEM((count, 8, block), jnp.float32),
                pltpu.VMEM((count, 8, block), jnp.float32),
                pltpu.VMEM((count, ROWS, block), jnp.float32),
            ],
        ),
        out_shape=[
            jax.ShapeDtypeStruct((length // chunk, width, chunk), jnp.bfloat16),
            jax.ShapeDtypeStruct((max(8, count), length), jnp.float32),
        ],
        compiler_params=pltpu.CompilerParams(vmem_limit_bytes=40 << 20),
        cost_estimate=pl.CostEstimate(flops=area * 800, transcendentals=area, bytes_accessed=8 * length * width),
    )(low, high, place, qkv, key_ids, query_ids)


def attend_back_kernel(
    low_ref, high_ref, place_ref, qkv_ref, out_ref, log_ref, kid_ref, qid_ref, *rest, count, block, chunks,
):
    gm_refs, grad_ref = rest[:chunks], rest[chunks]
    q_t, k_t, k_n, v_n, g_t, delta, gq, gk, gv = rest[chunks + 1 :]
    step = pl.program_id(0)
    length = qkv_ref.shape[2]
    chunk = length // chunks
    per = chunk // block
    place = place_ref[0]
    scale = HEAD_SIZE ** (-0.5)
    factor = scale * LOG2E

    @pl.when(step == 0)
    def _():
        gq[...] = jnp.zeros(gq.shape, jnp.float32)

        @pl.loop(0, length // block)
        def _(part):
            near = pl.ds(pl.multiple_of(part * block, block), block)
            at = pl.ds(pl.multiple_of(swap_chunk(part, per, place) * block, block), block)
            for h, value in enumerate(split_refs(qkv_ref[0, :, near], count)):
                q_t[h, :, at] = grow_rows(value, PAD).astype(jnp.bfloat16)
            for h, value in enumerate(split_refs(qkv_ref[1, :, near], count)):
                value = grow_rows(value, PAD)
                k_t[h, :, at] = value[:ROWS].astype(jnp.bfloat16)
                k_n[h, at, :] = value.T.astype(jnp.bfloat16)
            for h, value in enumerate(split_refs(qkv_ref[2, :, near], count)):
                v_n[h, at, :] = grow_rows(value, PAD).T.astype(jnp.bfloat16)

        for piece in range(chunks):
            at = pl.ds(pl.multiple_of(lax.bitwise_xor(piece, place) * chunk, chunk), chunk)
            grads = split_refs(gm_refs[piece][...], count)
            outs = split_refs(out_ref[piece], count)
            for h in range(count):
                g_t[h, :, at] = grow_rows(grads[h], PAD).astype(jnp.bfloat16)
                delta[h, :, at] = jnp.sum(grads[h] * outs[h], axis=0, keepdims=True)

    gk[...] = jnp.zeros(gk.shape, jnp.float32)
    gv[...] = jnp.zeros(gv.shape, jnp.float32)
    key_start = pl.multiple_of(step * block, block)
    keys = pl.ds(key_start, block)

    def one(index, _):
        query_start = pl.multiple_of(index * block, block)
        queries = pl.ds(query_start, block)
        mask = same_picture(kid_ref, qid_ref, key_start, query_start, block)
        for h in range(count):
            scores = jnp.dot(k_n[h, keys, :], q_t[h, :, queries], preferred_element_type=jnp.float32)
            probs = jnp.where(mask, jnp.exp2(scores * factor - log_ref[h : h + 1, queries]), 0.0)
            back = jnp.dot(v_n[h, keys, :], g_t[h, :, queries], preferred_element_type=jnp.float32)
            slope = (probs * (back - delta[h, :, queries])).astype(jnp.bfloat16)
            nt = (((1,), (1,)), ((), ()))
            gv[h] += lax.dot_general(
                g_t[h, :ROWS, queries], probs.astype(jnp.bfloat16), nt, preferred_element_type=jnp.float32
            )
            gk[h] += lax.dot_general(q_t[h, :ROWS, queries], slope, nt, preferred_element_type=jnp.float32)
            gq[h, :, queries] += jnp.dot(k_t[h, :, keys], slope, preferred_element_type=jnp.float32)
        return 0

    lax.fori_loop(low_ref[step], high_ref[step], one, 0)
    near = pl.ds(pl.multiple_of(swap_chunk(step, per, place) * block, block), block)
    grad_ref[1, :, near] = (jnp.concatenate([gk[h, :HEAD_SIZE] for h in range(count)], axis=0) * scale).astype(jnp.bfloat16)
    grad_ref[2, :, near] = jnp.concatenate([gv[h, :HEAD_SIZE] for h in range(count)], axis=0).astype(jnp.bfloat16)

    @pl.when(step == pl.num_programs(0) - 1)
    def _():
        @pl.loop(0, length // block)
        def _(part):
            near = pl.ds(pl.multiple_of(part * block, block), block)
            at = pl.ds(pl.multiple_of(swap_chunk(part, per, place) * block, block), block)
            grad_ref[0, :, near] = (
                jnp.concatenate([gq[h, :HEAD_SIZE, at] for h in range(count)], axis=0) * scale
            ).astype(jnp.bfloat16)


def attend_back(qkv, grad_mixed, mixed, logsum, low, high, key_ids, query_ids, place):
    _, width, length = qkv.shape
    chunk = mixed.shape[2]
    count = width // HEAD_SIZE
    block = min(256, chunk)
    whole = lambda *shape: pl.BlockSpec(shape, lambda i, *_: (0,) * len(shape))
    area = length * length * count // 2
    return pl.pallas_call(
        functools.partial(attend_back_kernel, count=count, block=block, chunks=mixed.shape[0]),
        name="attend_back",
        grid_spec=pltpu.PrefetchScalarGridSpec(
            num_scalar_prefetch=3,
            grid=(length // block,),
            in_specs=[
                whole(3, width, length),
                whole(*mixed.shape),
                whole(max(8, count), length),
                whole(length, 128),
                whole(8, length),
            ]
            + [whole(*piece.shape) for piece in grad_mixed],
            out_specs=whole(3, width, length),
            scratch_shapes=[
                pltpu.VMEM((count, PAD, length), jnp.bfloat16),
                pltpu.VMEM((count, ROWS, length), jnp.bfloat16),
                pltpu.VMEM((count, length, PAD), jnp.bfloat16),
                pltpu.VMEM((count, length, PAD), jnp.bfloat16),
                pltpu.VMEM((count, PAD, length), jnp.bfloat16),
                pltpu.VMEM((count, 1, length), jnp.float32),
                pltpu.VMEM((count, ROWS, length), jnp.float32),
                pltpu.VMEM((count, ROWS, block), jnp.float32),
                pltpu.VMEM((count, ROWS, block), jnp.float32),
            ],
        ),
        out_shape=jax.ShapeDtypeStruct((3, width, length), jnp.bfloat16),
        compiler_params=pltpu.CompilerParams(vmem_limit_bytes=60 << 20),
        cost_estimate=pl.CostEstimate(flops=area * 2000, transcendentals=area, bytes_accessed=16 * length * width),
    )(low, high, place, qkv, mixed, logsum, key_ids, query_ids, *grad_mixed)


def block_ranges(ids, block):
    ids = jnp.where(ids < 0, 1 << 20, ids).reshape(-1, block)
    first, last = ids[:, 0], ids[:, -1]
    low = jnp.sum((last[None, :] < first[:, None]).astype(jnp.int32), axis=1)
    high = jnp.sum((first[None, :] <= last[:, None]).astype(jnp.int32), axis=1)
    return low, high


def norm_parts(value_rows):
    center = value_rows - jnp.mean(value_rows, axis=-1, keepdims=True)
    inverse = lax.rsqrt(jnp.mean(center * center, axis=-1, keepdims=True) + EPS)
    return center * inverse, inverse


def norm_back(grad, normed, inverse, gain):
    scaled = grad * gain
    flat = jnp.mean(scaled, axis=-1, keepdims=True)
    along = jnp.mean(scaled * normed, axis=-1, keepdims=True)
    return inverse * (scaled - flat - normed * along)


def contract(left, right, left_axis, right_axis):
    return lax.dot_general(left, right, (((left_axis,), (right_axis,)), ((), ())), preferred_element_type=jnp.float32)


def per_device(
    tokens, picture_ids, attn_gain, attn_shift, query_weight, query_bias, key_weight, value_weight, value_bias,
    output_weight, output_bias, mlp_gain, mlp_shift, up_weight, up_bias, down_weight, down_bias, cotangent,
    *, seq_count, row_count,
):
    count, chunk, width = tokens.shape
    length = chunk * seq_count
    part = width // seq_count
    band_width = width // row_count
    hidden_size = up_weight.shape[1]
    slab = -(-hidden_size // (seq_count * 128)) * 128
    place = lax.axis_index("seq")
    place_array = place.reshape(1).astype(jnp.int32)
    block = min(256, chunk)
    f32, bf16 = jnp.float32, jnp.bfloat16
    rest = range(1, seq_count)

    def swap(value, hop):
        return lax.ppermute(value, "seq", [(i, i ^ hop) for i in range(seq_count)])

    def own_columns(weight):
        return lax.dynamic_slice_in_dim(weight, place * part, part, axis=1)

    def relative(stacked):
        return [lax.dynamic_index_in_dim(stacked, place ^ hop, axis=0, keepdims=False) for hop in range(seq_count)]

    whole_rows = [[tokens[row]] for row in range(count)]
    token_rows = [tokens[row] for row in range(count)]
    for row in range(count):
        if row:
            held = lax.optimization_barrier((token_rows[row], *whole_rows[row - 1][1:]))
            token_rows[row], whole_rows[row - 1][1:] = held[0], list(held[1:])
        whole_rows[row] += [swap(token_rows[row], hop) for hop in rest]

    small = [attn_gain, attn_shift, query_bias, value_bias, output_bias, mlp_gain, mlp_shift, down_bias]
    wide = -(-up_bias.shape[0] // band_width)
    up_columns = jnp.pad(up_bias, (0, wide * band_width - up_bias.shape[0])).reshape(wide, band_width).T
    heads_shard = jnp.concatenate(
        [own_columns(query_weight), own_columns(key_weight), own_columns(value_weight), jnp.stack(small, axis=1), up_columns],
        axis=1,
    )
    gathered = lax.all_gather(heads_shard, "rows", axis=0, tiled=True)
    heads_weight = gathered[:, : 3 * part]
    extra = gathered[:, 3 * part :].astype(f32)
    gain1, shift1, query_off, value_off, output_off, gain2, shift2, down_off = [extra[:, i] for i in range(8)]
    up_off = extra[:, 8:].reshape(row_count, band_width, wide).transpose(0, 2, 1).reshape(row_count, wide * band_width)
    up_off = up_off[:, : up_bias.shape[0]].reshape(hidden_size)
    up_off = relative(jnp.pad(up_off, (0, slab * seq_count - hidden_size)).reshape(seq_count, slab))
    heads_off = jnp.concatenate(
        [
            lax.dynamic_slice_in_dim(query_off, place * part, part),
            jnp.zeros((part,), f32),
            lax.dynamic_slice_in_dim(value_off, place * part, part),
        ]
    )

    def in_slabs(weight):
        return jnp.pad(weight, ((0, 0), (0, slab * seq_count - hidden_size)))

    def own_slab(weight, hop):
        return lax.dynamic_slice_in_dim(weight, (place ^ hop) * slab, slab, axis=1)

    down_own = lax.all_gather(own_slab(in_slabs(down_weight.T), 0), "rows", axis=0, tiled=True)
    output_whole = lax.all_gather(output_weight, "rows", axis=0, tiled=True)
    near_up = jnp.concatenate([own_slab(in_slabs(up_weight), hop) for hop in range(seq_count)], axis=1)
    up_whole = lax.all_gather(near_up, "rows", axis=0, tiled=True)
    held = lax.optimization_barrier((down_own, *whole_rows[-1][1:]))
    down_own, whole_rows[-1][1:] = held[0], list(held[1:])
    downs = [down_own] + [swap(down_own, hop) for hop in rest]
    up_off = jnp.concatenate(up_off)
    outputs = relative(output_whole.reshape(seq_count, part, width))

    attn_inputs, packs, mixes, logs, tables, mixed_own = [], [], [], [], [], []
    for row in range(count):
        ids = picture_ids[row]
        low, high = block_ranges(ids, block)
        tables.append((low, high, jnp.broadcast_to(ids[:, None], (length, 128)), jnp.broadcast_to(ids[None], (8, length))))
        attn_input = jnp.concatenate(
            [(norm_parts(piece.astype(f32))[0] * gain1 + shift1).astype(bf16) for piece in whole_rows[row]], axis=0
        )
        pack = (contract(heads_weight, attn_input, 0, 1) + heads_off[:, None]).astype(bf16).reshape(3, part, length)
        mixed, logsum = attend(pack, *tables[row], place_array, chunk)
        attn_inputs.append(attn_input)
        packs.append(pack)
        mixes.append(mixed)
        logs.append(logsum)
        mixed_own.append([mixed[0]] + [swap(mixed[hop], hop) for hop in rest])

    mixed_all = jnp.concatenate(
        [jnp.concatenate([mixed_own[row][hop] for row in range(count)], axis=1) for hop in range(seq_count)], axis=0
    )
    output_near = jnp.concatenate(outputs, axis=0)
    tokens_own = tokens.reshape(count * chunk, width).astype(f32)
    resid = tokens_own + (contract(mixed_all, output_near, 0, 0) + output_off)
    normed2, inverse2 = norm_parts(resid)
    mlp_input = (normed2 * gain2 + shift2).astype(bf16)
    total = None
    hidden = contract(mlp_input, up_whole, 1, 0) + up_off
    gelu_out, pull = jax.vjp(lambda v: jax.nn.gelu(v, approximate=True), hidden)
    gelu_out, slope = gelu_out.astype(bf16), pull(jnp.ones_like(hidden))[0].astype(bf16)

    def slab_of(value, hop):
        return value[:, hop * slab : (hop + 1) * slab]

    for hop in range(seq_count):
        term = contract(slab_of(gelu_out, hop), downs[hop], 1, 1)
        total = term if total is None else total + term
    activations = resid + total + down_off

    def exchange_sum(pieces):
        total = pieces[0].astype(f32)
        for hop in rest:
            total = total + swap(pieces[hop], hop).astype(f32)
        return total

    cot = cotangent.reshape(count * chunk, width)
    grad_down = contract(cot, gelu_out, 0, 0).astype(bf16)
    cot, grad_down = lax.optimization_barrier((cot, grad_down))
    down_raw = lax.psum_scatter(grad_down, "rows", scatter_dimension=0, tiled=True)
    grad_hidden = jnp.concatenate(
        [(contract(cot, downs[hop], 1, 0) * slab_of(slope, hop).astype(f32)).astype(bf16) for hop in range(seq_count)], axis=1
    )
    grad_mlp_input = contract(grad_hidden, up_whole, 1, 1)
    grad_up = contract(mlp_input, grad_hidden, 0, 0).astype(bf16)
    grad_resid = cot.astype(f32) + norm_back(grad_mlp_input, normed2, inverse2, gain2)
    grad_attn = grad_resid.astype(bf16)

    grad_output = contract(mixed_all, grad_attn, 1, 0)
    grad_output = relative(grad_output.astype(bf16).reshape(seq_count, part, width))
    grad_output = jnp.concatenate(grad_output, axis=0)
    packs[0], down_raw, grad_up, grad_output = lax.optimization_barrier((packs[0], down_raw, grad_up, grad_output))
    up_raw = lax.psum_scatter(grad_up, "rows", scatter_dimension=0, tiled=True)
    down_share = exchange_sum([slab_of(down_raw, hop) for hop in range(seq_count)]).astype(bf16)
    heads_grad, query_grad, value_grad, gain_grad, shift_grad, grad_in = None, 0.0, 0.0, 0.0, 0.0, []
    after = None
    for row in range(count):
        grad_mixed = []
        for hop in range(seq_count):
            piece = contract(outputs[hop], grad_attn[row * chunk : (row + 1) * chunk], 1, 1).astype(bf16)
            grad_mixed.append(swap(piece, hop) if hop else piece)
        pack = packs[row]
        if after is not None:
            pack, grad_in[-1] = lax.optimization_barrier((pack, grad_in[-1]))
        grad_pack = attend_back(pack, grad_mixed, mixes[row], logs[row], *tables[row], place_array)
        if row == count - 1:
            grad_pack, up_raw, grad_output = lax.optimization_barrier((grad_pack, up_raw, grad_output))
            output_share = lax.psum_scatter(grad_output, "rows", scatter_dimension=0, tiled=True)
            up_share = exchange_sum([slab_of(up_raw, hop) for hop in range(seq_count)]).astype(bf16)
        query_grad = query_grad + jnp.sum(grad_pack[0].astype(f32), axis=1)
        value_grad = value_grad + jnp.sum(grad_pack[2].astype(f32), axis=1)
        grad_pack = grad_pack.reshape(3 * part, length)
        partial = []
        for hop in range(seq_count):
            piece = contract(grad_pack[:, hop * chunk : (hop + 1) * chunk], heads_weight, 0, 1)
            gain_grad = gain_grad + jnp.sum(piece * norm_parts(whole_rows[row][hop].astype(f32))[0], axis=0)
            shift_grad = shift_grad + jnp.sum(piece, axis=0)
            partial.append(piece.astype(bf16))
        grad_in.append(partial)
        after = partial
        term = contract(attn_inputs[row], grad_pack, 0, 1)
        heads_grad = term if heads_grad is None else heads_grad + term

    def placed(value):
        return lax.dynamic_update_slice_in_dim(jnp.zeros((width,), f32), value, place * part, axis=0)

    up_grads = jnp.stack(relative(jnp.sum(grad_hidden.astype(f32), axis=0).reshape(seq_count, slab)))
    small_grads = [
        gain_grad,
        shift_grad,
        placed(query_grad),
        placed(value_grad),
        jnp.sum(grad_attn.astype(f32), axis=0),
        jnp.sum(grad_mlp_input * normed2, axis=0),
        jnp.sum(grad_mlp_input, axis=0),
        jnp.sum(cot.astype(f32), axis=0),
        up_grads.reshape(slab * seq_count)[:hidden_size],
    ]
    together = jnp.concatenate([value.reshape(row_count, -1) for value in small_grads], axis=1)
    sizes = [value.shape[0] // row_count for value in small_grads]
    filled = -(-together.shape[1] // 2048) * 2048
    together = jnp.pad(together, ((0, 0), (0, filled - together.shape[1]))).reshape(row_count * filled // 128, 128)
    heads_grad = heads_grad.astype(bf16)
    heads_grad, output_share = lax.optimization_barrier((heads_grad, output_share))
    heads_share = lax.psum_scatter(heads_grad, "rows", scatter_dimension=0, tiled=True)
    together, heads_share = lax.optimization_barrier((together, heads_share))
    small_share = lax.psum_scatter(together, "rows", scatter_dimension=0, tiled=True)

    normed1, inverse1 = norm_parts(tokens_own)
    sums = []
    for row in range(count):
        sums.append(exchange_sum(grad_in[row]))
    grad_attn_input = jnp.concatenate(sums, axis=0)
    token_grad = grad_resid + norm_back(grad_attn_input, normed1, inverse1, gain1)

    def all_pieces(share):
        stacked = jnp.stack([share] + [swap(share, hop) for hop in rest])
        return relative(stacked)

    def seq_sum(share):
        total = share.astype(f32)
        for hop in rest:
            total = total + swap(share, hop).astype(f32)
        return total

    heads_all = [piece.astype(f32) for piece in all_pieces(heads_share)]
    small_sum = seq_sum(small_share).reshape(-1)
    vectors, start = [], 0
    for size in sizes:
        vectors.append(small_sum[start : start + size])
        start += size

    def take(which):
        return jnp.concatenate([piece[:, which * part : (which + 1) * part] for piece in heads_all], axis=1)

    def slabs(share):
        return jnp.concatenate([piece.astype(f32) for piece in all_pieces(share)], axis=1)[:, :hidden_size]

    return (
        activations.reshape(count, chunk, width),
        token_grad.reshape(count, chunk, width),
        vectors[0],
        vectors[1],
        take(0),
        vectors[2],
        take(1),
        take(2),
        vectors[3],
        seq_sum(output_share),
        vectors[4],
        vectors[5],
        vectors[6],
        slabs(up_share),
        vectors[8],
        slabs(down_share).T,
        vectors[7],
    )


def solution(mesh):
    matrix, vector, batch = P("rows", None), P("rows"), P("rows", "seq", None)
    columns = P(None, "rows")

    def body(*arguments):
        return per_device(*arguments, seq_count=mesh.shape["seq"], row_count=mesh.shape["rows"])

    return jax.shard_map(
        body,
        mesh=mesh,
        in_specs=(
            batch, matrix, vector, vector, matrix, vector, matrix, matrix, vector, matrix, vector, vector, vector, matrix,
            vector, columns, vector, batch,
        ),
        out_specs=(
            batch, batch, vector, vector, matrix, vector, matrix, matrix, vector, matrix, vector, vector, vector, matrix,
            vector, columns, vector,
        ),
        check_vma=False,
    )
```

time: 956 us -> 902 us (0.944)
  blocking collectives: 71.9 us -> 0 us
  waiting for transfers between devices: 361 us -> 326 us
  local copies, waits for them, and re-layouts: 45.9 us -> 79.4 us
  starting transfers between devices: 27.5 us -> 56.3 us
  other arithmetic: 56.9 us -> 77.2 us
  Pallas kernels: 143 us -> 123 us
  matrix products: 223 us -> 213 us
    ppermute x0 -> x48, waiting for transfers between devices: none -> 272 us  [swap(): return lax.ppermute(value, 'seq', [(i, i ^ hop) for i in range(seq_count)])]
    all_gather x8 -> x3, waiting for transfers between devices: 279 us -> 22.2 us  [the longest x1 22.2 us: per_device(): up_whole = lax.all_gather(near_up, 'rows', axis=0, tiled=True)]
    all_to_all x6 -> x0, waiting for transfers between devices: 67.7 us -> none  [the longest x2 50 us: per_device(): lax.all_to_all(grad_in, 'seq', split_axis=0, concat_axis=0, tiled=True)]
    ppermute x0 -> x48, starting transfers between devices: none -> 55.8 us  [swap(): return lax.ppermute(value, 'seq', [(i, i ^ hop) for i in range(seq_count)])]
    psum x1 -> x0, blocking collectives: 45.4 us -> none  [per_device(): together = lax.psum(together, ('rows', 'seq'))]
    all_to_all x6 -> x0, starting transfers between devices: 26.8 us -> none  [the longest x2 10.2 us: per_device(): lax.all_to_all(grad_in, 'seq', split_axis=0, concat_axis=0, tiled=True)]
    all_gather x2 -> x0, blocking collectives: 26.5 us -> none  [the longest x1 14.2 us: per_device(): lax.all_gather(heads_share, 'seq', axis=0, tiled=False).astype(f32)]
    reduce_scatter x4 -> x3, waiting for transfers between devices: 10.5 us -> 30.9 us  [the longest x1 30.9 us: per_device(): lax.psum_scatter(together, 'rows', scatter_dimension=0, tiled=True)]
  transfers between devices with their start and end apart: 19 -> 57, of which waited for: 11 -> 18; matrix products, arithmetic and copies ran while one was open for 25% -> 31% of each run, Pallas kernels for 15% -> 14%
where the time goes in v2:
time: 902 us; the launch traced here: 891 us
  waiting for transfers between devices  326 us (36%)
  matrix products  213 us (24%)
  Pallas kernels  123 us (14%)
  local copies, waits for them, and re-layouts  79.4 us (9%)
  other arithmetic  77.2 us (9%)
  starting transfers between devices  56.3 us (6%)
  between operations  16.2 us (2%)
    ppermute x48, waiting for transfers between devices, swap(): return lax.ppermute(value, 'seq', [(i, i ^ hop) for i in range(seq_count)])  272 us
    dot_general x34, matrix products, contract(): lax.dot_general(left, right, (((left_axis,), (right_axis,)), ((), ())), p...  213 us
    pallas_call x2, Pallas kernels, attend_back(): pl.pallas_call(functools.partial(attend_back_kernel, count=count, block=b...  83.8 us
    ppermute x48, starting transfers between devices, swap(): return lax.ppermute(value, 'seq', [(i, i ^ hop) for i in range(seq_count)])  55.8 us
    pallas_call x2, Pallas kernels, attend(): pl.pallas_call(functools.partial(attend_kernel, count=count, block=block,...  39 us
    unnamed x256, local copies, waits for them, and re-layouts  37.5 us
    reduce_scatter x1, waiting for transfers between devices, per_device(): lax.psum_scatter(together, 'rows', scatter_dimension=0, tiled=True)  30.9 us
    all_gather x1, waiting for transfers between devices, per_device(): up_whole = lax.all_gather(near_up, 'rows', axis=0, tiled=True)  22.2 us
  transfers between devices with their start and end apart: 57, of which 18 were waited for; matrix products, arithmetic and copies ran while one was open for 31% of the time, Pallas kernels for 14%

profile of v2, /device:TPU:16, one launch (start us, length us, event | category | flops | bytes accessed | tf_op | source)
XLA Modules:
  0.0 891.0 jit_solution(7068915566963056821)
XLA Ops:
  29.5 23.6 %collective-permute-done = bf16[512,1152]{1,0:T(8,128)(2,1)} collective-permute-done((bf16[512,1152]{1,0:T(8,128)(2,1)}, bf16[512,1152]{1,0:T(8,128)(2,1)}, u32[]{:S(2)}, u32[]{:S(2)}) %collective-permute-start) | collective-permute-done | bytes 1179680 | tf_op jit(solution)/shard_map/ppermute | solution.py:288
  53.1 25.4 %collective-permute-done.1 = bf16[512,1152]{1,0:T(8,128)(2,1)} collective-permute-done((bf16[512,1152]{1,0:T(8,128)(2,1)}, bf16[512,1152]{1,0:T(8,128)(2,1)}, u32[]{:S(2)}, u32[]{:S(2)}) %collective-permute-start.1) | collective-permute-done | bytes 1179680 | tf_op jit(solution)/shard_map/ppermute | solution.py:288
  94.9 5.7 fusion.63
  100.7 5.0 add_convert_fusion.1
  106.3 19.5 %attend.2 = (bf16[4,288,512]{2,1,0:T(8,128)(2,1)S(1)}, f32[8,2048]{1,0:T(8,128)S(1)}) custom-call(s32[8]{0:T(128)S(1)} %get-tuple-element.305.low_ref, s32[8]{0:T(128)S(1)} %get-tuple-element.306.high_ref, s32[1]{0:T(128)} %bitcast.3.place_ref, bf16[3,288,2048]{2,1,0:T(8,128)(2,1)S(1)} %bitcast.178, s32[2048,128]{1,0:T(8,128)S(1)} %broadcast_in_dim.22.kid_ref, ...), custom_call_target="tpu_custom_call" | custom-call | flops 6710886400 | bytes 4718592 | tf_op jit(solution)/shard_map/attend/pallas_call | solution.py:99
  144.5 5.0 add_convert_fusion
  149.9 19.5 %attend.3 = (bf16[4,288,512]{2,1,0:T(8,128)(2,1)S(1)}, f32[8,2048]{1,0:T(8,128)S(1)}) custom-call(s32[8]{0:T(128)S(1)} %get-tuple-element.186.low_ref, s32[8]{0:T(128)S(1)} %get-tuple-element.185.high_ref, s32[1]{0:T(128)} %bitcast.3.place_ref, bf16[3,288,2048]{2,1,0:T(8,128)(2,1)S(1)} %bitcast.176, s32[2048,128]{1,0:T(8,128)S(1)} %broadcast_in_dim.25.kid_ref, ...), custom_call_target="tpu_custom_call" | custom-call | flops 6710886400 | bytes 4718592 | tf_op jit(solution)/shard_map/attend/pallas_call | solution.py:99
  180.4 8.3 collective-permute-done.9
  188.7 5.6 fusion.168
  196.6 22.2 %all-gather.11.cloned.1.call-done = bf16[1152,4608]{1,0:T(8,128)(2,1)} async-done(((bf16[144,4608]{1,0:T(8,128)(2,1)}), bf16[1152,4608]{1,0:T(8,128)(2,1)}) %all-gather.11.cloned.1.call-update) | async-done | bytes 10616848 | tf_op jit(solution)/shard_map/all_gather | solution.py:335
  218.7 29.7 %fusion.6 = (bf16[1024,4608]{1,0:T(8,128)(2,1)}, bf16[1024,4608]{1,0:T(8,128)(2,1)S(1)}) fusion(f32[4608]{0:T(1024)S(1)} %pad_maximum_fusion.22, bf16[1152,4608]{1,0:T(8,128)(2,1)} %all-gather.11.cloned.1.call-done, f32[1024,1152]{1,0:T(8,128)} %copy-done.19, f32[1152]{0:T(1024)S(1)} %get-tuple-element.262, f32[1152]{0:T(1024)S(1)} %get-tuple-element.261, ...), kind=kOutput, calls=%fused_computation.10 | convolution fusion | flops 10976624640 | bytes 34245632 | tf_op jit(solution)/shard_map/dot_general | solution.py:267
  251.9 14.8 %fusion.7 = bf16[1152,4608]{0,1:T(8,128)(2,1)} fusion(bf16[1024,4608]{1,0:T(8,128)(2,1)S(1)} %get-tuple-element.191, bf16[1024,1152]{1,0:T(8,128)(2,1)S(1)} %bitcast.190), kind=kOutput, calls=%fused_computation.13 | convolution fusion | flops 10876944384 | bytes 22413312 | tf_op jit(solution)/shard_map/dot_general | solution.py:267
  266.7 15.3 %copy.105 = bf16[1152,4608]{1,0:T(8,128)(2,1)} copy(bf16[1152,4608]{0,1:T(8,128)(2,1)} %fusion.7) | data formatting | bytes 21233664
  285.6 7.5 fusion.18
  293.1 50.6 %collective-permute-done.14 = bf16[1152,1152]{1,0:T(8,128)(2,1)S(1)} collective-permute-done((bf16[1152,1152]{1,0:T(8,128)(2,1)}, bf16[1152,1152]{1,0:T(8,128)(2,1)S(1)}, u32[]{:S(2)}, u32[]{:S(2)}) %collective-permute-start.14) | collective-permute-done | bytes 2654240 | tf_op jit(solution)/shard_map/ppermute | solution.py:288
  343.7 6.9 fusion.21
  350.7 49.2 %collective-permute-done.13 = bf16[1152,1152]{1,0:T(8,128)(2,1)S(1)} collective-permute-done((bf16[1152,1152]{1,0:T(8,128)(2,1)}, bf16[1152,1152]{1,0:T(8,128)(2,1)S(1)}, u32[]{:S(2)}, u32[]{:S(2)}) %collective-permute-start.13) | collective-permute-done | bytes 2654240 | tf_op jit(solution)/shard_map/ppermute | solution.py:288
  399.9 4.8 fusion.20
  406.2 4.8 fusion.19
  411.0 19.5 %multiply_reduce_fusion = (f32[1152]{0:T(1024)S(1)}, f32[1024]{0:T(1024)S(1)}, f32[1024]{0:T(1024)S(1)}, f32[1152]{0:T(1024)S(1)}, f32[1024,1152]{1,0:T(8,128)}) fusion(f32[1024,1152]{1,0:T(8,128)S(1)} %bitcast.182, f32[1024]{0:T(1024)S(1)} %add_rsqrt_fusion.1, f32[1024]{0:T(1024)S(1)} %broadcast_multiply_fusion.4, f32[1152]{0:T(1024)S(1)} %get-tuple-element.261, ...), kind=kOutput, calls=%fused_computation.41 | convolution fusion | flops 10919997440 | bytes 29521408 | tf_op jit(solution)/shard_map/dot_general | solution.py:267
  430.5 5.9 convert_reduce_fusion.3
  436.4 5.5 convolution_convert_fusion.2
  442.1 6.0 pad_maximum_fusion.4
  448.1 19.0 %convolution_convert_fusion = bf16[1152,4608]{1,0:T(8,128)(2,1)} fusion(f32[1024,1152]{1,0:T(8,128)} %copy-done.19, f32[1152]{0:T(1024)S(1)} %get-tuple-element.262, f32[1152]{0:T(1024)S(1)} %get-tuple-element.261, f32[1024]{0:T(1024)S(1)} %add_rsqrt_fusion.1, f32[1024]{0:T(1024)S(1)} %broadcast_multiply_fusion.4, bf16[1024,1152]{1,0:T(8,128)(2,1)} %fusion.21, ...), kind=kOutput, calls=%fused_computation.2 | convolution fusion | flops 10920591360 | bytes 24790016 | tf_op jit(solution)/shard_map/dot_general | solution.py:267
  487.1 5.9 convert_reduce_fusion
  500.0 5.4 fusion.102
  505.4 5.2 fusion.98
  510.6 5.3 fusion.100
  515.9 10.7 %add_add_fusion = f32[1024,1152]{1,0:T(8,128)} fusion(f32[1024,1152]{1,0:T(8,128)S(1)} %bitcast.184, f32[1024,1152]{1,0:T(8,128)} %fusion.98, f32[1024,1152]{1,0:T(8,128)S(1)} %fusion.102, f32[1024,1152]{1,0:T(8,128)} %fusion.100, bf16[1152,1152]{1,0:T(8,128)(2,1)S(1)} %copy-done.105, bf16[1024,4608]{1,0:T(8,128)(2,1)} %copy-done.112, f32[1152]{0:T(1024)S(1)} %copy-done.84), kind=kOutput, calls=%fused_computation.44 | convolution fusion | flops 2723807232 | bytes 28611072 | tf_op jit(solution)/shard_map/dot_general | solution.py:267
  540.9 42.1 %attend_back.2 = bf16[3,288,2048]{2,1,0:T(8,128)(2,1)} custom-call(s32[8]{0:T(128)} %copy-done.10, s32[8]{0:T(128)} %copy-done.11, s32[1]{0:T(128)} %bitcast.3.place_ref, bf16[3,288,2048]{2,1,0:T(8,128)(2,1)} %bitcast.179, bf16[4,288,512]{2,1,0:T(8,128)(2,1)} %copy-done.3, f32[8,2048]{1,0:T(8,128)} %copy-done.15, s32[2048,128]{1,0:T(8,128)} %copy-done.5, ...), custom_call_target="tpu_custom_call" | custom-call | flops 16777216000 | bytes 9437184 | tf_op jit(solution)/shard_map/attend_back/pallas_call | solution.py:212
  583.1 5.1 fusion.153
  588.3 4.1 fusion.155
  609.3 41.7 %attend_back.3 = bf16[3,288,2048]{2,1,0:T(8,128)(2,1)} custom-call(s32[8]{0:T(128)} %copy-done.9, s32[8]{0:T(128)} %copy-done.8, s32[1]{0:T(128)} %bitcast.3.place_ref, bf16[3,288,2048]{2,1,0:T(8,128)(2,1)} %bitcast.177, bf16[4,288,512]{2,1,0:T(8,128)(2,1)} %copy-done.2, f32[8,2048]{1,0:T(8,128)} %copy-done.14, s32[2048,128]{1,0:T(8,128)} %copy-done.4, ...), custom_call_target="tpu_custom_call" | custom-call | flops 16777216000 | bytes 9437184 | tf_op jit(solution)/shard_map/attend_back/pallas_call | solution.py:212
  653.8 21.5 %collective-permute-done.46 = bf16[144,1152]{1,0:T(8,128)(2,1)S(1)} collective-permute-done((bf16[144,1152]{1,0:T(8,128)(2,1)S(1)}, bf16[144,1152]{1,0:T(8,128)(2,1)S(1)}, u32[]{:S(2)}, u32[]{:S(2)}) %collective-permute-start.46) | collective-permute-done | bytes 331808 | tf_op jit(solution)/shard_map/ppermute | solution.py:288
  677.6 4.4 convert_add_fusion.2
  687.2 4.8 fusion.158
  698.3 4.7 fusion.121
  703.1 6.0 fusion.22
  709.8 10.1 %collective-permute-done.38 = bf16[144,1152]{1,0:T(8,128)(2,1)S(1)} collective-permute-done((bf16[144,1152]{1,0:T(8,128)(2,1)}, bf16[144,1152]{1,0:T(8,128)(2,1)S(1)}, u32[]{:S(2)}, u32[]{:S(2)}) %collective-permute-start.38) | collective-permute-done | bytes 331808 | tf_op jit(solution)/shard_map/ppermute | solution.py:288
  719.9 35.7 %collective-permute-done.37 = bf16[144,1152]{1,0:T(8,128)(2,1)S(1)} collective-permute-done((bf16[144,1152]{1,0:T(8,128)(2,1)}, bf16[144,1152]{1,0:T(8,128)(2,1)S(1)}, u32[]{:S(2)}, u32[]{:S(2)}) %collective-permute-start.37) | collective-permute-done | bytes 331808 | tf_op jit(solution)/shard_map/ppermute | solution.py:288
  764.5 4.5 fusion.157
  770.1 4.5 collective-permute-done.40
  778.2 21.3 %collective-permute-done.24 = bf16[512,1152]{1,0:T(8,128)(2,1)S(1)} collective-permute-done((bf16[512,1152]{1,0:T(8,128)(2,1)S(1)}, bf16[512,1152]{1,0:T(8,128)(2,1)S(1)}, u32[]{:S(2)}, u32[]{:S(2)}) %collective-permute-start.24) | collective-permute-done | bytes 1179680 | tf_op jit(solution)/shard_map/ppermute | solution.py:288
  799.6 4.6 fusion.154
  812.5 6.3 fusion.17
  818.8 30.9 %reduce-scatter.14.cloned.1.call-done = f32[16,128]{1,0:T(8,128)} async-done(((f32[128,128]{1,0:T(8,128)}), f32[16,128]{1,0:T(8,128)}) %reduce-scatter.14.cloned.1.call-update) | async-done | bytes 8208 | tf_op jit(solution)/shard_map/reduce_scatter | solution.py:455
  860.8 8.5 collective-permute-done.32
  869.3 8.1 collective-permute-done.31
  (524 shorter events, 194.1 us)
Async XLA Ops:
  7.2 83.5 %all-gather.5.cloned.1.call-start = ((), (), s32[]{:S(2)}) async-start(), calls=%async_computation.5 | async-start | bytes 2322432 | tf_op jit(solution)/shard_map/all_gather | solution.py:311
  18.2 113.9 %all-gather.7.cloned.1.call-start = ((), (), s32[]{:S(2)}) async-start(), calls=%async_computation.6 | async-start | bytes 2985984 | tf_op jit(solution)/shard_map/all_gather | solution.py:332
  19.1 155.8 %all-gather.9.cloned.1.call-start = ((), (), s32[]{:S(2)}) async-start(), calls=%async_computation.7 | async-start | bytes 2985984 | tf_op jit(solution)/shard_map/all_gather | solution.py:333
  19.8 198.9 %all-gather.11.cloned.1.call-start = ((), (), s32[]{:S(2)}) async-start(), calls=%async_computation.8 | async-start | bytes 11943936 | tf_op jit(solution)/shard_map/all_gather | solution.py:335
  21.4 445.8 %reduce-scatter.16.cloned.1.call-start = ((), (), s32[]{:S(2)}) async-start(), calls=%async_computation.12 | async-start | bytes 11943936
  23.9 29.2 %collective-permute-start = (bf16[512,1152]{1,0:T(8,128)(2,1)}, bf16[512,1152]{1,0:T(8,128)(2,1)}, u32[]{:S(2)}, u32[]{:S(2)}) collective-permute-start(bf16[512,1152]{1,0:T(8,128)(2,1)} %get-tuple-element.215), channel_id=1, source_target_pairs={{0,1},{1,0},{2,3},{3,2},{4,5},{5,4},{6,7},{7,6},{8,9},{9,8},{10,11... | collective-permute-start | bytes 3538952 | tf_op jit(solution)/shard_map/ppermute | solution.py:288
  25.4 53.0 %collective-permute-start.1 = (bf16[512,1152]{1,0:T(8,128)(2,1)}, bf16[512,1152]{1,0:T(8,128)(2,1)}, u32[]{:S(2)}, u32[]{:S(2)}) collective-permute-start(bf16[512,1152]{1,0:T(8,128)(2,1)} %get-tuple-element.215), channel_id=1, source_target_pairs={{0,2},{1,3},{2,0},{3,1},{4,6},{5,7},{6,4},{7,5},{8,10},{9,11},{10,... | collective-permute-start | bytes 3538952 | tf_op jit(solution)/shard_map/ppermute | solution.py:288
  26.9 51.5 %collective-permute-start.2 = (bf16[512,1152]{1,0:T(8,128)(2,1)}, bf16[512,1152]{1,0:T(8,128)(2,1)}, u32[]{:S(2)}, u32[]{:S(2)}) collective-permute-start(bf16[512,1152]{1,0:T(8,128)(2,1)} %get-tuple-element.215), channel_id=1, source_target_pairs={{0,3},{1,2},{2,1},{3,0},{4,7},{5,6},{6,5},{7,4},{8,11},{9,10},{10,... | collective-permute-start | bytes 3538952 | tf_op jit(solution)/shard_map/ppermute | solution.py:288
  78.5 52.9 %collective-permute-start.3 = (bf16[512,1152]{1,0:T(8,128)(2,1)}, bf16[512,1152]{1,0:T(8,128)(2,1)}, u32[]{:S(2)}, u32[]{:S(2)}) collective-permute-start(bf16[512,1152]{1,0:T(8,128)(2,1)} %get-tuple-element.51), channel_id=1, source_target_pairs={{0,1},{1,0},{2,3},{3,2},{4,5},{5,4},{6,7},{7,6},{8,9},{9,8},{10,11... | collective-permute-start | bytes 3538952 | tf_op jit(solution)/shard_map/ppermute | solution.py:288
  79.7 52.5 %collective-permute-start.4 = (bf16[512,1152]{1,0:T(8,128)(2,1)}, bf16[512,1152]{1,0:T(8,128)(2,1)}, u32[]{:S(2)}, u32[]{:S(2)}) collective-permute-start(bf16[512,1152]{1,0:T(8,128)(2,1)} %get-tuple-element.51), channel_id=1, source_target_pairs={{0,2},{1,3},{2,0},{3,1},{4,6},{5,7},{6,4},{7,5},{8,10},{9,11},{10,... | collective-permute-start | bytes 3538952 | tf_op jit(solution)/shard_map/ppermute | solution.py:288
  80.5 51.6 %collective-permute-start.5 = (bf16[512,1152]{1,0:T(8,128)(2,1)}, bf16[512,1152]{1,0:T(8,128)(2,1)}, u32[]{:S(2)}, u32[]{:S(2)}) collective-permute-start(bf16[512,1152]{1,0:T(8,128)(2,1)} %get-tuple-element.51), channel_id=1, source_target_pairs={{0,3},{1,2},{2,1},{3,0},{4,7},{5,6},{6,5},{7,4},{8,11},{9,10},{10,... | collective-permute-start | bytes 3538952 | tf_op jit(solution)/shard_map/ppermute | solution.py:288
  127.9 46.4 %collective-permute-start.10 = (bf16[288,512]{1,0:T(8,128)(2,1)}, bf16[288,512]{1,0:T(8,128)(2,1)}, u32[]{:S(2)}, u32[]{:S(2)}) collective-permute-start(bf16[288,512]{1,0:T(8,128)(2,1)} %get-tuple-element.237), channel_id=1, source_target_pairs={{0,3},{1,2},{2,1},{3,0},{4,7},{5,6},{6,5},{7,4},{8,11},{9,10},{10,... | collective-permute-start | bytes 884744 | tf_op jit(solution)/shard_map/ppermute | solution.py:288
  129.5 47.5 %collective-permute-start.8 = (bf16[288,512]{1,0:T(8,128)(2,1)}, bf16[288,512]{1,0:T(8,128)(2,1)}, u32[]{:S(2)}, u32[]{:S(2)}) collective-permute-start(bf16[288,512]{1,0:T(8,128)(2,1)} %get-tuple-element.238), channel_id=1, source_target_pairs={{0,2},{1,3},{2,0},{3,1},{4,6},{5,7},{6,4},{7,5},{8,10},{9,11},{10,... | collective-permute-start | bytes 884744 | tf_op jit(solution)/shard_map/ppermute | solution.py:288
  131.4 45.6 %collective-permute-start.6 = (bf16[288,512]{1,0:T(8,128)(2,1)}, bf16[288,512]{1,0:T(8,128)(2,1)}, u32[]{:S(2)}, u32[]{:S(2)}) collective-permute-start(bf16[288,512]{1,0:T(8,128)(2,1)} %get-tuple-element.239), channel_id=1, source_target_pairs={{0,1},{1,0},{2,3},{3,2},{4,5},{5,4},{6,7},{7,6},{8,9},{9,8},{10,11... | collective-permute-start | bytes 884744 | tf_op jit(solution)/shard_map/ppermute | solution.py:288
  282.0 395.3 %reduce-scatter.10.cloned.1.call-start = ((), (), s32[]{:S(2)}) async-start(), calls=%async_computation.9 | async-start | bytes 11943936 | tf_op jit(solution)/shard_map/reduce_scatter | solution.py:401
  282.1 61.7 %collective-permute-start.14 = (bf16[1152,1152]{1,0:T(8,128)(2,1)}, bf16[1152,1152]{1,0:T(8,128)(2,1)S(1)}, u32[]{:S(2)}, u32[]{:S(2)}) collective-permute-start(bf16[1152,1152]{1,0:T(8,128)(2,1)} %all-gather.7.cloned.1.call-done), channel_id=1, source_target_pairs={{0,3},{1,2},{2,1},{3,0},{4,7},{5,6},{6,5},{7,4},{8,11},{9,10},{10,... | collective-permute-start | bytes 7962632 | tf_op jit(solution)/shard_map/ppermute | solution.py:288
  284.5 115.3 %collective-permute-start.13 = (bf16[1152,1152]{1,0:T(8,128)(2,1)}, bf16[1152,1152]{1,0:T(8,128)(2,1)S(1)}, u32[]{:S(2)}, u32[]{:S(2)}) collective-permute-start(bf16[1152,1152]{1,0:T(8,128)(2,1)} %all-gather.7.cloned.1.call-done), channel_id=1, source_target_pairs={{0,2},{1,3},{2,0},{3,1},{4,6},{5,7},{6,4},{7,5},{8,10},{9,11},{10,... | collective-permute-start | bytes 7962632 | tf_op jit(solution)/shard_map/ppermute | solution.py:288
  285.1 119.6 %collective-permute-start.12 = (bf16[1152,1152]{1,0:T(8,128)(2,1)}, bf16[1152,1152]{1,0:T(8,128)(2,1)S(1)}, u32[]{:S(2)}, u32[]{:S(2)}) collective-permute-start(bf16[1152,1152]{1,0:T(8,128)(2,1)} %all-gather.7.cloned.1.call-done), channel_id=1, source_target_pairs={{0,1},{1,0},{2,3},{3,2},{4,5},{5,4},{6,7},{7,6},{8,9},{9,8},{10,11... | collective-permute-start | bytes 7962632 | tf_op jit(solution)/shard_map/ppermute | solution.py:288
  471.0 289.3 %reduce-scatter.12.cloned.1.call-start = ((), (), s32[]{:S(2)}) async-start(), calls=%async_computation.10 | async-start | bytes 2985984 | tf_op jit(solution)/shard_map/reduce_scatter | solution.py:416
  475.8 61.6 %collective-permute-start.15 = (bf16[288,512]{1,0:T(8,128)(2,1)}, bf16[288,512]{1,0:T(8,128)(2,1)}, u32[]{:S(2)}, u32[]{:S(2)}) collective-permute-start(bf16[288,512]{1,0:T(8,128)(2,1)} %convolution_convert_fusion.9), channel_id=1, source_target_pairs={{0,1},{1,0},{2,3},{3,2},{4,5},{5,4},{6,7},{7,6},{8,9},{9,8},{10,11... | collective-permute-start | bytes 884744 | tf_op jit(solution)/shard_map/ppermute | solution.py:288
  478.5 60.1 %collective-permute-start.16 = (bf16[288,512]{1,0:T(8,128)(2,1)}, bf16[288,512]{1,0:T(8,128)(2,1)}, u32[]{:S(2)}, u32[]{:S(2)}) collective-permute-start(bf16[288,512]{1,0:T(8,128)(2,1)} %convolution_convert_fusion.8), channel_id=1, source_target_pairs={{0,2},{1,3},{2,0},{3,1},{4,6},{5,7},{6,4},{7,5},{8,10},{9,11},{10,... | collective-permute-start | bytes 884744 | tf_op jit(solution)/shard_map/ppermute | solution.py:288
  480.7 59.4 %collective-permute-start.17 = (bf16[288,512]{1,0:T(8,128)(2,1)}, bf16[288,512]{1,0:T(8,128)(2,1)}, u32[]{:S(2)}, u32[]{:S(2)}) collective-permute-start(bf16[288,512]{1,0:T(8,128)(2,1)} %convolution_convert_fusion.7), channel_id=1, source_target_pairs={{0,3},{1,2},{2,1},{3,0},{4,7},{5,6},{6,5},{7,4},{8,11},{9,10},{10,... | collective-permute-start | bytes 884744 | tf_op jit(solution)/shard_map/ppermute | solution.py:288
  483.2 121.8 %collective-permute-start.21 = (bf16[288,512]{1,0:T(8,128)(2,1)}, bf16[288,512]{1,0:T(8,128)(2,1)}, u32[]{:S(2)}, u32[]{:S(2)}) collective-permute-start(bf16[288,512]{1,0:T(8,128)(2,1)} %convolution_convert_fusion.5), channel_id=1, source_target_pairs={{0,1},{1,0},{2,3},{3,2},{4,5},{5,4},{6,7},{7,6},{8,9},{9,8},{10,11... | collective-permute-start | bytes 884744 | tf_op jit(solution)/shard_map/ppermute | solution.py:288
  485.9 120.6 %collective-permute-start.22 = (bf16[288,512]{1,0:T(8,128)(2,1)}, bf16[288,512]{1,0:T(8,128)(2,1)}, u32[]{:S(2)}, u32[]{:S(2)}) collective-permute-start(bf16[288,512]{1,0:T(8,128)(2,1)} %convolution_convert_fusion.4), channel_id=1, source_target_pairs={{0,2},{1,3},{2,0},{3,1},{4,6},{5,7},{6,4},{7,5},{8,10},{9,11},{10,... | collective-permute-start | bytes 884744 | tf_op jit(solution)/shard_map/ppermute | solution.py:288
  537.4 62.5 %collective-permute-start.44 = (bf16[144,1152]{1,0:T(8,128)(2,1)}, bf16[144,1152]{1,0:T(8,128)(2,1)S(1)}, u32[]{:S(2)}, u32[]{:S(2)}) collective-permute-start(bf16[144,1152]{1,0:T(8,128)(2,1)} %copy.101), channel_id=1, source_target_pairs={{0,3},{1,2},{2,1},{3,0},{4,7},{5,6},{6,5},{7,4},{8,11},{9,10},{10,... | collective-permute-start | bytes 995336 | tf_op jit(solution)/shard_map/ppermute | solution.py:288
  538.6 62.3 %collective-permute-start.43 = (bf16[144,1152]{1,0:T(8,128)(2,1)}, bf16[144,1152]{1,0:T(8,128)(2,1)S(1)}, u32[]{:S(2)}, u32[]{:S(2)}) collective-permute-start(bf16[144,1152]{1,0:T(8,128)(2,1)} %copy.100), channel_id=1, source_target_pairs={{0,2},{1,3},{2,0},{3,1},{4,6},{5,7},{6,4},{7,5},{8,10},{9,11},{10,... | collective-permute-start | bytes 995336 | tf_op jit(solution)/shard_map/ppermute | solution.py:288
  540.1 62.7 %collective-permute-start.42 = (bf16[144,1152]{1,0:T(8,128)(2,1)S(1)}, bf16[144,1152]{1,0:T(8,128)(2,1)S(1)}, u32[]{:S(2)}, u32[]{:S(2)}) collective-permute-start(bf16[144,1152]{1,0:T(8,128)(2,1)S(1)} %copy.99), channel_id=1, source_target_pairs={{0,1},{1,0},{2,3},{3,2},{4,5},{5,4},{6,7},{7,6},{8,9},{9,8},{10,11... | collective-permute-start | bytes 995336 | tf_op jit(solution)/shard_map/ppermute | solution.py:288
  600.9 76.7 %collective-permute-start.20 = (bf16[512,1152]{1,0:T(8,128)(2,1)}, bf16[512,1152]{1,0:T(8,128)(2,1)}, u32[]{:S(2)}, u32[]{:S(2)}) collective-permute-start(bf16[512,1152]{1,0:T(8,128)(2,1)} %get-tuple-element.64), channel_id=1, source_target_pairs={{0,3},{1,2},{2,1},{3,0},{4,7},{5,6},{6,5},{7,4},{8,11},{9,10},{10,... | collective-permute-start | bytes 3538952 | tf_op jit(solution)/shard_map/ppermute | solution.py:288
  602.8 74.8 %collective-permute-start.19 = (bf16[512,1152]{1,0:T(8,128)(2,1)}, bf16[512,1152]{1,0:T(8,128)(2,1)}, u32[]{:S(2)}, u32[]{:S(2)}) collective-permute-start(bf16[512,1152]{1,0:T(8,128)(2,1)} %get-tuple-element.63), channel_id=1, source_target_pairs={{0,2},{1,3},{2,0},{3,1},{4,6},{5,7},{6,4},{7,5},{8,10},{9,11},{10,... | collective-permute-start | bytes 3538952 | tf_op jit(solution)/shard_map/ppermute | solution.py:288
  604.9 48.1 %collective-permute-start.47 = (bf16[144,1152]{1,0:T(8,128)(2,1)S(1)}, bf16[144,1152]{1,0:T(8,128)(2,1)S(1)}, u32[]{:S(2)}, u32[]{:S(2)}) collective-permute-start(bf16[144,1152]{1,0:T(8,128)(2,1)S(1)} %add_convert_fusion.3), channel_id=1, source_target_pairs={{0,3},{1,2},{2,1},{3,0},{4,7},{5,6},{6,5},{7,4},{8,11},{9,10},{10,... | collective-permute-start | bytes 995336 | tf_op jit(solution)/shard_map/ppermute | solution.py:288
  606.5 68.8 %collective-permute-start.46 = (bf16[144,1152]{1,0:T(8,128)(2,1)S(1)}, bf16[144,1152]{1,0:T(8,128)(2,1)S(1)}, u32[]{:S(2)}, u32[]{:S(2)}) collective-permute-start(bf16[144,1152]{1,0:T(8,128)(2,1)S(1)} %add_convert_fusion.3), channel_id=1, source_target_pairs={{0,2},{1,3},{2,0},{3,1},{4,6},{5,7},{6,4},{7,5},{8,10},{9,11},{10,... | collective-permute-start | bytes 995336 | tf_op jit(solution)/shard_map/ppermute | solution.py:288
  608.3 67.0 %collective-permute-start.45 = (bf16[144,1152]{1,0:T(8,128)(2,1)S(1)}, bf16[144,1152]{1,0:T(8,128)(2,1)S(1)}, u32[]{:S(2)}, u32[]{:S(2)}) collective-permute-start(bf16[144,1152]{1,0:T(8,128)(2,1)S(1)} %add_convert_fusion.3), channel_id=1, source_target_pairs={{0,1},{1,0},{2,3},{3,2},{4,5},{5,4},{6,7},{7,6},{8,9},{9,8},{10,11... | collective-permute-start | bytes 995336 | tf_op jit(solution)/shard_map/ppermute | solution.py:288
  653.0 24.6 %collective-permute-start.18 = (bf16[512,1152]{1,0:T(8,128)(2,1)}, bf16[512,1152]{1,0:T(8,128)(2,1)}, u32[]{:S(2)}, u32[]{:S(2)}) collective-permute-start(bf16[512,1152]{1,0:T(8,128)(2,1)} %get-tuple-element.62), channel_id=1, source_target_pairs={{0,1},{1,0},{2,3},{3,2},{4,5},{5,4},{6,7},{7,6},{8,9},{9,8},{10,11... | collective-permute-start | bytes 3538952 | tf_op jit(solution)/shard_map/ppermute | solution.py:288
  677.3 134.0 %reduce-scatter.18.cloned.1.call-start = ((), (), s32[]{:S(2)}) async-start(), calls=%async_computation.13 | async-start | bytes 2322432
  686.2 92.0 %collective-permute-start.26 = (bf16[512,1152]{1,0:T(8,128)(2,1)}, bf16[512,1152]{1,0:T(8,128)(2,1)}, u32[]{:S(2)}, u32[]{:S(2)}) collective-permute-start(bf16[512,1152]{1,0:T(8,128)(2,1)} %get-tuple-element.214), channel_id=1, source_target_pairs={{0,3},{1,2},{2,1},{3,0},{4,7},{5,6},{6,5},{7,4},{8,11},{9,10},{10,... | collective-permute-start | bytes 3538952 | tf_op jit(solution)/shard_map/ppermute | solution.py:288
  692.0 86.2 %collective-permute-start.25 = (bf16[512,1152]{1,0:T(8,128)(2,1)}, bf16[512,1152]{1,0:T(8,128)(2,1)}, u32[]{:S(2)}, u32[]{:S(2)}) collective-permute-start(bf16[512,1152]{1,0:T(8,128)(2,1)} %get-tuple-element.213), channel_id=1, source_target_pairs={{0,2},{1,3},{2,0},{3,1},{4,6},{5,7},{6,4},{7,5},{8,10},{9,11},{10,... | collective-permute-start | bytes 3538952 | tf_op jit(solution)/shard_map/ppermute | solution.py:288
  694.4 25.5 %collective-permute-start.38 = (bf16[144,1152]{1,0:T(8,128)(2,1)}, bf16[144,1152]{1,0:T(8,128)(2,1)S(1)}, u32[]{:S(2)}, u32[]{:S(2)}) collective-permute-start(bf16[144,1152]{1,0:T(8,128)(2,1)} %get-tuple-element.230), channel_id=1, source_target_pairs={{0,3},{1,2},{2,1},{3,0},{4,7},{5,6},{6,5},{7,4},{8,11},{9,10},{10,... | collective-permute-start | bytes 995336 | tf_op jit(solution)/shard_map/ppermute | solution.py:288
  695.8 59.7 %collective-permute-start.37 = (bf16[144,1152]{1,0:T(8,128)(2,1)}, bf16[144,1152]{1,0:T(8,128)(2,1)S(1)}, u32[]{:S(2)}, u32[]{:S(2)}) collective-permute-start(bf16[144,1152]{1,0:T(8,128)(2,1)} %get-tuple-element.231), channel_id=1, source_target_pairs={{0,2},{1,3},{2,0},{3,1},{4,6},{5,7},{6,4},{7,5},{8,10},{9,11},{10,... | collective-permute-start | bytes 995336 | tf_op jit(solution)/shard_map/ppermute | solution.py:288
  696.9 58.6 %collective-permute-start.36 = (bf16[144,1152]{1,0:T(8,128)(2,1)S(1)}, bf16[144,1152]{1,0:T(8,128)(2,1)}, u32[]{:S(2)}, u32[]{:S(2)}) collective-permute-start(bf16[144,1152]{1,0:T(8,128)(2,1)S(1)} %get-tuple-element.229), channel_id=1, source_target_pairs={{0,1},{1,0},{2,3},{3,2},{4,5},{5,4},{6,7},{7,6},{8,9},{9,8},{10,11... | collective-permute-start | bytes 995336 | tf_op jit(solution)/shard_map/ppermute | solution.py:288
  757.9 16.6 %collective-permute-start.40 = (bf16[144,1152]{1,0:T(8,128)(2,1)S(1)}, bf16[144,1152]{1,0:T(8,128)(2,1)S(1)}, u32[]{:S(2)}, u32[]{:S(2)}) collective-permute-start(bf16[144,1152]{1,0:T(8,128)(2,1)S(1)} %add_convert_fusion.4), channel_id=1, source_target_pairs={{0,2},{1,3},{2,0},{3,1},{4,6},{5,7},{6,4},{7,5},{8,10},{9,11},{10,... | collective-permute-start | bytes 995336 | tf_op jit(solution)/shard_map/ppermute | solution.py:288
  759.4 15.8 %collective-permute-start.39 = (bf16[144,1152]{1,0:T(8,128)(2,1)S(1)}, bf16[144,1152]{1,0:T(8,128)(2,1)}, u32[]{:S(2)}, u32[]{:S(2)}) collective-permute-start(bf16[144,1152]{1,0:T(8,128)(2,1)S(1)} %add_convert_fusion.4), channel_id=1, source_target_pairs={{0,1},{1,0},{2,3},{3,2},{4,5},{5,4},{6,7},{7,6},{8,9},{9,8},{10,11... | collective-permute-start | bytes 995336 | tf_op jit(solution)/shard_map/ppermute | solution.py:288
  764.5 85.3 %reduce-scatter.14.cloned.1.call-start = ((), (), s32[]{:S(2)}) async-start(), calls=%async_computation.11 | async-start | bytes 73728 | tf_op jit(solution)/shard_map/reduce_scatter | solution.py:455
  769.1 30.5 %collective-permute-start.24 = (bf16[512,1152]{1,0:T(8,128)(2,1)S(1)}, bf16[512,1152]{1,0:T(8,128)(2,1)S(1)}, u32[]{:S(2)}, u32[]{:S(2)}) collective-permute-start(bf16[512,1152]{1,0:T(8,128)(2,1)S(1)} %get-tuple-element.212), channel_id=1, source_target_pairs={{0,1},{1,0},{2,3},{3,2},{4,5},{5,4},{6,7},{7,6},{8,9},{9,8},{10,11... | collective-permute-start | bytes 3538952 | tf_op jit(solution)/shard_map/ppermute | solution.py:288
  807.9 44.7 %collective-permute-start.35 = (bf16[144,1152]{1,0:T(8,128)(2,1)S(1)}, bf16[144,1152]{1,0:T(8,128)(2,1)S(1)}, u32[]{:S(2)}, u32[]{:S(2)}) collective-permute-start(bf16[144,1152]{1,0:T(8,128)(2,1)S(1)} %copy-done.56), channel_id=1, source_target_pairs={{0,3},{1,2},{2,1},{3,0},{4,7},{5,6},{6,5},{7,4},{8,11},{9,10},{10,... | collective-permute-start | bytes 995336 | tf_op jit(solution)/shard_map/ppermute | solution.py:288
  809.4 43.8 %collective-permute-start.34 = (bf16[144,1152]{1,0:T(8,128)(2,1)S(1)}, bf16[144,1152]{1,0:T(8,128)(2,1)}, u32[]{:S(2)}, u32[]{:S(2)}) collective-permute-start(bf16[144,1152]{1,0:T(8,128)(2,1)S(1)} %copy-done.56), channel_id=1, source_target_pairs={{0,2},{1,3},{2,0},{3,1},{4,6},{5,7},{6,4},{7,5},{8,10},{9,11},{10,... | collective-permute-start | bytes 995336 | tf_op jit(solution)/shard_map/ppermute | solution.py:288
  810.0 43.2 %collective-permute-start.33 = (bf16[144,1152]{1,0:T(8,128)(2,1)S(1)}, bf16[144,1152]{1,0:T(8,128)(2,1)}, u32[]{:S(2)}, u32[]{:S(2)}) collective-permute-start(bf16[144,1152]{1,0:T(8,128)(2,1)S(1)} %copy-done.56), channel_id=1, source_target_pairs={{0,1},{1,0},{2,3},{3,2},{4,5},{5,4},{6,7},{7,6},{8,9},{9,8},{10,11... | collective-permute-start | bytes 995336 | tf_op jit(solution)/shard_map/ppermute | solution.py:288
  857.7 19.7 %collective-permute-start.31 = (bf16[144,864]{0,1:T(8,128)(2,1)S(1)}, bf16[144,864]{0,1:T(8,128)(2,1)S(1)}, u32[]{:S(2)}, u32[]{:S(2)}) collective-permute-start(bf16[144,864]{0,1:T(8,128)(2,1)S(1)} %copy.108), channel_id=1, source_target_pairs={{0,2},{1,3},{2,0},{3,1},{4,6},{5,7},{6,4},{7,5},{8,10},{9,11},{10,... | collective-permute-start | bytes 746504 | tf_op jit(solution)/shard_map/ppermute | solution.py:288
  858.2 19.5 %collective-permute-start.30 = (bf16[144,864]{0,1:T(8,128)(2,1)S(1)}, bf16[144,864]{0,1:T(8,128)(2,1)S(1)}, u32[]{:S(2)}, u32[]{:S(2)}) collective-permute-start(bf16[144,864]{0,1:T(8,128)(2,1)S(1)} %copy.108), channel_id=1, source_target_pairs={{0,1},{1,0},{2,3},{3,2},{4,5},{5,4},{6,7},{7,6},{8,9},{9,8},{10,11... | collective-permute-start | bytes 746504 | tf_op jit(solution)/shard_map/ppermute | solution.py:288
  (133 other events, 2162.4 us)
Sparse Core Ops, SparseCore 0:
  18.3 29.3 all-gather.4
  49.9 33.0 all-gather.6
  84.7 33.0 all-gather.8
  119.9 98.8 all-gather.10
  282.1 108.0 reduce-scatter.15
  471.1 107.4 reduce-scatter.9
  677.4 35.9 reduce-scatter.11
  764.6 41.9 reduce-scatter.17
  812.7 37.0 reduce-scatter.13

commit v3 on v2

--- a/solution.py
+++ b/solution.py
@@ -3,6 +3,7 @@
 import jax.numpy as jnp
 from jax import lax
 from jax.experimental import pallas as pl
+from jax.experimental.layout import Layout, with_layout_constraint
 from jax.experimental.pallas import tpu as pltpu
 from jax.sharding import PartitionSpec as P
 
@@ -301,19 +302,30 @@
             token_rows[row], whole_rows[row - 1][1:] = held[0], list(held[1:])
         whole_rows[row] += [swap(token_rows[row], hop) for hop in rest]
 
-    small = [attn_gain, attn_shift, query_bias, value_bias, output_bias, mlp_gain, mlp_shift, down_bias]
-    wide = -(-up_bias.shape[0] // band_width)
-    up_columns = jnp.pad(up_bias, (0, wide * band_width - up_bias.shape[0])).reshape(wide, band_width).T
-    heads_shard = jnp.concatenate(
-        [own_columns(query_weight), own_columns(key_weight), own_columns(value_weight), jnp.stack(small, axis=1), up_columns],
-        axis=1,
-    )
-    gathered = lax.all_gather(heads_shard, "rows", axis=0, tiled=True)
-    heads_weight = gathered[:, : 3 * part]
-    extra = gathered[:, 3 * part :].astype(f32)
-    gain1, shift1, query_off, value_off, output_off, gain2, shift2, down_off = [extra[:, i] for i in range(8)]
-    up_off = extra[:, 8:].reshape(row_count, band_width, wide).transpose(0, 2, 1).reshape(row_count, wide * band_width)
-    up_off = up_off[:, : up_bias.shape[0]].reshape(hidden_size)
+    small = [attn_gain, attn_shift, query_bias, value_bias, output_bias, mlp_gain, mlp_shift, down_bias, up_bias]
+    sizes = [value.shape[0] for value in small]
+    extra_rows = -(-sum(sizes) // (24 * part)) * 8
+
+    def beside(matrix, vectors):
+        lead = vectors.shape[:-1]
+        vectors = jnp.pad(vectors, [(0, 0)] * len(lead) + [(0, extra_rows * 3 * part - vectors.shape[-1])])
+        return jnp.concatenate([matrix, vectors.reshape(*lead, extra_rows, 3 * part)], axis=-2)
+
+    def split(vectors):
+        pieces, start = [], 0
+        for size in sizes:
+            pieces.append(vectors[..., start : start + size])
+            start += size
+        return pieces
+
+    heads_shard = jnp.concatenate([own_columns(query_weight), own_columns(key_weight), own_columns(value_weight)], axis=1)
+    heads_shard = beside(heads_shard, jnp.concatenate(small))
+    gathered = lax.all_gather(heads_shard, "rows", axis=0, tiled=False)
+    heads_weight = gathered[:, :band_width].reshape(width, 3 * part)
+    extra = gathered[:, band_width:].reshape(row_count, extra_rows * 3 * part).astype(f32)
+    gain1, shift1, query_off, value_off, output_off, gain2, shift2, down_off, up_off = [
+        piece.reshape(-1) for piece in split(extra)
+    ]
     up_off = relative(jnp.pad(up_off, (0, slab * seq_count - hidden_size)).reshape(seq_count, slab))
     heads_off = jnp.concatenate(
         [
@@ -329,13 +341,23 @@
     def own_slab(weight, hop):
         return lax.dynamic_slice_in_dim(weight, (place ^ hop) * slab, slab, axis=1)
 
-    down_own = lax.all_gather(own_slab(in_slabs(down_weight.T), 0), "rows", axis=0, tiled=True)
+    def near_slabs(weight, hops):
+        weight = in_slabs(weight)
+        return lax.all_gather(jnp.concatenate([own_slab(weight, hop) for hop in hops], axis=1), "rows", axis=0, tiled=True)
+
+    direct = list(rest)[:2]
+    down_turned = down_weight.T
+    down_own = near_slabs(down_turned, [0])
     output_whole = lax.all_gather(output_weight, "rows", axis=0, tiled=True)
-    near_up = jnp.concatenate([own_slab(in_slabs(up_weight), hop) for hop in range(seq_count)], axis=1)
-    up_whole = lax.all_gather(near_up, "rows", axis=0, tiled=True)
+    up_whole = near_slabs(up_weight, range(seq_count))
+    late = [hop for hop in rest if hop not in direct]
     held = lax.optimization_barrier((down_own, *whole_rows[-1][1:]))
     down_own, whole_rows[-1][1:] = held[0], list(held[1:])
-    downs = [down_own] + [swap(down_own, hop) for hop in rest]
+    downs = [down_own] + [swap(down_own, hop) for hop in direct]
+    if late:
+        down_turned, up_whole = lax.optimization_barrier((down_turned, up_whole))
+        down_late = near_slabs(down_turned, late)
+        downs += [down_late[:, i * slab : (i + 1) * slab] for i in range(len(late))]
     up_off = jnp.concatenate(up_off)
     outputs = relative(output_whole.reshape(seq_count, part, width))
 
@@ -371,10 +393,9 @@
     def slab_of(value, hop):
         return value[:, hop * slab : (hop + 1) * slab]
 
-    for hop in range(seq_count):
-        term = contract(slab_of(gelu_out, hop), downs[hop], 1, 1)
-        total = term if total is None else total + term
-    activations = resid + total + down_off
+    def all_pieces(share):
+        stacked = jnp.stack([share] + [swap(share, hop) for hop in rest])
+        return relative(stacked)
 
     def exchange_sum(pieces):
         total = pieces[0].astype(f32)
@@ -383,7 +404,7 @@
         return total
 
     cot = cotangent.reshape(count * chunk, width)
-    grad_down = contract(cot, gelu_out, 0, 0).astype(bf16)
+    grad_down = with_layout_constraint(contract(cot, gelu_out, 0, 0).astype(bf16), Layout(major_to_minor=(0, 1)))
     cot, grad_down = lax.optimization_barrier((cot, grad_down))
     down_raw = lax.psum_scatter(grad_down, "rows", scatter_dimension=0, tiled=True)
     grad_hidden = jnp.concatenate(
@@ -397,9 +418,10 @@
     grad_output = contract(mixed_all, grad_attn, 1, 0)
     grad_output = relative(grad_output.astype(bf16).reshape(seq_count, part, width))
     grad_output = jnp.concatenate(grad_output, axis=0)
-    packs[0], down_raw, grad_up, grad_output = lax.optimization_barrier((packs[0], down_raw, grad_up, grad_output))
-    up_raw = lax.psum_scatter(grad_up, "rows", scatter_dimension=0, tiled=True)
+    packs[0], down_raw, grad_output = lax.optimization_barrier((packs[0], down_raw, grad_output))
+    output_share = lax.psum_scatter(grad_output, "rows", scatter_dimension=0, tiled=True)
     down_share = exchange_sum([slab_of(down_raw, hop) for hop in range(seq_count)]).astype(bf16)
+    down_pieces = all_pieces(down_share)
     heads_grad, query_grad, value_grad, gain_grad, shift_grad, grad_in = None, 0.0, 0.0, 0.0, 0.0, []
     after = None
     for row in range(count):
@@ -411,10 +433,9 @@
         if after is not None:
             pack, grad_in[-1] = lax.optimization_barrier((pack, grad_in[-1]))
         grad_pack = attend_back(pack, grad_mixed, mixes[row], logs[row], *tables[row], place_array)
-        if row == count - 1:
-            grad_pack, up_raw, grad_output = lax.optimization_barrier((grad_pack, up_raw, grad_output))
-            output_share = lax.psum_scatter(grad_output, "rows", scatter_dimension=0, tiled=True)
-            up_share = exchange_sum([slab_of(up_raw, hop) for hop in range(seq_count)]).astype(bf16)
+        if row == 0:
+            grad_pack, output_share, grad_up = lax.optimization_barrier((grad_pack, output_share, grad_up))
+            up_raw = lax.psum_scatter(grad_up, "rows", scatter_dimension=0, tiled=True)
         query_grad = query_grad + jnp.sum(grad_pack[0].astype(f32), axis=1)
         value_grad = value_grad + jnp.sum(grad_pack[2].astype(f32), axis=1)
         grad_pack = grad_pack.reshape(3 * part, length)
@@ -444,16 +465,17 @@
         jnp.sum(cot.astype(f32), axis=0),
         up_grads.reshape(slab * seq_count)[:hidden_size],
     ]
-    together = jnp.concatenate([value.reshape(row_count, -1) for value in small_grads], axis=1)
-    sizes = [value.shape[0] // row_count for value in small_grads]
-    filled = -(-together.shape[1] // 2048) * 2048
-    together = jnp.pad(together, ((0, 0), (0, filled - together.shape[1]))).reshape(row_count * filled // 128, 128)
-    heads_grad = heads_grad.astype(bf16)
-    heads_grad, output_share = lax.optimization_barrier((heads_grad, output_share))
-    heads_share = lax.psum_scatter(heads_grad, "rows", scatter_dimension=0, tiled=True)
-    together, heads_share = lax.optimization_barrier((together, heads_share))
-    small_share = lax.psum_scatter(together, "rows", scatter_dimension=0, tiled=True)
-
+    together = jnp.concatenate([value.reshape(row_count, -1) for value in small_grads], axis=1).astype(bf16)
+    heads_grad = beside(heads_grad.astype(bf16).reshape(row_count, band_width, 3 * part), together)
+    heads_grad, up_raw = lax.optimization_barrier((heads_grad, up_raw))
+    gelu_late, output_share, up_raw, heads_grad = lax.optimization_barrier((gelu_out, output_share, up_raw, heads_grad))
+    total = resid
+    for hop in range(seq_count):
+        total = total + contract(slab_of(gelu_late, hop), downs[hop], 1, 1)
+    activations = total + down_off
+    up_share = exchange_sum([slab_of(up_raw, hop) for hop in range(seq_count)]).astype(bf16)
+
+    heads_share = lax.psum_scatter(heads_grad, "rows", scatter_dimension=0, tiled=False)
     normed1, inverse1 = norm_parts(tokens_own)
     sums = []
     for row in range(count):
@@ -461,10 +483,6 @@
     grad_attn_input = jnp.concatenate(sums, axis=0)
     token_grad = grad_resid + norm_back(grad_attn_input, normed1, inverse1, gain1)
 
-    def all_pieces(share):
-        stacked = jnp.stack([share] + [swap(share, hop) for hop in rest])
-        return relative(stacked)
-
     def seq_sum(share):
         total = share.astype(f32)
         for hop in rest:
@@ -472,17 +490,14 @@
         return total
 
     heads_all = [piece.astype(f32) for piece in all_pieces(heads_share)]
-    small_sum = seq_sum(small_share).reshape(-1)
-    vectors, start = [], 0
-    for size in sizes:
-        vectors.append(small_sum[start : start + size])
-        start += size
+    small_sum = sum(piece[band_width:] for piece in heads_all).reshape(extra_rows * 3 * part)
+    vectors = split(small_sum)
 
     def take(which):
-        return jnp.concatenate([piece[:, which * part : (which + 1) * part] for piece in heads_all], axis=1)
-
-    def slabs(share):
-        return jnp.concatenate([piece.astype(f32) for piece in all_pieces(share)], axis=1)[:, :hidden_size]
+        return jnp.concatenate([piece[:band_width, which * part : (which + 1) * part] for piece in heads_all], axis=1)
+
+    def slabs(pieces):
+        return jnp.concatenate([piece.astype(f32) for piece in pieces], axis=1)[:, :hidden_size]
 
     return (
         activations.reshape(count, chunk, width),
@@ -498,9 +513,9 @@
         vectors[4],
         vectors[5],
         vectors[6],
-        slabs(up_share),
+        slabs(all_pieces(up_share)),
         vectors[8],
-        slabs(down_share).T,
+        slabs(down_pieces).T,
         vectors[7],
     )
 

time: 902 us -> 827 us (0.917)
  the two profiles are of different devices: /device:TPU:16 before, /device:TPU:9 now
where the time goes in v3:
time: 827 us; the launch traced here: 820 us
  matrix products  248 us (30%)
  waiting for transfers between devices  194 us (23%)
  Pallas kernels  147 us (18%)
  local copies, waits for them, and re-layouts  91.7 us (11%)
  other arithmetic  83.6 us (10%)
  starting transfers between devices  39.5 us (5%)
  between operations  15.9 us (2%)
    dot_general x34, matrix products, contract(): lax.dot_general(left, right, (((left_axis,), (right_axis,)), ((), ())), p...  248 us
    ppermute x44, waiting for transfers between devices, swap(): return lax.ppermute(value, 'seq', [(i, i ^ hop) for i in range(seq_count)])  193 us
    pallas_call x2, Pallas kernels, attend_back(): pl.pallas_call(functools.partial(attend_back_kernel, count=count, block=b...  99.7 us
    pallas_call x2, Pallas kernels, attend(): pl.pallas_call(functools.partial(attend_kernel, count=count, block=block,...  47.7 us
    ppermute x44, starting transfers between devices, swap(): return lax.ppermute(value, 'seq', [(i, i ^ hop) for i in range(seq_count)])  39.1 us
    unnamed x265, local copies, waits for them, and re-layouts  22 us
  transfers between devices with their start and end apart: 53, of which 18 were waited for; matrix products, arithmetic and copies ran while one was open for 47% of the time, Pallas kernels for 18%

profile of v3, /device:TPU:9, one launch (start us, length us, event | category | flops | bytes accessed | tf_op | source)
XLA Modules:
  0.0 819.8 jit_solution(2652747404931645334)
XLA Ops:
  7.3 6.3 concatenate.78
  33.6 15.1 %collective-permute-done = bf16[512,1152]{1,0:T(8,128)(2,1)} collective-permute-done((bf16[512,1152]{1,0:T(8,128)(2,1)}, bf16[512,1152]{1,0:T(8,128)(2,1)}, u32[]{:S(2)}, u32[]{:S(2)}) %collective-permute-start) | collective-permute-done | bytes 1179680 | tf_op jit(solution)/shard_map/ppermute | solution.py:289
  49.6 25.3 %collective-permute-done.2 = bf16[512,1152]{1,0:T(8,128)(2,1)S(1)} collective-permute-done((bf16[512,1152]{1,0:T(8,128)(2,1)}, bf16[512,1152]{1,0:T(8,128)(2,1)S(1)}, u32[]{:S(2)}, u32[]{:S(2)}) %collective-permute-start.2) | collective-permute-done | bytes 1179680 | tf_op jit(solution)/shard_map/ppermute | solution.py:289
  104.6 5.2 fusion.63
  109.9 8.2 %add_convert_fusion.1 = bf16[864,2048]{1,0:T(8,128)(2,1)S(1)} fusion(bf16[1152,864]{1,0:T(8,128)(2,1)S(1)} %bitcast.203, f32[864]{0:T(1024)S(1)} %pad_maximum_fusion.23, bf16[512,1152]{1,0:T(8,128)(2,1)S(1)} %get-tuple-element.215, bf16[512,1152]{1,0:T(8,128)(2,1)S(1)} %get-tuple-element.214, bf16[512,1152]{1,0:T(8,128)(2,1)S(1)} %get-tuple-element.213, ...), kind=kOutput, calls=%fused_computation.17 | convolution fusion | flops 4099276800 | bytes 10251648 | tf_op jit(solution)/shard_map/dot_general | solution.py:268
  127.2 24.6 %attend.2 = (bf16[4,288,512]{2,1,0:T(8,128)(2,1)S(1)}, f32[8,2048]{1,0:T(8,128)S(1)}) custom-call(s32[8]{0:T(128)S(1)} %get-tuple-element.239.low_ref, s32[8]{0:T(128)S(1)} %get-tuple-element.240.high_ref, s32[1]{0:T(128)} %bitcast.3.place_ref, bf16[3,288,2048]{2,1,0:T(8,128)(2,1)S(1)} %bitcast.180, s32[2048,128]{1,0:T(8,128)S(1)} %broadcast_in_dim.22.kid_ref, ...), custom_call_target="tpu_custom_call" | custom-call | flops 6710886400 | bytes 4718592 | tf_op jit(solution)/shard_map/attend/pallas_call | solution.py:100
  168.4 8.4 %add_convert_fusion = bf16[864,2048]{1,0:T(8,128)(2,1)S(1)} fusion(bf16[1152,864]{1,0:T(8,128)(2,1)S(1)} %bitcast.204, f32[864]{0:T(1024)S(1)} %copy-done.109, bf16[512,1152]{1,0:T(8,128)(2,1)S(1)} %get-tuple-element.219, bf16[512,1152]{1,0:T(8,128)(2,1)S(1)} %get-tuple-element.218, bf16[512,1152]{1,0:T(8,128)(2,1)S(1)} %get-tuple-element.217, ...), kind=kOutput, calls=%fused_computation.16 | convolution fusion | flops 4099276800 | bytes 10251648 | tf_op jit(solution)/shard_map/dot_general | solution.py:268
  177.3 23.1 %attend.3 = (bf16[4,288,512]{2,1,0:T(8,128)(2,1)S(1)}, f32[8,2048]{1,0:T(8,128)S(1)}) custom-call(s32[8]{0:T(128)S(1)} %get-tuple-element.118.low_ref, s32[8]{0:T(128)S(1)} %get-tuple-element.117.high_ref, s32[1]{0:T(128)} %bitcast.3.place_ref, bf16[3,288,2048]{2,1,0:T(8,128)(2,1)S(1)} %bitcast.178, s32[2048,128]{1,0:T(8,128)S(1)} %broadcast_in_dim.25.kid_ref, ...), custom_call_target="tpu_custom_call" | custom-call | flops 6710886400 | bytes 4718592 | tf_op jit(solution)/shard_map/attend/pallas_call | solution.py:100
  206.4 4.9 collective-permute-done.11
  211.3 6.1 collective-permute-done.9
  217.5 5.2 fusion.167
  227.2 29.9 %fusion.6 = (bf16[1024,4608]{1,0:T(8,128)(2,1)}, bf16[1024,4608]{1,0:T(8,128)(2,1)S(1)}) fusion(f32[4608]{0:T(1024)S(1)} %pad_maximum_fusion.21, bf16[1152,4608]{1,0:T(8,128)(2,1)} %all-gather.11.cloned.1.call-done, f32[1024,1152]{1,0:T(8,128)} %copy-done.20, f32[1152]{0:T(1024)S(1)} %add.471, f32[1152]{0:T(1024)S(1)} %mul.411, ...), kind=kOutput, calls=%fused_computation.10 | convolution fusion | flops 10976624640 | bytes 34245632 | tf_op jit(solution)/shard_map/dot_general | solution.py:268
  260.8 14.3 %fusion.7 = bf16[1152,4608]{1,0:T(8,128)(2,1)} fusion(bf16[1024,4608]{1,0:T(8,128)(2,1)S(1)} %get-tuple-element.74, bf16[1024,1152]{1,0:T(8,128)(2,1)S(1)} %bitcast.195), kind=kOutput, calls=%fused_computation.13 | convolution fusion | flops 10876944384 | bytes 22413312 | tf_op jit(solution)/shard_map/dot_general | solution.py:268
  276.6 7.0 fusion.18
  283.7 50.2 %collective-permute-done.13 = bf16[1152,1152]{1,0:T(8,128)(2,1)S(1)} collective-permute-done((bf16[1152,1152]{1,0:T(8,128)(2,1)}, bf16[1152,1152]{1,0:T(8,128)(2,1)S(1)}, u32[]{:S(2)}, u32[]{:S(2)}) %collective-permute-start.13) | collective-permute-done | bytes 2654240 | tf_op jit(solution)/shard_map/ppermute | solution.py:289
  333.9 6.9 fusion.20
  342.3 6.1 fusion.19
  348.3 8.3 %fusion.21 = bf16[1024,1152]{1,0:T(8,128)(2,1)} fusion(bf16[1024,1152]{1,0:T(8,128)(2,1)} %bitcast.193, bf16[1152,1152]{1,0:T(8,128)(2,1)} %all-gather.13.cloned.1.call-done, bf16[1024,4608]{1,0:T(8,128)(2,1)} %get-tuple-element.122), kind=kOutput, calls=%fused_computation.52 | convolution fusion | flops 2721447936 | bytes 9732096 | tf_op jit(solution)/shard_map/dot_general | solution.py:268
  356.6 19.9 %multiply_reduce_fusion = (bf16[1152]{0:T(1024)(128)(2,1)S(1)}, f32[1024]{0:T(1024)S(1)}, f32[1024]{0:T(1024)S(1)}, bf16[1152]{0:T(1024)(128)(2,1)S(1)}, f32[1024,1152]{1,0:T(8,128)}) fusion(f32[1024,1152]{1,0:T(8,128)} %copy-done.20, f32[1024]{0:T(1024)S(1)} %add_rsqrt_fusion.1, f32[1024]{0:T(1024)S(1)} %broadcast_multiply_fusion.4, f32[1152]{0:T(1024)S(1)} %mul.411, ...), kind=kOutput, calls=%fused_computation.40 | convolution fusion | flops 10919997440 | bytes 29516800 | tf_op jit(solution)/shard_map/dot_general | solution.py:268
  376.6 7.3 fusion.158
  384.0 4.7 convolution_convert_fusion.2
  388.9 6.0 pad_maximum_fusion.4
  404.3 19.9 %convolution_convert_fusion = bf16[1152,4608]{1,0:T(8,128)(2,1)} fusion(f32[1024,1152]{1,0:T(8,128)} %copy-done.20, f32[1152]{0:T(1024)S(1)} %add.471, f32[1152]{0:T(1024)S(1)} %mul.411, f32[1024]{0:T(1024)S(1)} %add_rsqrt_fusion.1, f32[1024]{0:T(1024)S(1)} %broadcast_multiply_fusion.4, bf16[1024,1152]{1,0:T(8,128)(2,1)} %fusion.21, ...), kind=kOutput, calls=%fused_computation.2 | convolution fusion | flops 10920591360 | bytes 24790016 | tf_op jit(solution)/shard_map/dot_general | solution.py:268
  427.4 50.8 %attend_back.2 = bf16[3,288,2048]{2,1,0:T(8,128)(2,1)} custom-call(s32[8]{0:T(128)} %copy-done.10, s32[8]{0:T(128)} %copy-done.11, s32[1]{0:T(128)} %bitcast.3.place_ref, bf16[3,288,2048]{2,1,0:T(8,128)(2,1)} %bitcast.181, bf16[4,288,512]{2,1,0:T(8,128)(2,1)} %copy-done.3, f32[8,2048]{1,0:T(8,128)} %copy-done.15, s32[2048,128]{1,0:T(8,128)} %copy-done.5, ...), custom_call_target="tpu_custom_call" | custom-call | flops 16777216000 | bytes 9437184 | tf_op jit(solution)/shard_map/attend_back/pallas_call | solution.py:213
  490.5 5.4 convert_reduce_fusion
  507.0 8.0 collective-permute-done.39
  527.2 7.6 collective-permute-done.42
  539.9 4.8 fusion.151
  544.7 4.8 fusion.153
  556.6 48.9 %attend_back.3 = bf16[3,288,2048]{2,1,0:T(8,128)(2,1)} custom-call(s32[8]{0:T(128)} %copy-done.9, s32[8]{0:T(128)} %copy-done.8, s32[1]{0:T(128)} %bitcast.3.place_ref, bf16[3,288,2048]{2,1,0:T(8,128)(2,1)} %bitcast.179, bf16[4,288,512]{2,1,0:T(8,128)(2,1)} %copy-done.2, f32[8,2048]{1,0:T(8,128)} %copy-done.14, s32[2048,128]{1,0:T(8,128)} %copy-done.4, ...), custom_call_target="tpu_custom_call" | custom-call | flops 16777216000 | bytes 9437184 | tf_op jit(solution)/shard_map/attend_back/pallas_call | solution.py:213
  605.6 5.7 fusion.157
  612.0 4.7 fusion.156
  617.0 4.8 fusion.155
  624.5 6.7 fusion.121
  637.8 10.6 %fusion.22 = bf16[1152,864]{0,1:T(8,128)(2,1)} fusion(f32[1152,864]{0,1:T(8,128)} %fusion.121, bf16[864,2048]{1,0:T(8,128)(2,1)} %bitcast.217, bf16[512,1152]{1,0:T(8,128)(2,1)} %copy-done.52, bf16[512,1152]{1,0:T(8,128)(2,1)} %copy-done.51, bf16[512,1152]{1,0:T(8,128)(2,1)} %copy-done.50, bf16[512,1152]{1,0:T(8,128)(2,1)} %get-tuple-element.135), kind=kOutput, calls=%fused_computation.53 | convolution fusion | flops 4097728512 | bytes 14229504 | tf_op jit(solution)/shard_map/dot_general | solution.py:268
  648.4 4.6 copy.54
  655.6 10.3 %collective-permute-done.24 = bf16[512,1152]{1,0:T(8,128)(2,1)} collective-permute-done((bf16[512,1152]{1,0:T(8,128)(2,1)}, bf16[512,1152]{1,0:T(8,128)(2,1)}, u32[]{:S(2)}, u32[]{:S(2)}) %collective-permute-start.24) | collective-permute-done | bytes 1179680 | tf_op jit(solution)/shard_map/ppermute | solution.py:289
  665.9 7.9 fusion.152
  683.2 7.6 collective-permute-done.22
  690.8 21.8 %collective-permute-done.21 = bf16[512,1152]{1,0:T(8,128)(2,1)} collective-permute-done((bf16[512,1152]{1,0:T(8,128)(2,1)}, bf16[512,1152]{1,0:T(8,128)(2,1)}, u32[]{:S(2)}, u32[]{:S(2)}) %collective-permute-start.21) | collective-permute-done | bytes 1179680 | tf_op jit(solution)/shard_map/ppermute | solution.py:289
  719.1 6.4 fusion.17
  726.7 8.2 fusion.102
  739.1 8.5 %fusion.94 = f32[1024,1152]{1,0:T(8,128)} fusion(bf16[1152,1152]{1,0:T(8,128)(2,1)} %all-gather.13.cloned.1.call-done, bf16[1024,4608]{1,0:T(8,128)(2,1)} %copy-done.124), kind=kOutput, calls=%fused_computation.146 | convolution fusion | flops 2717908992 | bytes 9732096 | tf_op jit(solution)/shard_map/dot_general | solution.py:268
  747.7 7.6 fusion.100
  755.4 10.9 %add_add_fusion = f32[1024,1152]{1,0:T(8,128)} fusion(f32[1024,1152]{1,0:T(8,128)} %fusion.94, f32[1024,1152]{1,0:T(8,128)} %fusion.100, f32[1024,1152]{1,0:T(8,128)S(1)} %bitcast.186, f32[1024,1152]{1,0:T(8,128)S(1)} %bitcast.242, f32[1152]{0:T(1024)S(1)} %copy-done.97, bf16[1152,1152]{1,0:T(8,128)(2,1)S(1)} %copy-done.111, bf16[1024,4608]{1,0:T(8,128)(2,1)} %copy-done.124), kind=kOutput, calls=%fused_computation.39 | convolution fusion | flops 2723807232 | bytes 28611072 | tf_op jit(solution)/shard_map/dot_general | solution.py:268
  775.3 6.6 collective-permute-done.37
  781.8 6.7 collective-permute-done.35
  796.0 8.3 %collective-permute-done.27 = bf16[152,864]{1,0:T(8,128)(2,1)S(1)} collective-permute-done((bf16[152,864]{1,0:T(8,128)(2,1)}, bf16[152,864]{1,0:T(8,128)(2,1)S(1)}, u32[]{:S(2)}, u32[]{:S(2)}) %collective-permute-start.27) | collective-permute-done | bytes 262688 | tf_op jit(solution)/shard_map/ppermute | solution.py:289
  (524 shorter events, 212.7 us)
Async XLA Ops:
  7.2 80.4 %all-gather.15.cloned.1.call-start = ((), (), s32[]{:S(2)}) async-start(), calls=%async_computation.11 | async-start | bytes 2451456 | tf_op jit(solution)/shard_map/all_gather | solution.py:323
  15.8 140.3 %all-gather.7.cloned.1.call-start = ((), (), s32[]{:S(2)}) async-start(), calls=%async_computation.4 | async-start | bytes 2985984 | tf_op jit(solution)/shard_map/all_gather | solution.py:346
  16.7 187.6 %all-gather.9.cloned.1.call-start = ((), (), s32[]{:S(2)}) async-start(), calls=%async_computation.5 | async-start | bytes 2985984 | tf_op jit(solution)/shard_map/all_gather | solution.py:351
  17.4 208.3 %all-gather.11.cloned.1.call-start = ((), (), s32[]{:S(2)}) async-start(), calls=%async_computation.6 | async-start | bytes 11943936 | tf_op jit(solution)/shard_map/all_gather | solution.py:346
  19.0 329.4 %all-gather.13.cloned.1.call-start = ((), (), s32[]{:S(2)}) async-start(), calls=%async_computation.8 | async-start | bytes 2985984 | tf_op jit(solution)/shard_map/all_gather | solution.py:346
  21.5 27.2 %collective-permute-start = (bf16[512,1152]{1,0:T(8,128)(2,1)}, bf16[512,1152]{1,0:T(8,128)(2,1)}, u32[]{:S(2)}, u32[]{:S(2)}) collective-permute-start(bf16[512,1152]{1,0:T(8,128)(2,1)} %get-tuple-element.144), channel_id=1, source_target_pairs={{0,1},{1,0},{2,3},{3,2},{4,5},{5,4},{6,7},{7,6},{8,9},{9,8},{10,11... | collective-permute-start | bytes 3538952 | tf_op jit(solution)/shard_map/ppermute | solution.py:289
  22.7 26.9 %collective-permute-start.1 = (bf16[512,1152]{1,0:T(8,128)(2,1)}, bf16[512,1152]{1,0:T(8,128)(2,1)}, u32[]{:S(2)}, u32[]{:S(2)}) collective-permute-start(bf16[512,1152]{1,0:T(8,128)(2,1)} %get-tuple-element.144), channel_id=1, source_target_pairs={{0,2},{1,3},{2,0},{3,1},{4,6},{5,7},{6,4},{7,5},{8,10},{9,11},{10,... | collective-permute-start | bytes 3538952 | tf_op jit(solution)/shard_map/ppermute | solution.py:289
  23.9 51.0 %collective-permute-start.2 = (bf16[512,1152]{1,0:T(8,128)(2,1)}, bf16[512,1152]{1,0:T(8,128)(2,1)S(1)}, u32[]{:S(2)}, u32[]{:S(2)}) collective-permute-start(bf16[512,1152]{1,0:T(8,128)(2,1)} %get-tuple-element.144), channel_id=1, source_target_pairs={{0,3},{1,2},{2,1},{3,0},{4,7},{5,6},{6,5},{7,4},{8,11},{9,10},{10,... | collective-permute-start | bytes 3538952 | tf_op jit(solution)/shard_map/ppermute | solution.py:289
  75.0 80.4 %collective-permute-start.3 = (bf16[512,1152]{1,0:T(8,128)(2,1)}, bf16[512,1152]{1,0:T(8,128)(2,1)}, u32[]{:S(2)}, u32[]{:S(2)}) collective-permute-start(bf16[512,1152]{1,0:T(8,128)(2,1)} %get-tuple-element.54), channel_id=1, source_target_pairs={{0,1},{1,0},{2,3},{3,2},{4,5},{5,4},{6,7},{7,6},{8,9},{9,8},{10,11... | collective-permute-start | bytes 3538952 | tf_op jit(solution)/shard_map/ppermute | solution.py:289
  76.1 80.0 %collective-permute-start.4 = (bf16[512,1152]{1,0:T(8,128)(2,1)}, bf16[512,1152]{1,0:T(8,128)(2,1)}, u32[]{:S(2)}, u32[]{:S(2)}) collective-permute-start(bf16[512,1152]{1,0:T(8,128)(2,1)} %get-tuple-element.54), channel_id=1, source_target_pairs={{0,2},{1,3},{2,0},{3,1},{4,6},{5,7},{6,4},{7,5},{8,10},{9,11},{10,... | collective-permute-start | bytes 3538952 | tf_op jit(solution)/shard_map/ppermute | solution.py:289
  76.3 79.8 %collective-permute-start.5 = (bf16[512,1152]{1,0:T(8,128)(2,1)}, bf16[512,1152]{1,0:T(8,128)(2,1)}, u32[]{:S(2)}, u32[]{:S(2)}) collective-permute-start(bf16[512,1152]{1,0:T(8,128)(2,1)} %get-tuple-element.54), channel_id=1, source_target_pairs={{0,3},{1,2},{2,1},{3,0},{4,7},{5,6},{6,5},{7,4},{8,11},{9,10},{10,... | collective-permute-start | bytes 3538952 | tf_op jit(solution)/shard_map/ppermute | solution.py:289
  153.0 50.6 %collective-permute-start.10 = (bf16[288,512]{1,0:T(8,128)(2,1)S(1)}, bf16[288,512]{1,0:T(8,128)(2,1)S(1)}, u32[]{:S(2)}, u32[]{:S(2)}) collective-permute-start(bf16[288,512]{1,0:T(8,128)(2,1)S(1)} %get-tuple-element.165), channel_id=1, source_target_pairs={{0,3},{1,2},{2,1},{3,0},{4,7},{5,6},{6,5},{7,4},{8,11},{9,10},{10,... | collective-permute-start | bytes 884744 | tf_op jit(solution)/shard_map/ppermute | solution.py:289
  153.9 52.5 %collective-permute-start.8 = (bf16[288,512]{1,0:T(8,128)(2,1)S(1)}, bf16[288,512]{1,0:T(8,128)(2,1)S(1)}, u32[]{:S(2)}, u32[]{:S(2)}) collective-permute-start(bf16[288,512]{1,0:T(8,128)(2,1)S(1)} %get-tuple-element.166), channel_id=1, source_target_pairs={{0,2},{1,3},{2,0},{3,1},{4,6},{5,7},{6,4},{7,5},{8,10},{9,11},{10,... | collective-permute-start | bytes 884744 | tf_op jit(solution)/shard_map/ppermute | solution.py:289
  155.4 51.0 %collective-permute-start.6 = (bf16[288,512]{1,0:T(8,128)(2,1)S(1)}, bf16[288,512]{1,0:T(8,128)(2,1)S(1)}, u32[]{:S(2)}, u32[]{:S(2)}) collective-permute-start(bf16[288,512]{1,0:T(8,128)(2,1)S(1)} %get-tuple-element.167), channel_id=1, source_target_pairs={{0,1},{1,0},{2,3},{3,2},{4,5},{5,4},{6,7},{7,6},{8,9},{9,8},{10,11... | collective-permute-start | bytes 884744 | tf_op jit(solution)/shard_map/ppermute | solution.py:289
  202.3 15.2 %collective-permute-start.9 = (bf16[288,512]{1,0:T(8,128)(2,1)S(1)}, bf16[288,512]{1,0:T(8,128)(2,1)}, u32[]{:S(2)}, u32[]{:S(2)}) collective-permute-start(bf16[288,512]{1,0:T(8,128)(2,1)S(1)} %get-tuple-element.170), channel_id=1, source_target_pairs={{0,2},{1,3},{2,0},{3,1},{4,6},{5,7},{6,4},{7,5},{8,10},{9,11},{10,... | collective-permute-start | bytes 884744 | tf_op jit(solution)/shard_map/ppermute | solution.py:289
  203.6 13.9 %collective-permute-start.7 = (bf16[288,512]{1,0:T(8,128)(2,1)S(1)}, bf16[288,512]{1,0:T(8,128)(2,1)S(1)}, u32[]{:S(2)}, u32[]{:S(2)}) collective-permute-start(bf16[288,512]{1,0:T(8,128)(2,1)S(1)} %get-tuple-element.171), channel_id=1, source_target_pairs={{0,1},{1,0},{2,3},{3,2},{4,5},{5,4},{6,7},{7,6},{8,9},{9,8},{10,11... | collective-permute-start | bytes 884744 | tf_op jit(solution)/shard_map/ppermute | solution.py:289
  227.1 167.8 %reduce-scatter.7.cloned.1.call-start = ((), (), s32[]{:S(2)}) async-start(), calls=%async_computation.7 | async-start | bytes 11943936 | tf_op jit(solution)/shard_map/reduce_scatter | solution.py:409
  275.0 203.2 %reduce-scatter.9.cloned.1.call-start = ((), (), s32[]{:S(2)}) async-start(), calls=%async_computation.9 | async-start | bytes 2985984 | tf_op jit(solution)/shard_map/reduce_scatter | solution.py:422
  275.1 58.8 %collective-permute-start.13 = (bf16[1152,1152]{1,0:T(8,128)(2,1)}, bf16[1152,1152]{1,0:T(8,128)(2,1)S(1)}, u32[]{:S(2)}, u32[]{:S(2)}) collective-permute-start(bf16[1152,1152]{1,0:T(8,128)(2,1)} %all-gather.7.cloned.1.call-done), channel_id=1, source_target_pairs={{0,2},{1,3},{2,0},{3,1},{4,6},{5,7},{6,4},{7,5},{8,10},{9,11},{10,... | collective-permute-start | bytes 7962632 | tf_op jit(solution)/shard_map/ppermute | solution.py:289
  275.5 65.2 %collective-permute-start.12 = (bf16[1152,1152]{1,0:T(8,128)(2,1)}, bf16[1152,1152]{1,0:T(8,128)(2,1)S(1)}, u32[]{:S(2)}, u32[]{:S(2)}) collective-permute-start(bf16[1152,1152]{1,0:T(8,128)(2,1)} %all-gather.7.cloned.1.call-done), channel_id=1, source_target_pairs={{0,1},{1,0},{2,3},{3,2},{4,5},{5,4},{6,7},{7,6},{8,9},{9,8},{10,11... | collective-permute-start | bytes 7962632 | tf_op jit(solution)/shard_map/ppermute | solution.py:289
  395.0 330.6 %reduce-scatter.11.cloned.1.call-start = ((), (), s32[]{:S(2)}) async-start(), calls=%async_computation.10 | async-start | bytes 11943936 | tf_op jit(solution)/shard_map/reduce_scatter | solution.py:438
  399.1 27.6 %collective-permute-start.14 = (bf16[288,512]{1,0:T(8,128)(2,1)}, bf16[288,512]{1,0:T(8,128)(2,1)S(1)}, u32[]{:S(2)}, u32[]{:S(2)}) collective-permute-start(bf16[288,512]{1,0:T(8,128)(2,1)} %convolution_convert_fusion.9), channel_id=1, source_target_pairs={{0,1},{1,0},{2,3},{3,2},{4,5},{5,4},{6,7},{7,6},{8,9},{9,8},{10,11... | collective-permute-start | bytes 884744 | tf_op jit(solution)/shard_map/ppermute | solution.py:289
  400.4 26.3 %collective-permute-start.15 = (bf16[288,512]{1,0:T(8,128)(2,1)}, bf16[288,512]{1,0:T(8,128)(2,1)}, u32[]{:S(2)}, u32[]{:S(2)}) collective-permute-start(bf16[288,512]{1,0:T(8,128)(2,1)} %convolution_convert_fusion.8), channel_id=1, source_target_pairs={{0,2},{1,3},{2,0},{3,1},{4,6},{5,7},{6,4},{7,5},{8,10},{9,11},{10,... | collective-permute-start | bytes 884744 | tf_op jit(solution)/shard_map/ppermute | solution.py:289
  403.5 23.2 %collective-permute-start.16 = (bf16[288,512]{1,0:T(8,128)(2,1)}, bf16[288,512]{1,0:T(8,128)(2,1)}, u32[]{:S(2)}, u32[]{:S(2)}) collective-permute-start(bf16[288,512]{1,0:T(8,128)(2,1)} %convolution_convert_fusion.7), channel_id=1, source_target_pairs={{0,3},{1,2},{2,1},{3,0},{4,7},{5,6},{6,5},{7,4},{8,11},{9,10},{10,... | collective-permute-start | bytes 884744 | tf_op jit(solution)/shard_map/ppermute | solution.py:289
  478.2 310.6 %reduce-scatter.13.cloned.1.call-start = ((), (), s32[]{:S(2)}) async-start(), calls=%async_computation.12 | async-start | bytes 2451456
  486.4 69.5 %collective-permute-start.17 = (bf16[288,512]{1,0:T(8,128)(2,1)}, bf16[288,512]{1,0:T(8,128)(2,1)}, u32[]{:S(2)}, u32[]{:S(2)}) collective-permute-start(bf16[288,512]{1,0:T(8,128)(2,1)} %convolution_convert_fusion.5), channel_id=1, source_target_pairs={{0,1},{1,0},{2,3},{3,2},{4,5},{5,4},{6,7},{7,6},{8,9},{9,8},{10,11... | collective-permute-start | bytes 884744 | tf_op jit(solution)/shard_map/ppermute | solution.py:289
  489.1 66.8 %collective-permute-start.18 = (bf16[288,512]{1,0:T(8,128)(2,1)}, bf16[288,512]{1,0:T(8,128)(2,1)}, u32[]{:S(2)}, u32[]{:S(2)}) collective-permute-start(bf16[288,512]{1,0:T(8,128)(2,1)} %convolution_convert_fusion.4), channel_id=1, source_target_pairs={{0,2},{1,3},{2,0},{3,1},{4,6},{5,7},{6,4},{7,5},{8,10},{9,11},{10,... | collective-permute-start | bytes 884744 | tf_op jit(solution)/shard_map/ppermute | solution.py:289
  498.2 16.9 %collective-permute-start.39 = (bf16[144,1152]{1,0:T(8,128)(2,1)S(1)}, bf16[144,1152]{1,0:T(8,128)(2,1)S(1)}, u32[]{:S(2)}, u32[]{:S(2)}) collective-permute-start(bf16[144,1152]{1,0:T(8,128)(2,1)S(1)} %get-tuple-element.152), channel_id=1, source_target_pairs={{0,2},{1,3},{2,0},{3,1},{4,6},{5,7},{6,4},{7,5},{8,10},{9,11},{10,... | collective-permute-start | bytes 995336 | tf_op jit(solution)/shard_map/ppermute | solution.py:289
  498.5 16.6 %collective-permute-start.38 = (bf16[144,1152]{1,0:T(8,128)(2,1)S(1)}, bf16[144,1152]{1,0:T(8,128)(2,1)S(1)}, u32[]{:S(2)}, u32[]{:S(2)}) collective-permute-start(bf16[144,1152]{1,0:T(8,128)(2,1)S(1)} %get-tuple-element.150), channel_id=1, source_target_pairs={{0,1},{1,0},{2,3},{3,2},{4,5},{5,4},{6,7},{7,6},{8,9},{9,8},{10,11... | collective-permute-start | bytes 995336 | tf_op jit(solution)/shard_map/ppermute | solution.py:289
  517.2 17.6 %collective-permute-start.42 = (bf16[144,1152]{1,0:T(8,128)(2,1)S(1)}, bf16[144,1152]{1,0:T(8,128)(2,1)}, u32[]{:S(2)}, u32[]{:S(2)}) collective-permute-start(bf16[144,1152]{1,0:T(8,128)(2,1)S(1)} %add_convert_fusion.3), channel_id=1, source_target_pairs={{0,2},{1,3},{2,0},{3,1},{4,6},{5,7},{6,4},{7,5},{8,10},{9,11},{10,... | collective-permute-start | bytes 995336 | tf_op jit(solution)/shard_map/ppermute | solution.py:289
  517.5 17.3 %collective-permute-start.41 = (bf16[144,1152]{1,0:T(8,128)(2,1)S(1)}, bf16[144,1152]{1,0:T(8,128)(2,1)}, u32[]{:S(2)}, u32[]{:S(2)}) collective-permute-start(bf16[144,1152]{1,0:T(8,128)(2,1)S(1)} %add_convert_fusion.3), channel_id=1, source_target_pairs={{0,1},{1,0},{2,3},{3,2},{4,5},{5,4},{6,7},{7,6},{8,9},{9,8},{10,11... | collective-permute-start | bytes 995336 | tf_op jit(solution)/shard_map/ppermute | solution.py:289
  526.3 29.6 %collective-permute-start.19 = (bf16[288,512]{1,0:T(8,128)(2,1)S(1)}, bf16[288,512]{1,0:T(8,128)(2,1)S(1)}, u32[]{:S(2)}, u32[]{:S(2)}) collective-permute-start(bf16[288,512]{1,0:T(8,128)(2,1)S(1)} %convolution_convert_fusion.3), channel_id=1, source_target_pairs={{0,3},{1,2},{2,1},{3,0},{4,7},{5,6},{6,5},{7,4},{8,11},{9,10},{10,... | collective-permute-start | bytes 884744 | tf_op jit(solution)/shard_map/ppermute | solution.py:289
  611.3 43.9 %collective-permute-start.25 = (bf16[512,1152]{1,0:T(8,128)(2,1)}, bf16[512,1152]{1,0:T(8,128)(2,1)}, u32[]{:S(2)}, u32[]{:S(2)}) collective-permute-start(bf16[512,1152]{1,0:T(8,128)(2,1)} %get-tuple-element.139), channel_id=1, source_target_pairs={{0,3},{1,2},{2,1},{3,0},{4,7},{5,6},{6,5},{7,4},{8,11},{9,10},{10,... | collective-permute-start | bytes 3538952 | tf_op jit(solution)/shard_map/ppermute | solution.py:289
  616.7 49.2 %collective-permute-start.24 = (bf16[512,1152]{1,0:T(8,128)(2,1)}, bf16[512,1152]{1,0:T(8,128)(2,1)}, u32[]{:S(2)}, u32[]{:S(2)}) collective-permute-start(bf16[512,1152]{1,0:T(8,128)(2,1)} %get-tuple-element.138), channel_id=1, source_target_pairs={{0,2},{1,3},{2,0},{3,1},{4,6},{5,7},{6,4},{7,5},{8,10},{9,11},{10,... | collective-permute-start | bytes 3538952 | tf_op jit(solution)/shard_map/ppermute | solution.py:289
  621.8 44.1 %collective-permute-start.23 = (bf16[512,1152]{1,0:T(8,128)(2,1)}, bf16[512,1152]{1,0:T(8,128)(2,1)}, u32[]{:S(2)}, u32[]{:S(2)}) collective-permute-start(bf16[512,1152]{1,0:T(8,128)(2,1)} %get-tuple-element.137), channel_id=1, source_target_pairs={{0,1},{1,0},{2,3},{3,2},{4,5},{5,4},{6,7},{7,6},{8,9},{9,8},{10,11... | collective-permute-start | bytes 3538952 | tf_op jit(solution)/shard_map/ppermute | solution.py:289
  652.9 37.9 %collective-permute-start.22 = (bf16[512,1152]{1,0:T(8,128)(2,1)}, bf16[512,1152]{1,0:T(8,128)(2,1)}, u32[]{:S(2)}, u32[]{:S(2)}) collective-permute-start(bf16[512,1152]{1,0:T(8,128)(2,1)} %get-tuple-element.78), channel_id=1, source_target_pairs={{0,3},{1,2},{2,1},{3,0},{4,7},{5,6},{6,5},{7,4},{8,11},{9,10},{10,... | collective-permute-start | bytes 3538952 | tf_op jit(solution)/shard_map/ppermute | solution.py:289
  654.1 58.6 %collective-permute-start.21 = (bf16[512,1152]{1,0:T(8,128)(2,1)}, bf16[512,1152]{1,0:T(8,128)(2,1)}, u32[]{:S(2)}, u32[]{:S(2)}) collective-permute-start(bf16[512,1152]{1,0:T(8,128)(2,1)} %get-tuple-element.77), channel_id=1, source_target_pairs={{0,2},{1,3},{2,0},{3,1},{4,6},{5,7},{6,4},{7,5},{8,10},{9,11},{10,... | collective-permute-start | bytes 3538952 | tf_op jit(solution)/shard_map/ppermute | solution.py:289
  655.2 57.4 %collective-permute-start.20 = (bf16[512,1152]{1,0:T(8,128)(2,1)}, bf16[512,1152]{1,0:T(8,128)(2,1)}, u32[]{:S(2)}, u32[]{:S(2)}) collective-permute-start(bf16[512,1152]{1,0:T(8,128)(2,1)} %get-tuple-element.76), channel_id=1, source_target_pairs={{0,1},{1,0},{2,3},{3,2},{4,5},{5,4},{6,7},{7,6},{8,9},{9,8},{10,11... | collective-permute-start | bytes 3538952 | tf_op jit(solution)/shard_map/ppermute | solution.py:289
  725.6 43.6 %collective-permute-start.31 = (bf16[144,1152]{1,0:T(8,128)(2,1)S(1)}, bf16[144,1152]{1,0:T(8,128)(2,1)S(1)}, u32[]{:S(2)}, u32[]{:S(2)}) collective-permute-start(bf16[144,1152]{1,0:T(8,128)(2,1)S(1)} %copy-done.61), channel_id=1, source_target_pairs={{0,3},{1,2},{2,1},{3,0},{4,7},{5,6},{6,5},{7,4},{8,11},{9,10},{10,... | collective-permute-start | bytes 995336 | tf_op jit(solution)/shard_map/ppermute | solution.py:289
  726.3 44.3 %collective-permute-start.30 = (bf16[144,1152]{1,0:T(8,128)(2,1)S(1)}, bf16[144,1152]{1,0:T(8,128)(2,1)S(1)}, u32[]{:S(2)}, u32[]{:S(2)}) collective-permute-start(bf16[144,1152]{1,0:T(8,128)(2,1)S(1)} %copy-done.61), channel_id=1, source_target_pairs={{0,2},{1,3},{2,0},{3,1},{4,6},{5,7},{6,4},{7,5},{8,10},{9,11},{10,... | collective-permute-start | bytes 995336 | tf_op jit(solution)/shard_map/ppermute | solution.py:289
  736.3 30.0 %collective-permute-start.34 = (bf16[144,1152]{1,0:T(8,128)(2,1)S(1)}, bf16[144,1152]{1,0:T(8,128)(2,1)S(1)}, u32[]{:S(2)}, u32[]{:S(2)}) collective-permute-start(bf16[144,1152]{1,0:T(8,128)(2,1)S(1)} %get-tuple-element.158), channel_id=1, source_target_pairs={{0,3},{1,2},{2,1},{3,0},{4,7},{5,6},{6,5},{7,4},{8,11},{9,10},{10,... | collective-permute-start | bytes 995336 | tf_op jit(solution)/shard_map/ppermute | solution.py:289
  737.8 29.9 %collective-permute-start.33 = (bf16[144,1152]{1,0:T(8,128)(2,1)S(1)}, bf16[144,1152]{1,0:T(8,128)(2,1)S(1)}, u32[]{:S(2)}, u32[]{:S(2)}) collective-permute-start(bf16[144,1152]{1,0:T(8,128)(2,1)S(1)} %get-tuple-element.159), channel_id=1, source_target_pairs={{0,2},{1,3},{2,0},{3,1},{4,6},{5,7},{6,4},{7,5},{8,10},{9,11},{10,... | collective-permute-start | bytes 995336 | tf_op jit(solution)/shard_map/ppermute | solution.py:289
  739.1 28.6 %collective-permute-start.32 = (bf16[144,1152]{1,0:T(8,128)(2,1)S(1)}, bf16[144,1152]{1,0:T(8,128)(2,1)S(1)}, u32[]{:S(2)}, u32[]{:S(2)}) collective-permute-start(bf16[144,1152]{1,0:T(8,128)(2,1)S(1)} %get-tuple-element.157), channel_id=1, source_target_pairs={{0,1},{1,0},{2,3},{3,2},{4,5},{5,4},{6,7},{7,6},{8,9},{9,8},{10,11... | collective-permute-start | bytes 995336 | tf_op jit(solution)/shard_map/ppermute | solution.py:289
  767.9 13.9 %collective-permute-start.37 = (bf16[144,1152]{1,0:T(8,128)(2,1)S(1)}, bf16[144,1152]{1,0:T(8,128)(2,1)S(1)}, u32[]{:S(2)}, u32[]{:S(2)}) collective-permute-start(bf16[144,1152]{1,0:T(8,128)(2,1)S(1)} %add_convert_fusion.4), channel_id=1, source_target_pairs={{0,3},{1,2},{2,1},{3,0},{4,7},{5,6},{6,5},{7,4},{8,11},{9,10},{10,... | collective-permute-start | bytes 995336 | tf_op jit(solution)/shard_map/ppermute | solution.py:289
  768.6 13.2 %collective-permute-start.36 = (bf16[144,1152]{1,0:T(8,128)(2,1)S(1)}, bf16[144,1152]{1,0:T(8,128)(2,1)S(1)}, u32[]{:S(2)}, u32[]{:S(2)}) collective-permute-start(bf16[144,1152]{1,0:T(8,128)(2,1)S(1)} %add_convert_fusion.4), channel_id=1, source_target_pairs={{0,2},{1,3},{2,0},{3,1},{4,6},{5,7},{6,4},{7,5},{8,10},{9,11},{10,... | collective-permute-start | bytes 995336 | tf_op jit(solution)/shard_map/ppermute | solution.py:289
  769.2 19.3 %collective-permute-start.35 = (bf16[144,1152]{1,0:T(8,128)(2,1)S(1)}, bf16[144,1152]{1,0:T(8,128)(2,1)S(1)}, u32[]{:S(2)}, u32[]{:S(2)}) collective-permute-start(bf16[144,1152]{1,0:T(8,128)(2,1)S(1)} %add_convert_fusion.4), channel_id=1, source_target_pairs={{0,1},{1,0},{2,3},{3,2},{4,5},{5,4},{6,7},{7,6},{8,9},{9,8},{10,11... | collective-permute-start | bytes 995336 | tf_op jit(solution)/shard_map/ppermute | solution.py:289
  789.9 14.5 %collective-permute-start.27 = (bf16[152,864]{1,0:T(8,128)(2,1)}, bf16[152,864]{1,0:T(8,128)(2,1)S(1)}, u32[]{:S(2)}, u32[]{:S(2)}) collective-permute-start(bf16[152,864]{1,0:T(8,128)(2,1)} %bitcast.227), channel_id=1, source_target_pairs={{0,2},{1,3},{2,0},{3,1},{4,6},{5,7},{6,4},{7,5},{8,10},{9,11},{10,... | collective-permute-start | bytes 787976 | tf_op jit(solution)/shard_map/ppermute | solution.py:289
  791.4 12.9 %collective-permute-start.26 = (bf16[152,864]{1,0:T(8,128)(2,1)}, bf16[152,864]{1,0:T(8,128)(2,1)S(1)}, u32[]{:S(2)}, u32[]{:S(2)}) collective-permute-start(bf16[152,864]{1,0:T(8,128)(2,1)} %bitcast.228), channel_id=1, source_target_pairs={{0,1},{1,0},{2,3},{3,2},{4,5},{5,4},{6,7},{7,6},{8,9},{9,8},{10,11... | collective-permute-start | bytes 787976 | tf_op jit(solution)/shard_map/ppermute | solution.py:289
  (136 other events, 1722.3 us)
Sparse Core Ops, SparseCore 0:
  15.9 31.2 all-gather.14
  49.5 32.9 all-gather.6
  84.1 33.0 all-gather.8
  119.3 97.2 all-gather.10
  227.2 35.1 all-gather.12
  275.2 110.5 reduce-scatter.6
  395.1 32.9 reduce-scatter.8
  478.3 106.9 reduce-scatter.10
  735.0 33.9 reduce-scatter.12

commit v4 on v3

--- a/solution.py
+++ b/solution.py
@@ -1,4 +1,6 @@
 import functools
+import math
+
 import jax
 import jax.numpy as jnp
 from jax import lax
@@ -264,6 +266,14 @@
     return inverse * (scaled - flat - normed * along)
 
 
+def gelu_parts(hidden):
+    first, third = math.sqrt(2 / math.pi), 0.044715 * math.sqrt(2 / math.pi)
+    square = hidden * hidden
+    half = 0.5 + 0.5 * jnp.tanh(hidden * (first + third * square))
+    value = hidden * half
+    return value, half + 2 * value * (1 - half) * (first + 3 * third * square)
+
+
 def contract(left, right, left_axis, right_axis):
     return lax.dot_general(left, right, (((left_axis,), (right_axis,)), ((), ())), preferred_element_type=jnp.float32)
 
@@ -365,7 +375,8 @@
     for row in range(count):
         ids = picture_ids[row]
         low, high = block_ranges(ids, block)
-        tables.append((low, high, jnp.broadcast_to(ids[:, None], (length, 128)), jnp.broadcast_to(ids[None], (8, length))))
+        ids_table = (jnp.broadcast_to(ids[:, None], (length, 128)), jnp.broadcast_to(ids[None], (8, length)))
+        tables.append((low, high, *ids_table))
         attn_input = jnp.concatenate(
             [(norm_parts(piece.astype(f32))[0] * gain1 + shift1).astype(bf16) for piece in whole_rows[row]], axis=0
         )
@@ -387,8 +398,8 @@
     mlp_input = (normed2 * gain2 + shift2).astype(bf16)
     total = None
     hidden = contract(mlp_input, up_whole, 1, 0) + up_off
-    gelu_out, pull = jax.vjp(lambda v: jax.nn.gelu(v, approximate=True), hidden)
-    gelu_out, slope = gelu_out.astype(bf16), pull(jnp.ones_like(hidden))[0].astype(bf16)
+    gelu_out, slope = gelu_parts(hidden)
+    gelu_out, slope = gelu_out.astype(bf16), slope.astype(bf16)
 
     def slab_of(value, hop):
         return value[:, hop * slab : (hop + 1) * slab]
@@ -418,24 +429,30 @@
     grad_output = contract(mixed_all, grad_attn, 1, 0)
     grad_output = relative(grad_output.astype(bf16).reshape(seq_count, part, width))
     grad_output = jnp.concatenate(grad_output, axis=0)
-    packs[0], down_raw, grad_output = lax.optimization_barrier((packs[0], down_raw, grad_output))
-    output_share = lax.psum_scatter(grad_output, "rows", scatter_dimension=0, tiled=True)
+    mixed_grads = []
+    for row in range(count):
+        pieces = []
+        for hop in range(seq_count):
+            piece = contract(outputs[hop], grad_attn[row * chunk : (row + 1) * chunk], 1, 1).astype(bf16)
+            pieces.append(swap(piece, hop) if hop else piece)
+        mixed_grads.append(pieces)
+    held = lax.optimization_barrier((packs[0], down_raw, grad_up, grad_output, *mixed_grads[0]))
+    packs[0], down_raw, grad_up, grad_output = held[:4]
+    mixed_grads[0] = list(held[4:])
+    up_raw = lax.psum_scatter(grad_up, "rows", scatter_dimension=0, tiled=True)
     down_share = exchange_sum([slab_of(down_raw, hop) for hop in range(seq_count)]).astype(bf16)
     down_pieces = all_pieces(down_share)
     heads_grad, query_grad, value_grad, gain_grad, shift_grad, grad_in = None, 0.0, 0.0, 0.0, 0.0, []
     after = None
     for row in range(count):
-        grad_mixed = []
-        for hop in range(seq_count):
-            piece = contract(outputs[hop], grad_attn[row * chunk : (row + 1) * chunk], 1, 1).astype(bf16)
-            grad_mixed.append(swap(piece, hop) if hop else piece)
+        grad_mixed = mixed_grads[row]
         pack = packs[row]
         if after is not None:
             pack, grad_in[-1] = lax.optimization_barrier((pack, grad_in[-1]))
         grad_pack = attend_back(pack, grad_mixed, mixes[row], logs[row], *tables[row], place_array)
-        if row == 0:
-            grad_pack, output_share, grad_up = lax.optimization_barrier((grad_pack, output_share, grad_up))
-            up_raw = lax.psum_scatter(grad_up, "rows", scatter_dimension=0, tiled=True)
+        if row == count - 1:
+            grad_pack, up_raw, grad_output = lax.optimization_barrier((grad_pack, up_raw, grad_output))
+            output_share = lax.psum_scatter(grad_output, "rows", scatter_dimension=0, tiled=True)
         query_grad = query_grad + jnp.sum(grad_pack[0].astype(f32), axis=1)
         value_grad = value_grad + jnp.sum(grad_pack[2].astype(f32), axis=1)
         grad_pack = grad_pack.reshape(3 * part, length)
@@ -467,7 +484,10 @@
     ]
     together = jnp.concatenate([value.reshape(row_count, -1) for value in small_grads], axis=1).astype(bf16)
     heads_grad = beside(heads_grad.astype(bf16).reshape(row_count, band_width, 3 * part), together)
-    heads_grad, up_raw = lax.optimization_barrier((heads_grad, up_raw))
+    held = lax.optimization_barrier((heads_grad, output_share, *[pieces[0] for pieces in grad_in]))
+    heads_grad, output_share = held[:2]
+    for row in range(count):
+        grad_in[row][0] = held[2 + row]
     gelu_late, output_share, up_raw, heads_grad = lax.optimization_barrier((gelu_out, output_share, up_raw, heads_grad))
     total = resid
     for hop in range(seq_count):

time: 827 us -> 814 us (0.984)
  matrix products: 248 us -> 234 us
    dot_general x34, matrix products: 248 us -> 234 us  [contract(): lax.dot_general(left, right, (((left_axis,), (right_axis,)), ((), ())), p...]
    unnamed x265 -> x277, local copies, waits for them, and re-layouts: 22 us -> 19.4 us
  transfers between devices with their start and end apart: 53 -> 53, of which waited for: 18 -> 16; matrix products, arithmetic and copies ran while one was open for 47% -> 46% of each run, Pallas kernels for 18% -> 18%
where the time goes in v4:
time: 814 us; the launch traced here: 806 us
  matrix products  234 us (29%)
  waiting for transfers between devices  194 us (24%)
  Pallas kernels  148 us (18%)
  local copies, waits for them, and re-layouts  90.7 us (11%)
  other arithmetic  85.2 us (10%)
  starting transfers between devices  38.4 us (5%)
  between operations  16.2 us (2%)
    dot_general x34, matrix products, contract(): lax.dot_general(left, right, (((left_axis,), (right_axis,)), ((), ())), p...  234 us
    ppermute x44, waiting for transfers between devices, swap(): return lax.ppermute(value, 'seq', [(i, i ^ hop) for i in range(seq_count)])  193 us
    pallas_call x2, Pallas kernels, attend_back(): pl.pallas_call(functools.partial(attend_back_kernel, count=count, block=b...  100 us
    pallas_call x2, Pallas kernels, attend(): pl.pallas_call(functools.partial(attend_kernel, count=count, block=block,...  47.7 us
    ppermute x44, starting transfers between devices, swap(): return lax.ppermute(value, 'seq', [(i, i ^ hop) for i in range(seq_count)])  38 us
    unnamed x277, local copies, waits for them, and re-layouts  19.4 us
  transfers between devices with their start and end apart: 53, of which 16 were waited for; matrix products, arithmetic and copies ran while one was open for 46% of the time, Pallas kernels for 18%

profile of v4, /device:TPU:9, one launch (start us, length us, event | category | flops | bytes accessed | tf_op | source)
XLA Modules:
  0.0 806.0 jit_solution(2910013751718070803)
XLA Ops:
  7.3 6.3 concatenate.78
  33.6 15.1 %collective-permute-done.1 = bf16[512,1152]{1,0:T(8,128)(2,1)} collective-permute-done((bf16[512,1152]{1,0:T(8,128)(2,1)}, bf16[512,1152]{1,0:T(8,128)(2,1)}, u32[]{:S(2)}, u32[]{:S(2)}) %collective-permute-start.1) | collective-permute-done | bytes 1179680 | tf_op jit(solution)/shard_map/ppermute | solution.py:299
  49.6 25.2 %collective-permute-done.2 = bf16[512,1152]{1,0:T(8,128)(2,1)} collective-permute-done((bf16[512,1152]{1,0:T(8,128)(2,1)}, bf16[512,1152]{1,0:T(8,128)(2,1)}, u32[]{:S(2)}, u32[]{:S(2)}) %collective-permute-start.2) | collective-permute-done | bytes 1179680 | tf_op jit(solution)/shard_map/ppermute | solution.py:299
  103.5 5.6 fusion.58
  109.1 8.2 %add_convert_fusion.2 = bf16[864,2048]{1,0:T(8,128)(2,1)S(1)} fusion(bf16[1152,864]{1,0:T(8,128)(2,1)S(1)} %bitcast.204, f32[864]{0:T(1024)S(1)} %pad_maximum_fusion.23, bf16[512,1152]{1,0:T(8,128)(2,1)S(1)} %get-tuple-element.229, bf16[512,1152]{1,0:T(8,128)(2,1)S(1)} %get-tuple-element.228, bf16[512,1152]{1,0:T(8,128)(2,1)S(1)} %get-tuple-element.227, ...), kind=kOutput, calls=%fused_computation.11 | convolution fusion | flops 4099276800 | bytes 10251648 | tf_op jit(solution)/shard_map/dot_general | solution.py:278
  129.2 24.6 %attend.2 = (bf16[4,288,512]{2,1,0:T(8,128)(2,1)S(1)}, f32[8,2048]{1,0:T(8,128)S(1)}) custom-call(s32[8]{0:T(128)S(1)} %get-tuple-element.254.low_ref, s32[8]{0:T(128)S(1)} %get-tuple-element.255.high_ref, s32[1]{0:T(128)} %bitcast.3.place_ref, bf16[3,288,2048]{2,1,0:T(8,128)(2,1)S(1)} %bitcast.180, s32[2048,128]{1,0:T(8,128)S(1)} %broadcast_in_dim.22.kid_ref, ...), custom_call_target="tpu_custom_call" | custom-call | flops 6710886400 | bytes 4718592 | tf_op jit(solution)/shard_map/attend/pallas_call | solution.py:102
  170.1 8.4 %add_convert_fusion.1 = bf16[864,2048]{1,0:T(8,128)(2,1)S(1)} fusion(bf16[1152,864]{1,0:T(8,128)(2,1)S(1)} %bitcast.205, f32[864]{0:T(1024)S(1)} %copy-done.114, bf16[512,1152]{1,0:T(8,128)(2,1)S(1)} %get-tuple-element.233, bf16[512,1152]{1,0:T(8,128)(2,1)S(1)} %get-tuple-element.232, bf16[512,1152]{1,0:T(8,128)(2,1)S(1)} %get-tuple-element.231, ...), kind=kOutput, calls=%fused_computation.10 | convolution fusion | flops 4099276800 | bytes 10251648 | tf_op jit(solution)/shard_map/dot_general | solution.py:278
  178.9 23.1 %attend.3 = (bf16[4,288,512]{2,1,0:T(8,128)(2,1)S(1)}, f32[8,2048]{1,0:T(8,128)S(1)}) custom-call(s32[8]{0:T(128)S(1)} %get-tuple-element.132.low_ref, s32[8]{0:T(128)S(1)} %get-tuple-element.131.high_ref, s32[1]{0:T(128)} %bitcast.3.place_ref, bf16[3,288,2048]{2,1,0:T(8,128)(2,1)S(1)} %bitcast.178, s32[2048,128]{1,0:T(8,128)S(1)} %broadcast_in_dim.25.kid_ref, ...), custom_call_target="tpu_custom_call" | custom-call | flops 6710886400 | bytes 4718592 | tf_op jit(solution)/shard_map/attend/pallas_call | solution.py:102
  208.1 4.9 collective-permute-done.11
  213.0 6.5 collective-permute-done.9
  219.6 5.2 fusion.162
  229.3 26.8 %add_convert_fusion = (bf16[1024,4608]{1,0:T(8,128)(2,1)}, bf16[1024,4608]{1,0:T(8,128)(2,1)S(1)}) fusion(f32[4608]{0:T(1024)S(1)} %pad_maximum_fusion.21, bf16[1152,4608]{1,0:T(8,128)(2,1)} %all-gather.11.cloned.1.call-done, f32[1024,1152]{1,0:T(8,128)} %copy-done.19, f32[1152]{0:T(1024)S(1)} %copy-done.100, f32[1152]{0:T(1024)S(1)} %copy-done.72, ...), kind=kOutput, calls=%fused_computation.3 | convolution fusion | flops 10957750272 | bytes 34245632 | tf_op jit(solution)/shard_map/dot_general | solution.py:278
  256.1 3.6 copy-done.128
  259.7 14.3 %fusion.2 = bf16[1152,4608]{1,0:T(8,128)(2,1)} fusion(bf16[1024,4608]{1,0:T(8,128)(2,1)S(1)} %get-tuple-element.87, bf16[1024,1152]{1,0:T(8,128)(2,1)S(1)} %bitcast.197), kind=kOutput, calls=%fused_computation.7 | convolution fusion | flops 10876944384 | bytes 22413312 | tf_op jit(solution)/shard_map/dot_general | solution.py:278
  275.4 7.2 fusion.13
  282.6 50.5 %collective-permute-done.13 = bf16[1152,1152]{1,0:T(8,128)(2,1)S(1)} collective-permute-done((bf16[1152,1152]{1,0:T(8,128)(2,1)}, bf16[1152,1152]{1,0:T(8,128)(2,1)S(1)}, u32[]{:S(2)}, u32[]{:S(2)}) %collective-permute-start.13) | collective-permute-done | bytes 2654240 | tf_op jit(solution)/shard_map/ppermute | solution.py:299
  333.2 6.9 fusion.15
  341.6 6.0 fusion.14
  347.6 8.2 %fusion.16 = bf16[1024,1152]{1,0:T(8,128)(2,1)} fusion(bf16[1024,1152]{1,0:T(8,128)(2,1)} %bitcast.195, bf16[1152,1152]{1,0:T(8,128)(2,1)} %all-gather.13.cloned.1.call-done, bf16[1024,4608]{1,0:T(8,128)(2,1)} %get-tuple-element.136), kind=kOutput, calls=%fused_computation.46 | convolution fusion | flops 2721447936 | bytes 9732096 | tf_op jit(solution)/shard_map/dot_general | solution.py:278
  355.9 19.9 %multiply_reduce_fusion = (bf16[1152]{0:T(1024)(128)(2,1)S(1)}, f32[1024]{0:T(1024)S(1)}, f32[1024]{0:T(1024)S(1)}, bf16[1152]{0:T(1024)(128)(2,1)S(1)}, f32[1024,1152]{1,0:T(8,128)}) fusion(f32[1024,1152]{1,0:T(8,128)} %copy-done.19, f32[1024]{0:T(1024)S(1)} %add_rsqrt_fusion.1, f32[1024]{0:T(1024)S(1)} %broadcast_multiply_fusion.4, ...), kind=kOutput, calls=%fused_computation.34 | convolution fusion | flops 10919997440 | bytes 29516800 | tf_op jit(solution)/shard_map/dot_general | solution.py:278
  375.8 7.4 fusion.153
  389.9 4.4 convolution_convert_fusion.2
  394.5 19.5 %convolution_convert_fusion = bf16[1152,4608]{1,0:T(8,128)(2,1)} fusion(f32[1024,1152]{1,0:T(8,128)} %copy-done.19, f32[1152]{0:T(1024)S(1)} %copy-done.100, f32[1152]{0:T(1024)S(1)} %copy-done.72, f32[1024]{0:T(1024)S(1)} %add_rsqrt_fusion.1, f32[1024]{0:T(1024)S(1)} %broadcast_multiply_fusion.4, bf16[1024,1152]{1,0:T(8,128)(2,1)} %fusion.16, ...), kind=kOutput, calls=%fused_computation | convolution fusion | flops 10920591360 | bytes 24790016 | tf_op jit(solution)/shard_map/dot_general | solution.py:278
  414.0 6.1 pad_maximum_fusion.4
  429.3 5.8 convert_reduce_fusion
  450.4 51.3 %attend_back.2 = bf16[3,288,2048]{2,1,0:T(8,128)(2,1)} custom-call(s32[8]{0:T(128)} %copy-done.10, s32[8]{0:T(128)} %copy-done.11, s32[1]{0:T(128)} %bitcast.3.place_ref, bf16[3,288,2048]{2,1,0:T(8,128)(2,1)} %bitcast.181, bf16[4,288,512]{2,1,0:T(8,128)(2,1)} %copy-done.3, f32[8,2048]{1,0:T(8,128)} %copy-done.15, s32[2048,128]{1,0:T(8,128)} %copy-done.5, ...), custom_call_target="tpu_custom_call" | custom-call | flops 16777216000 | bytes 9437184 | tf_op jit(solution)/shard_map/attend_back/pallas_call | solution.py:215
  501.8 5.7 fusion.149
  507.5 4.8 fusion.148
  515.9 6.7 fusion.116
  534.9 48.7 %attend_back.3 = bf16[3,288,2048]{2,1,0:T(8,128)(2,1)} custom-call(s32[8]{0:T(128)} %copy-done.9, s32[8]{0:T(128)} %copy-done.8, s32[1]{0:T(128)} %bitcast.3.place_ref, bf16[3,288,2048]{2,1,0:T(8,128)(2,1)} %bitcast.179, bf16[4,288,512]{2,1,0:T(8,128)(2,1)} %copy-done.2, f32[8,2048]{1,0:T(8,128)} %copy-done.14, s32[2048,128]{1,0:T(8,128)} %copy-done.4, ...), custom_call_target="tpu_custom_call" | custom-call | flops 16777216000 | bytes 9437184 | tf_op jit(solution)/shard_map/attend_back/pallas_call | solution.py:215
  591.3 4.7 fusion.151
  596.8 4.7 fusion.152
  601.6 4.8 fusion.150
  606.5 3.9 fusion.147
  611.0 6.0 fusion.17
  625.2 4.3 copy.54
  639.7 8.3 %fusion.97 = f32[1024,1152]{1,0:T(8,128)} fusion(bf16[1152,1152]{1,0:T(8,128)(2,1)} %all-gather.7.cloned.1.call-done, bf16[1024,4608]{1,0:T(8,128)(2,1)} %copy-done.128), kind=kOutput, calls=%fused_computation.146 | convolution fusion | flops 2717908992 | bytes 9732096 | tf_op jit(solution)/shard_map/dot_general | solution.py:278
  649.6 12.8 %collective-permute-done.23 = bf16[512,1152]{1,0:T(8,128)(2,1)} collective-permute-done((bf16[512,1152]{1,0:T(8,128)(2,1)}, bf16[512,1152]{1,0:T(8,128)(2,1)}, u32[]{:S(2)}, u32[]{:S(2)}) %collective-permute-start.23) | collective-permute-done | bytes 1179680 | tf_op jit(solution)/shard_map/ppermute | solution.py:299
  663.9 24.6 %collective-permute-done.25 = bf16[512,1152]{1,0:T(8,128)(2,1)} collective-permute-done((bf16[512,1152]{1,0:T(8,128)(2,1)}, bf16[512,1152]{1,0:T(8,128)(2,1)}, u32[]{:S(2)}, u32[]{:S(2)}) %collective-permute-start.25) | collective-permute-done | bytes 1179680 | tf_op jit(solution)/shard_map/ppermute | solution.py:299
  693.4 20.5 %collective-permute-done.22 = bf16[512,1152]{1,0:T(8,128)(2,1)S(1)} collective-permute-done((bf16[512,1152]{1,0:T(8,128)(2,1)S(1)}, bf16[512,1152]{1,0:T(8,128)(2,1)S(1)}, u32[]{:S(2)}, u32[]{:S(2)}) %collective-permute-start.22) | collective-permute-done | bytes 1179680 | tf_op jit(solution)/shard_map/ppermute | solution.py:299
  718.8 7.5 fusion.89
  726.3 7.4 fusion.95
  733.8 12.9 %add_add_fusion = f32[1024,1152]{1,0:T(8,128)} fusion(f32[1024,1152]{1,0:T(8,128)} %fusion.89, f32[1024,1152]{1,0:T(8,128)} %fusion.95, f32[1024,1152]{1,0:T(8,128)S(1)} %bitcast.186, f32[1024,1152]{1,0:T(8,128)} %fusion.97, f32[1152]{0:T(1024)S(1)} %copy-done.99, bf16[1152,1152]{1,0:T(8,128)(2,1)} %copy-done.116, bf16[1024,4608]{1,0:T(8,128)(2,1)} %copy-done.128), kind=kOutput, calls=%fused_computation.33 | convolution fusion | flops 2723807232 | bytes 28611072 | tf_op jit(solution)/shard_map/dot_general | solution.py:278
  753.9 6.3 collective-permute-done.29
  762.3 5.9 collective-permute-done.37
  769.9 4.5 collective-permute-done.35
  779.1 4.3 collective-permute-done.28
  783.4 6.8 collective-permute-done.27
  (537 shorter events, 202.4 us)
Async XLA Ops:
  7.2 79.9 %all-gather.15.cloned.1.call-start = ((), (), s32[]{:S(2)}) async-start(), calls=%async_computation.11 | async-start | bytes 2451456 | tf_op jit(solution)/shard_map/all_gather | solution.py:333
  15.8 142.1 %all-gather.7.cloned.1.call-start = ((), (), s32[]{:S(2)}) async-start(), calls=%async_computation.4 | async-start | bytes 2985984 | tf_op jit(solution)/shard_map/all_gather | solution.py:356
  16.7 189.2 %all-gather.9.cloned.1.call-start = ((), (), s32[]{:S(2)}) async-start(), calls=%async_computation.5 | async-start | bytes 2985984 | tf_op jit(solution)/shard_map/all_gather | solution.py:361
  17.4 210.3 %all-gather.11.cloned.1.call-start = ((), (), s32[]{:S(2)}) async-start(), calls=%async_computation.6 | async-start | bytes 11943936 | tf_op jit(solution)/shard_map/all_gather | solution.py:356
  19.0 328.7 %all-gather.13.cloned.1.call-start = ((), (), s32[]{:S(2)}) async-start(), calls=%async_computation.8 | async-start | bytes 2985984 | tf_op jit(solution)/shard_map/all_gather | solution.py:356
  21.5 27.2 %collective-permute-start.1 = (bf16[512,1152]{1,0:T(8,128)(2,1)}, bf16[512,1152]{1,0:T(8,128)(2,1)}, u32[]{:S(2)}, u32[]{:S(2)}) collective-permute-start(bf16[512,1152]{1,0:T(8,128)(2,1)} %get-tuple-element.158), channel_id=1, source_target_pairs={{0,2},{1,3},{2,0},{3,1},{4,6},{5,7},{6,4},{7,5},{8,10},{9,11},{10,... | collective-permute-start | bytes 3538952 | tf_op jit(solution)/shard_map/ppermute | solution.py:299
  22.7 26.9 %collective-permute-start = (bf16[512,1152]{1,0:T(8,128)(2,1)}, bf16[512,1152]{1,0:T(8,128)(2,1)S(1)}, u32[]{:S(2)}, u32[]{:S(2)}) collective-permute-start(bf16[512,1152]{1,0:T(8,128)(2,1)} %get-tuple-element.158), channel_id=1, source_target_pairs={{0,1},{1,0},{2,3},{3,2},{4,5},{5,4},{6,7},{7,6},{8,9},{9,8},{10,11... | collective-permute-start | bytes 3538952 | tf_op jit(solution)/shard_map/ppermute | solution.py:299
  23.9 50.9 %collective-permute-start.2 = (bf16[512,1152]{1,0:T(8,128)(2,1)}, bf16[512,1152]{1,0:T(8,128)(2,1)}, u32[]{:S(2)}, u32[]{:S(2)}) collective-permute-start(bf16[512,1152]{1,0:T(8,128)(2,1)} %get-tuple-element.158), channel_id=1, source_target_pairs={{0,3},{1,2},{2,1},{3,0},{4,7},{5,6},{6,5},{7,4},{8,11},{9,10},{10,... | collective-permute-start | bytes 3538952 | tf_op jit(solution)/shard_map/ppermute | solution.py:299
  74.9 82.3 %collective-permute-start.5 = (bf16[512,1152]{1,0:T(8,128)(2,1)}, bf16[512,1152]{1,0:T(8,128)(2,1)}, u32[]{:S(2)}, u32[]{:S(2)}) collective-permute-start(bf16[512,1152]{1,0:T(8,128)(2,1)} %get-tuple-element.61), channel_id=1, source_target_pairs={{0,3},{1,2},{2,1},{3,0},{4,7},{5,6},{6,5},{7,4},{8,11},{9,10},{10,... | collective-permute-start | bytes 3538952 | tf_op jit(solution)/shard_map/ppermute | solution.py:299
  77.0 80.8 %collective-permute-start.4 = (bf16[512,1152]{1,0:T(8,128)(2,1)}, bf16[512,1152]{1,0:T(8,128)(2,1)}, u32[]{:S(2)}, u32[]{:S(2)}) collective-permute-start(bf16[512,1152]{1,0:T(8,128)(2,1)} %get-tuple-element.61), channel_id=1, source_target_pairs={{0,2},{1,3},{2,0},{3,1},{4,6},{5,7},{6,4},{7,5},{8,10},{9,11},{10,... | collective-permute-start | bytes 3538952 | tf_op jit(solution)/shard_map/ppermute | solution.py:299
  77.3 80.6 %collective-permute-start.3 = (bf16[512,1152]{1,0:T(8,128)(2,1)}, bf16[512,1152]{1,0:T(8,128)(2,1)}, u32[]{:S(2)}, u32[]{:S(2)}) collective-permute-start(bf16[512,1152]{1,0:T(8,128)(2,1)} %get-tuple-element.61), channel_id=1, source_target_pairs={{0,1},{1,0},{2,3},{3,2},{4,5},{5,4},{6,7},{7,6},{8,9},{9,8},{10,11... | collective-permute-start | bytes 3538952 | tf_op jit(solution)/shard_map/ppermute | solution.py:299
  155.0 50.4 %collective-permute-start.10 = (bf16[288,512]{1,0:T(8,128)(2,1)S(1)}, bf16[288,512]{1,0:T(8,128)(2,1)S(1)}, u32[]{:S(2)}, u32[]{:S(2)}) collective-permute-start(bf16[288,512]{1,0:T(8,128)(2,1)S(1)} %get-tuple-element.179), channel_id=1, source_target_pairs={{0,3},{1,2},{2,1},{3,0},{4,7},{5,6},{6,5},{7,4},{8,11},{9,10},{10,... | collective-permute-start | bytes 884744 | tf_op jit(solution)/shard_map/ppermute | solution.py:299
  156.9 51.2 %collective-permute-start.8 = (bf16[288,512]{1,0:T(8,128)(2,1)S(1)}, bf16[288,512]{1,0:T(8,128)(2,1)S(1)}, u32[]{:S(2)}, u32[]{:S(2)}) collective-permute-start(bf16[288,512]{1,0:T(8,128)(2,1)S(1)} %get-tuple-element.180), channel_id=1, source_target_pairs={{0,2},{1,3},{2,0},{3,1},{4,6},{5,7},{6,4},{7,5},{8,10},{9,11},{10,... | collective-permute-start | bytes 884744 | tf_op jit(solution)/shard_map/ppermute | solution.py:299
  157.2 50.9 %collective-permute-start.6 = (bf16[288,512]{1,0:T(8,128)(2,1)S(1)}, bf16[288,512]{1,0:T(8,128)(2,1)S(1)}, u32[]{:S(2)}, u32[]{:S(2)}) collective-permute-start(bf16[288,512]{1,0:T(8,128)(2,1)S(1)} %get-tuple-element.181), channel_id=1, source_target_pairs={{0,1},{1,0},{2,3},{3,2},{4,5},{5,4},{6,7},{7,6},{8,9},{9,8},{10,11... | collective-permute-start | bytes 884744 | tf_op jit(solution)/shard_map/ppermute | solution.py:299
  205.1 14.4 %collective-permute-start.9 = (bf16[288,512]{1,0:T(8,128)(2,1)S(1)}, bf16[288,512]{1,0:T(8,128)(2,1)}, u32[]{:S(2)}, u32[]{:S(2)}) collective-permute-start(bf16[288,512]{1,0:T(8,128)(2,1)S(1)} %get-tuple-element.184), channel_id=1, source_target_pairs={{0,2},{1,3},{2,0},{3,1},{4,6},{5,7},{6,4},{7,5},{8,10},{9,11},{10,... | collective-permute-start | bytes 884744 | tf_op jit(solution)/shard_map/ppermute | solution.py:299
  205.4 14.2 %collective-permute-start.7 = (bf16[288,512]{1,0:T(8,128)(2,1)S(1)}, bf16[288,512]{1,0:T(8,128)(2,1)}, u32[]{:S(2)}, u32[]{:S(2)}) collective-permute-start(bf16[288,512]{1,0:T(8,128)(2,1)S(1)} %get-tuple-element.185), channel_id=1, source_target_pairs={{0,1},{1,0},{2,3},{3,2},{4,5},{5,4},{6,7},{7,6},{8,9},{9,8},{10,11... | collective-permute-start | bytes 884744 | tf_op jit(solution)/shard_map/ppermute | solution.py:299
  229.2 193.5 %reduce-scatter.7.cloned.1.call-start = ((), (), s32[]{:S(2)}) async-start(), calls=%async_computation.7 | async-start | bytes 11943936 | tf_op jit(solution)/shard_map/reduce_scatter | solution.py:420
  274.0 312.2 %reduce-scatter.9.cloned.1.call-start = ((), (), s32[]{:S(2)}) async-start(), calls=%async_computation.9 | async-start | bytes 11943936 | tf_op jit(solution)/shard_map/reduce_scatter | solution.py:442
  274.1 59.1 %collective-permute-start.13 = (bf16[1152,1152]{1,0:T(8,128)(2,1)}, bf16[1152,1152]{1,0:T(8,128)(2,1)S(1)}, u32[]{:S(2)}, u32[]{:S(2)}) collective-permute-start(bf16[1152,1152]{1,0:T(8,128)(2,1)} %all-gather.7.cloned.1.call-done), channel_id=1, source_target_pairs={{0,2},{1,3},{2,0},{3,1},{4,6},{5,7},{6,4},{7,5},{8,10},{9,11},{10,... | collective-permute-start | bytes 7962632 | tf_op jit(solution)/shard_map/ppermute | solution.py:299
  275.1 64.9 %collective-permute-start.12 = (bf16[1152,1152]{1,0:T(8,128)(2,1)}, bf16[1152,1152]{1,0:T(8,128)(2,1)S(1)}, u32[]{:S(2)}, u32[]{:S(2)}) collective-permute-start(bf16[1152,1152]{1,0:T(8,128)(2,1)} %all-gather.7.cloned.1.call-done), channel_id=1, source_target_pairs={{0,1},{1,0},{2,3},{3,2},{4,5},{5,4},{6,7},{7,6},{8,9},{9,8},{10,11... | collective-permute-start | bytes 7962632 | tf_op jit(solution)/shard_map/ppermute | solution.py:299
  384.6 38.1 %collective-permute-start.14 = (bf16[288,512]{1,0:T(8,128)(2,1)}, bf16[288,512]{1,0:T(8,128)(2,1)}, u32[]{:S(2)}, u32[]{:S(2)}) collective-permute-start(bf16[288,512]{1,0:T(8,128)(2,1)} %convolution_convert_fusion.9), channel_id=1, source_target_pairs={{0,1},{1,0},{2,3},{3,2},{4,5},{5,4},{6,7},{7,6},{8,9},{9,8},{10,11... | collective-permute-start | bytes 884744 | tf_op jit(solution)/shard_map/ppermute | solution.py:299
  386.8 35.9 %collective-permute-start.16 = (bf16[288,512]{1,0:T(8,128)(2,1)}, bf16[288,512]{1,0:T(8,128)(2,1)}, u32[]{:S(2)}, u32[]{:S(2)}) collective-permute-start(bf16[288,512]{1,0:T(8,128)(2,1)} %convolution_convert_fusion.7), channel_id=1, source_target_pairs={{0,3},{1,2},{2,1},{3,0},{4,7},{5,6},{6,5},{7,4},{8,11},{9,10},{10,... | collective-permute-start | bytes 884744 | tf_op jit(solution)/shard_map/ppermute | solution.py:299
  389.4 33.3 %collective-permute-start.15 = (bf16[288,512]{1,0:T(8,128)(2,1)}, bf16[288,512]{1,0:T(8,128)(2,1)}, u32[]{:S(2)}, u32[]{:S(2)}) collective-permute-start(bf16[288,512]{1,0:T(8,128)(2,1)} %convolution_convert_fusion.8), channel_id=1, source_target_pairs={{0,2},{1,3},{2,0},{3,1},{4,6},{5,7},{6,4},{7,5},{8,10},{9,11},{10,... | collective-permute-start | bytes 884744 | tf_op jit(solution)/shard_map/ppermute | solution.py:299
  422.8 216.9 %reduce-scatter.11.cloned.1.call-start = ((), (), s32[]{:S(2)}) async-start(), calls=%async_computation.10 | async-start | bytes 2985984 | tf_op jit(solution)/shard_map/reduce_scatter | solution.py:455
  439.6 89.3 %collective-permute-start.17 = (bf16[288,512]{1,0:T(8,128)(2,1)}, bf16[288,512]{1,0:T(8,128)(2,1)}, u32[]{:S(2)}, u32[]{:S(2)}) collective-permute-start(bf16[288,512]{1,0:T(8,128)(2,1)} %convolution_convert_fusion.5), channel_id=1, source_target_pairs={{0,1},{1,0},{2,3},{3,2},{4,5},{5,4},{6,7},{7,6},{8,9},{9,8},{10,11... | collective-permute-start | bytes 884744 | tf_op jit(solution)/shard_map/ppermute | solution.py:299
  443.0 87.0 %collective-permute-start.19 = (bf16[288,512]{1,0:T(8,128)(2,1)}, bf16[288,512]{1,0:T(8,128)(2,1)}, u32[]{:S(2)}, u32[]{:S(2)}) collective-permute-start(bf16[288,512]{1,0:T(8,128)(2,1)} %convolution_convert_fusion.3), channel_id=1, source_target_pairs={{0,3},{1,2},{2,1},{3,0},{4,7},{5,6},{6,5},{7,4},{8,11},{9,10},{10,... | collective-permute-start | bytes 884744 | tf_op jit(solution)/shard_map/ppermute | solution.py:299
  447.8 78.2 %collective-permute-start.38 = (bf16[144,1152]{1,0:T(8,128)(2,1)}, bf16[144,1152]{1,0:T(8,128)(2,1)S(1)}, u32[]{:S(2)}, u32[]{:S(2)}) collective-permute-start(bf16[144,1152]{1,0:T(8,128)(2,1)} %get-tuple-element.164), channel_id=1, source_target_pairs={{0,1},{1,0},{2,3},{3,2},{4,5},{5,4},{6,7},{7,6},{8,9},{9,8},{10,11... | collective-permute-start | bytes 995336 | tf_op jit(solution)/shard_map/ppermute | solution.py:299
  448.4 77.8 %collective-permute-start.40 = (bf16[144,1152]{1,0:T(8,128)(2,1)}, bf16[144,1152]{1,0:T(8,128)(2,1)S(1)}, u32[]{:S(2)}, u32[]{:S(2)}) collective-permute-start(bf16[144,1152]{1,0:T(8,128)(2,1)} %get-tuple-element.165), channel_id=1, source_target_pairs={{0,3},{1,2},{2,1},{3,0},{4,7},{5,6},{6,5},{7,4},{8,11},{9,10},{10,... | collective-permute-start | bytes 995336 | tf_op jit(solution)/shard_map/ppermute | solution.py:299
  449.4 77.7 %collective-permute-start.39 = (bf16[144,1152]{1,0:T(8,128)(2,1)S(1)}, bf16[144,1152]{1,0:T(8,128)(2,1)S(1)}, u32[]{:S(2)}, u32[]{:S(2)}) collective-permute-start(bf16[144,1152]{1,0:T(8,128)(2,1)S(1)} %get-tuple-element.166), channel_id=1, source_target_pairs={{0,2},{1,3},{2,0},{3,1},{4,6},{5,7},{6,4},{7,5},{8,10},{9,11},{10,... | collective-permute-start | bytes 995336 | tf_op jit(solution)/shard_map/ppermute | solution.py:299
  526.1 164.8 %collective-permute-start.20 = (bf16[512,1152]{1,0:T(8,128)(2,1)}, bf16[512,1152]{1,0:T(8,128)(2,1)}, u32[]{:S(2)}, u32[]{:S(2)}) collective-permute-start(bf16[512,1152]{1,0:T(8,128)(2,1)} %get-tuple-element.89), channel_id=1, source_target_pairs={{0,1},{1,0},{2,3},{3,2},{4,5},{5,4},{6,7},{7,6},{8,9},{9,8},{10,11... | collective-permute-start | bytes 3538952 | tf_op jit(solution)/shard_map/ppermute | solution.py:299
  527.1 164.4 %collective-permute-start.21 = (bf16[512,1152]{1,0:T(8,128)(2,1)}, bf16[512,1152]{1,0:T(8,128)(2,1)}, u32[]{:S(2)}, u32[]{:S(2)}) collective-permute-start(bf16[512,1152]{1,0:T(8,128)(2,1)} %get-tuple-element.90), channel_id=1, source_target_pairs={{0,2},{1,3},{2,0},{3,1},{4,6},{5,7},{6,4},{7,5},{8,10},{9,11},{10,... | collective-permute-start | bytes 3538952 | tf_op jit(solution)/shard_map/ppermute | solution.py:299
  529.0 57.3 %collective-permute-start.43 = (bf16[144,1152]{1,0:T(8,128)(2,1)S(1)}, bf16[144,1152]{1,0:T(8,128)(2,1)S(1)}, u32[]{:S(2)}, u32[]{:S(2)}) collective-permute-start(bf16[144,1152]{1,0:T(8,128)(2,1)S(1)} %add_convert_fusion.4), channel_id=1, source_target_pairs={{0,3},{1,2},{2,1},{3,0},{4,7},{5,6},{6,5},{7,4},{8,11},{9,10},{10,... | collective-permute-start | bytes 995336 | tf_op jit(solution)/shard_map/ppermute | solution.py:299
  530.0 56.3 %collective-permute-start.42 = (bf16[144,1152]{1,0:T(8,128)(2,1)S(1)}, bf16[144,1152]{1,0:T(8,128)(2,1)S(1)}, u32[]{:S(2)}, u32[]{:S(2)}) collective-permute-start(bf16[144,1152]{1,0:T(8,128)(2,1)S(1)} %add_convert_fusion.4), channel_id=1, source_target_pairs={{0,2},{1,3},{2,0},{3,1},{4,6},{5,7},{6,4},{7,5},{8,10},{9,11},{10,... | collective-permute-start | bytes 995336 | tf_op jit(solution)/shard_map/ppermute | solution.py:299
  534.3 52.0 %collective-permute-start.41 = (bf16[144,1152]{1,0:T(8,128)(2,1)S(1)}, bf16[144,1152]{1,0:T(8,128)(2,1)}, u32[]{:S(2)}, u32[]{:S(2)}) collective-permute-start(bf16[144,1152]{1,0:T(8,128)(2,1)S(1)} %add_convert_fusion.4), channel_id=1, source_target_pairs={{0,1},{1,0},{2,3},{3,2},{4,5},{5,4},{6,7},{7,6},{8,9},{9,8},{10,11... | collective-permute-start | bytes 995336 | tf_op jit(solution)/shard_map/ppermute | solution.py:299
  586.3 188.5 %reduce-scatter.13.cloned.1.call-start = ((), (), s32[]{:S(2)}) async-start(), calls=%async_computation.12 | async-start | bytes 2451456
  596.0 52.0 %collective-permute-start.24 = (bf16[512,1152]{1,0:T(8,128)(2,1)}, bf16[512,1152]{1,0:T(8,128)(2,1)S(1)}, u32[]{:S(2)}, u32[]{:S(2)}) collective-permute-start(bf16[512,1152]{1,0:T(8,128)(2,1)} %get-tuple-element.151), channel_id=1, source_target_pairs={{0,2},{1,3},{2,0},{3,1},{4,6},{5,7},{6,4},{7,5},{8,10},{9,11},{10,... | collective-permute-start | bytes 3538952 | tf_op jit(solution)/shard_map/ppermute | solution.py:299
  634.1 28.3 %collective-permute-start.23 = (bf16[512,1152]{1,0:T(8,128)(2,1)}, bf16[512,1152]{1,0:T(8,128)(2,1)}, u32[]{:S(2)}, u32[]{:S(2)}) collective-permute-start(bf16[512,1152]{1,0:T(8,128)(2,1)} %get-tuple-element.150), channel_id=1, source_target_pairs={{0,1},{1,0},{2,3},{3,2},{4,5},{5,4},{6,7},{7,6},{8,9},{9,8},{10,11... | collective-permute-start | bytes 3538952 | tf_op jit(solution)/shard_map/ppermute | solution.py:299
  634.6 53.9 %collective-permute-start.25 = (bf16[512,1152]{1,0:T(8,128)(2,1)}, bf16[512,1152]{1,0:T(8,128)(2,1)}, u32[]{:S(2)}, u32[]{:S(2)}) collective-permute-start(bf16[512,1152]{1,0:T(8,128)(2,1)} %get-tuple-element.152), channel_id=1, source_target_pairs={{0,3},{1,2},{2,1},{3,0},{4,7},{5,6},{6,5},{7,4},{8,11},{9,10},{10,... | collective-permute-start | bytes 3538952 | tf_op jit(solution)/shard_map/ppermute | solution.py:299
  648.0 65.9 %collective-permute-start.22 = (bf16[512,1152]{1,0:T(8,128)(2,1)S(1)}, bf16[512,1152]{1,0:T(8,128)(2,1)S(1)}, u32[]{:S(2)}, u32[]{:S(2)}) collective-permute-start(bf16[512,1152]{1,0:T(8,128)(2,1)S(1)} %copy-done.119), channel_id=1, source_target_pairs={{0,3},{1,2},{2,1},{3,0},{4,7},{5,6},{6,5},{7,4},{8,11},{9,10},{10,... | collective-permute-start | bytes 3538952 | tf_op jit(solution)/shard_map/ppermute | solution.py:299
  662.4 90.9 %collective-permute-start.31 = (bf16[144,1152]{1,0:T(8,128)(2,1)}, bf16[144,1152]{1,0:T(8,128)(2,1)}, u32[]{:S(2)}, u32[]{:S(2)}) collective-permute-start(bf16[144,1152]{1,0:T(8,128)(2,1)} %reduce-scatter.11.cloned.1.call-done), channel_id=1, source_target_pairs={{0,3},{1,2},{2,1},{3,0},{4,7},{5,6},{6,5},{7,4},{8,11},{9,10},{10,... | collective-permute-start | bytes 995336 | tf_op jit(solution)/shard_map/ppermute | solution.py:299
  688.5 65.4 %collective-permute-start.30 = (bf16[144,1152]{1,0:T(8,128)(2,1)}, bf16[144,1152]{1,0:T(8,128)(2,1)}, u32[]{:S(2)}, u32[]{:S(2)}) collective-permute-start(bf16[144,1152]{1,0:T(8,128)(2,1)} %reduce-scatter.11.cloned.1.call-done), channel_id=1, source_target_pairs={{0,2},{1,3},{2,0},{3,1},{4,6},{5,7},{6,4},{7,5},{8,10},{9,11},{10,... | collective-permute-start | bytes 995336 | tf_op jit(solution)/shard_map/ppermute | solution.py:299
  690.9 59.5 %collective-permute-start.32 = (bf16[144,1152]{1,0:T(8,128)(2,1)}, bf16[144,1152]{1,0:T(8,128)(2,1)S(1)}, u32[]{:S(2)}, u32[]{:S(2)}) collective-permute-start(bf16[144,1152]{1,0:T(8,128)(2,1)} %get-tuple-element.171), channel_id=1, source_target_pairs={{0,1},{1,0},{2,3},{3,2},{4,5},{5,4},{6,7},{7,6},{8,9},{9,8},{10,11... | collective-permute-start | bytes 995336 | tf_op jit(solution)/shard_map/ppermute | solution.py:299
  691.5 59.4 %collective-permute-start.34 = (bf16[144,1152]{1,0:T(8,128)(2,1)}, bf16[144,1152]{1,0:T(8,128)(2,1)S(1)}, u32[]{:S(2)}, u32[]{:S(2)}) collective-permute-start(bf16[144,1152]{1,0:T(8,128)(2,1)} %get-tuple-element.172), channel_id=1, source_target_pairs={{0,3},{1,2},{2,1},{3,0},{4,7},{5,6},{6,5},{7,4},{8,11},{9,10},{10,... | collective-permute-start | bytes 995336 | tf_op jit(solution)/shard_map/ppermute | solution.py:299
  713.9 37.0 %collective-permute-start.33 = (bf16[144,1152]{1,0:T(8,128)(2,1)}, bf16[144,1152]{1,0:T(8,128)(2,1)S(1)}, u32[]{:S(2)}, u32[]{:S(2)}) collective-permute-start(bf16[144,1152]{1,0:T(8,128)(2,1)} %get-tuple-element.173), channel_id=1, source_target_pairs={{0,2},{1,3},{2,0},{3,1},{4,6},{5,7},{6,4},{7,5},{8,10},{9,11},{10,... | collective-permute-start | bytes 995336 | tf_op jit(solution)/shard_map/ppermute | solution.py:299
  751.1 17.1 %collective-permute-start.37 = (bf16[144,1152]{1,0:T(8,128)(2,1)S(1)}, bf16[144,1152]{1,0:T(8,128)(2,1)S(1)}, u32[]{:S(2)}, u32[]{:S(2)}) collective-permute-start(bf16[144,1152]{1,0:T(8,128)(2,1)S(1)} %add_convert_fusion.5), channel_id=1, source_target_pairs={{0,3},{1,2},{2,1},{3,0},{4,7},{5,6},{6,5},{7,4},{8,11},{9,10},{10,... | collective-permute-start | bytes 995336 | tf_op jit(solution)/shard_map/ppermute | solution.py:299
  753.1 16.8 %collective-permute-start.36 = (bf16[144,1152]{1,0:T(8,128)(2,1)S(1)}, bf16[144,1152]{1,0:T(8,128)(2,1)S(1)}, u32[]{:S(2)}, u32[]{:S(2)}) collective-permute-start(bf16[144,1152]{1,0:T(8,128)(2,1)S(1)} %add_convert_fusion.5), channel_id=1, source_target_pairs={{0,2},{1,3},{2,0},{3,1},{4,6},{5,7},{6,4},{7,5},{8,10},{9,11},{10,... | collective-permute-start | bytes 995336 | tf_op jit(solution)/shard_map/ppermute | solution.py:299
  753.3 21.1 %collective-permute-start.35 = (bf16[144,1152]{1,0:T(8,128)(2,1)S(1)}, bf16[144,1152]{1,0:T(8,128)(2,1)S(1)}, u32[]{:S(2)}, u32[]{:S(2)}) collective-permute-start(bf16[144,1152]{1,0:T(8,128)(2,1)S(1)} %add_convert_fusion.5), channel_id=1, source_target_pairs={{0,1},{1,0},{2,3},{3,2},{4,5},{5,4},{6,7},{7,6},{8,9},{9,8},{10,11... | collective-permute-start | bytes 995336 | tf_op jit(solution)/shard_map/ppermute | solution.py:299
  776.1 14.1 %collective-permute-start.27 = (bf16[152,864]{1,0:T(8,128)(2,1)}, bf16[152,864]{1,0:T(8,128)(2,1)S(1)}, u32[]{:S(2)}, u32[]{:S(2)}) collective-permute-start(bf16[152,864]{1,0:T(8,128)(2,1)} %bitcast.231), channel_id=1, source_target_pairs={{0,2},{1,3},{2,0},{3,1},{4,6},{5,7},{6,4},{7,5},{8,10},{9,11},{10,... | collective-permute-start | bytes 787976 | tf_op jit(solution)/shard_map/ppermute | solution.py:299
  (142 other events, 1830.2 us)
Sparse Core Ops, SparseCore 0:
  15.9 31.2 all-gather.14
  49.5 32.9 all-gather.6
  84.1 33.0 all-gather.8
  119.3 97.2 all-gather.10
  229.3 35.6 all-gather.12
  274.2 111.1 reduce-scatter.6
  422.9 108.9 reduce-scatter.8
  586.4 30.8 reduce-scatter.10
  639.8 32.6 reduce-scatter.12

commit v5 on v4

--- a/solution.py
+++ b/solution.py
@@ -359,34 +359,34 @@
     down_turned = down_weight.T
     down_own = near_slabs(down_turned, [0])
     output_whole = lax.all_gather(output_weight, "rows", axis=0, tiled=True)
-    up_whole = near_slabs(up_weight, range(seq_count))
+    halves = [range(seq_count // 2), range(seq_count // 2, seq_count)]
+    ups = [near_slabs(up_weight, hops) for hops in halves]
     late = [hop for hop in rest if hop not in direct]
-    held = lax.optimization_barrier((down_own, *whole_rows[-1][1:]))
-    down_own, whole_rows[-1][1:] = held[0], list(held[1:])
-    downs = [down_own] + [swap(down_own, hop) for hop in direct]
-    if late:
-        down_turned, up_whole = lax.optimization_barrier((down_turned, up_whole))
-        down_late = near_slabs(down_turned, late)
-        downs += [down_late[:, i * slab : (i + 1) * slab] for i in range(len(late))]
+    down_turned, ups[1] = lax.optimization_barrier((down_turned, ups[1]))
+    down_late = near_slabs(down_turned, late) if late else None
     up_off = jnp.concatenate(up_off)
     outputs = relative(output_whole.reshape(seq_count, part, width))
 
-    attn_inputs, packs, mixes, logs, tables, mixed_own = [], [], [], [], [], []
+    normed_rows, packs, mixes, logs, tables, mixed_own = [], [], [], [], [], []
     for row in range(count):
         ids = picture_ids[row]
         low, high = block_ranges(ids, block)
         ids_table = (jnp.broadcast_to(ids[:, None], (length, 128)), jnp.broadcast_to(ids[None], (8, length)))
         tables.append((low, high, *ids_table))
-        attn_input = jnp.concatenate(
-            [(norm_parts(piece.astype(f32))[0] * gain1 + shift1).astype(bf16) for piece in whole_rows[row]], axis=0
-        )
+        normed_pieces = [norm_parts(piece.astype(f32))[0] for piece in whole_rows[row]]
+        attn_input = jnp.concatenate([(piece * gain1 + shift1).astype(bf16) for piece in normed_pieces], axis=0)
+        normed_rows.append(jnp.concatenate([piece.astype(bf16) for piece in normed_pieces], axis=0))
         pack = (contract(heads_weight, attn_input, 0, 1) + heads_off[:, None]).astype(bf16).reshape(3, part, length)
         mixed, logsum = attend(pack, *tables[row], place_array, chunk)
-        attn_inputs.append(attn_input)
         packs.append(pack)
         mixes.append(mixed)
         logs.append(logsum)
         mixed_own.append([mixed[0]] + [swap(mixed[hop], hop) for hop in rest])
+
+    held = lax.optimization_barrier((down_own, *mixed_own[-1][1:]))
+    down_own, mixed_own[-1][1:] = held[0], list(held[1:])
+    downs = [down_own] + [swap(down_own, hop) for hop in direct]
+    downs += [down_late[:, i * slab : (i + 1) * slab] for i in range(len(late))]
 
     mixed_all = jnp.concatenate(
         [jnp.concatenate([mixed_own[row][hop] for row in range(count)], axis=1) for hop in range(seq_count)], axis=0
@@ -396,10 +396,12 @@
     resid = tokens_own + (contract(mixed_all, output_near, 0, 0) + output_off)
     normed2, inverse2 = norm_parts(resid)
     mlp_input = (normed2 * gain2 + shift2).astype(bf16)
-    total = None
-    hidden = contract(mlp_input, up_whole, 1, 0) + up_off
-    gelu_out, slope = gelu_parts(hidden)
-    gelu_out, slope = gelu_out.astype(bf16), slope.astype(bf16)
+    parts = []
+    for hops, weight in zip(halves, ups):
+        offset = up_off[hops[0] * slab : (hops[-1] + 1) * slab]
+        parts.append([v.astype(bf16) for v in gelu_parts(contract(mlp_input, weight, 1, 0) + offset)])
+    gelu_out = jnp.concatenate([pair[0] for pair in parts], axis=1)
+    slope = jnp.concatenate([pair[1] for pair in parts], axis=1)
 
     def slab_of(value, hop):
         return value[:, hop * slab : (hop + 1) * slab]
@@ -418,10 +420,13 @@
     grad_down = with_layout_constraint(contract(cot, gelu_out, 0, 0).astype(bf16), Layout(major_to_minor=(0, 1)))
     cot, grad_down = lax.optimization_barrier((cot, grad_down))
     down_raw = lax.psum_scatter(grad_down, "rows", scatter_dimension=0, tiled=True)
-    grad_hidden = jnp.concatenate(
-        [(contract(cot, downs[hop], 1, 0) * slab_of(slope, hop).astype(f32)).astype(bf16) for hop in range(seq_count)], axis=1
-    )
-    grad_mlp_input = contract(grad_hidden, up_whole, 1, 1)
+    grad_pieces = [(contract(cot, downs[hop], 1, 0) * slab_of(slope, hop).astype(f32)).astype(bf16) for hop in range(seq_count)]
+    up_grads = jnp.stack(relative(jnp.stack([jnp.sum(piece.astype(f32), axis=0) for piece in grad_pieces])))
+    grad_hidden = jnp.concatenate(grad_pieces, axis=1)
+    grad_mlp_input = None
+    for hops, weight in zip(halves, ups):
+        term = contract(grad_hidden[:, hops[0] * slab : (hops[-1] + 1) * slab], weight, 1, 1)
+        grad_mlp_input = term if grad_mlp_input is None else grad_mlp_input + term
     grad_up = contract(mlp_input, grad_hidden, 0, 0).astype(bf16)
     grad_resid = cot.astype(f32) + norm_back(grad_mlp_input, normed2, inverse2, gain2)
     grad_attn = grad_resid.astype(bf16)
@@ -442,47 +447,48 @@
     up_raw = lax.psum_scatter(grad_up, "rows", scatter_dimension=0, tiled=True)
     down_share = exchange_sum([slab_of(down_raw, hop) for hop in range(seq_count)]).astype(bf16)
     down_pieces = all_pieces(down_share)
-    heads_grad, query_grad, value_grad, gain_grad, shift_grad, grad_in = None, 0.0, 0.0, 0.0, 0.0, []
-    after = None
-    for row in range(count):
-        grad_mixed = mixed_grads[row]
-        pack = packs[row]
-        if after is not None:
-            pack, grad_in[-1] = lax.optimization_barrier((pack, grad_in[-1]))
-        grad_pack = attend_back(pack, grad_mixed, mixes[row], logs[row], *tables[row], place_array)
-        if row == count - 1:
-            grad_pack, up_raw, grad_output = lax.optimization_barrier((grad_pack, up_raw, grad_output))
-            output_share = lax.psum_scatter(grad_output, "rows", scatter_dimension=0, tiled=True)
-        query_grad = query_grad + jnp.sum(grad_pack[0].astype(f32), axis=1)
-        value_grad = value_grad + jnp.sum(grad_pack[2].astype(f32), axis=1)
-        grad_pack = grad_pack.reshape(3 * part, length)
-        partial = []
-        for hop in range(seq_count):
-            piece = contract(grad_pack[:, hop * chunk : (hop + 1) * chunk], heads_weight, 0, 1)
-            gain_grad = gain_grad + jnp.sum(piece * norm_parts(whole_rows[row][hop].astype(f32))[0], axis=0)
-            shift_grad = shift_grad + jnp.sum(piece, axis=0)
-            partial.append(piece.astype(bf16))
-        grad_in.append(partial)
-        after = partial
-        term = contract(attn_inputs[row], grad_pack, 0, 1)
-        heads_grad = term if heads_grad is None else heads_grad + term
-
-    def placed(value):
-        return lax.dynamic_update_slice_in_dim(jnp.zeros((width,), f32), value, place * part, axis=0)
-
-    up_grads = jnp.stack(relative(jnp.sum(grad_hidden.astype(f32), axis=0).reshape(seq_count, slab)))
-    small_grads = [
-        gain_grad,
-        shift_grad,
-        placed(query_grad),
-        placed(value_grad),
+    normed_grad, sum_grad, grad_in = None, 0.0, []
+    early_grads = [
         jnp.sum(grad_attn.astype(f32), axis=0),
         jnp.sum(grad_mlp_input * normed2, axis=0),
         jnp.sum(grad_mlp_input, axis=0),
         jnp.sum(cot.astype(f32), axis=0),
         up_grads.reshape(slab * seq_count)[:hidden_size],
     ]
-    together = jnp.concatenate([value.reshape(row_count, -1) for value in small_grads], axis=1).astype(bf16)
+    early_grads = jnp.concatenate([value.reshape(row_count, -1) for value in early_grads], axis=1)
+    after = None
+    for row in range(count):
+        grad_mixed = mixed_grads[row]
+        pack = packs[row]
+        if after is not None:
+            pack, grad_in[-1], early_grads = lax.optimization_barrier((pack, grad_in[-1], early_grads))
+        grad_pack = attend_back(pack, grad_mixed, mixes[row], logs[row], *tables[row], place_array)
+        if row == count - 1:
+            grad_pack, up_raw, grad_output = lax.optimization_barrier((grad_pack, up_raw, grad_output))
+            output_share = lax.psum_scatter(grad_output, "rows", scatter_dimension=0, tiled=True)
+        grad_pack = grad_pack.reshape(3 * part, length)
+        sum_grad = sum_grad + jnp.sum(grad_pack.astype(f32), axis=1)
+        partial = []
+        for hop in range(seq_count):
+            piece = contract(grad_pack[:, hop * chunk : (hop + 1) * chunk], heads_weight, 0, 1)
+            partial.append(piece.astype(bf16))
+        grad_in.append(partial)
+        after = partial
+        term = with_layout_constraint(contract(normed_rows[row], grad_pack, 0, 1), Layout(major_to_minor=(0, 1)))
+        normed_grad = term if normed_grad is None else normed_grad + term
+
+    def placed(value):
+        return lax.dynamic_update_slice_in_dim(jnp.zeros((width,), f32), value, place * part, axis=0)
+
+    wide_weight = heads_weight.astype(f32)
+    heads_grad = gain1[:, None] * normed_grad + shift1[:, None] * sum_grad
+    late_grads = [
+        jnp.sum(wide_weight * normed_grad, axis=1),
+        jnp.sum(wide_weight * sum_grad, axis=1),
+        placed(sum_grad[:part]),
+        placed(sum_grad[2 * part :]),
+    ]
+    together = jnp.concatenate([value.reshape(row_count, -1) for value in late_grads] + [early_grads], axis=1).astype(bf16)
     heads_grad = beside(heads_grad.astype(bf16).reshape(row_count, band_width, 3 * part), together)
     held = lax.optimization_barrier((heads_grad, output_share, *[pieces[0] for pieces in grad_in]))
     heads_grad, output_share = held[:2]

time: 814 us -> 819 us (level)
  the two profiles are of different devices: /device:TPU:9 before, /device:TPU:8 now
where the time goes in v5:
time: 819 us; the launch traced here: 811 us
  waiting for transfers between devices  244 us (30%)
  matrix products  238 us (29%)
  Pallas kernels  137 us (17%)
  other arithmetic  81.6 us (10%)
  starting transfers between devices  50.2 us (6%)
  local copies, waits for them, and re-layouts  43.9 us (5%)
  between operations  16.1 us (2%)
    ppermute x44, waiting for transfers between devices, swap(): return lax.ppermute(value, 'seq', [(i, i ^ hop) for i in range(seq_count)])  243 us
    dot_general x36, matrix products, contract(): lax.dot_general(left, right, (((left_axis,), (right_axis,)), ((), ())), p...  238 us
    pallas_call x2, Pallas kernels, attend_back(): pl.pallas_call(functools.partial(attend_back_kernel, count=count, block=b...  92.9 us
    ppermute x44, starting transfers between devices, swap(): return lax.ppermute(value, 'seq', [(i, i ^ hop) for i in range(seq_count)])  49.8 us
    pallas_call x2, Pallas kernels, attend(): pl.pallas_call(functools.partial(attend_kernel, count=count, block=block,...  44 us
    convert_element_type x6, other arithmetic, per_device(): piece.astype(bf16)  17.5 us
  transfers between devices with their start and end apart: 54, of which 17 were waited for; matrix products, arithmetic and copies ran while one was open for 42% of the time, Pallas kernels for 17%

profile of v5, /device:TPU:8, one launch (start us, length us, event | category | flops | bytes accessed | tf_op | source)
XLA Modules:
  0.0 810.7 jit_solution(9064766796939054627)
XLA Ops:
  7.3 6.2 concatenate.103
  28.0 22.7 %collective-permute-done = bf16[512,1152]{1,0:T(8,128)(2,1)} collective-permute-done((bf16[512,1152]{1,0:T(8,128)(2,1)}, bf16[512,1152]{1,0:T(8,128)(2,1)}, u32[]{:S(2)}, u32[]{:S(2)}) %collective-permute-start) | collective-permute-done | bytes 1179680 | tf_op jit(solution)/shard_map/ppermute | solution.py:299
  50.7 25.4 %collective-permute-done.1 = bf16[512,1152]{1,0:T(8,128)(2,1)} collective-permute-done((bf16[512,1152]{1,0:T(8,128)(2,1)}, bf16[512,1152]{1,0:T(8,128)(2,1)}, u32[]{:S(2)}, u32[]{:S(2)}) %collective-permute-start.1) | collective-permute-done | bytes 1179680 | tf_op jit(solution)/shard_map/ppermute | solution.py:299
  88.3 17.7 %collective-permute-done.5 = bf16[512,1152]{1,0:T(8,128)(2,1)S(1)} collective-permute-done((bf16[512,1152]{1,0:T(8,128)(2,1)}, bf16[512,1152]{1,0:T(8,128)(2,1)S(1)}, u32[]{:S(2)}, u32[]{:S(2)}) %collective-permute-start.5) | collective-permute-done | bytes 1179680 | tf_op jit(solution)/shard_map/ppermute | solution.py:299
  106.2 22.9 %collective-permute-done.4 = bf16[512,1152]{1,0:T(8,128)(2,1)S(1)} collective-permute-done((bf16[512,1152]{1,0:T(8,128)(2,1)}, bf16[512,1152]{1,0:T(8,128)(2,1)S(1)}, u32[]{:S(2)}, u32[]{:S(2)}) %collective-permute-start.4) | collective-permute-done | bytes 1179680 | tf_op jit(solution)/shard_map/ppermute | solution.py:299
  144.6 4.3 fusion.100
  148.9 7.9 add_convert_fusion.2
  157.2 20.7 %attend.3 = (bf16[4,288,512]{2,1,0:T(8,128)(2,1)S(1)}, f32[8,2048]{1,0:T(8,128)S(1)}) custom-call(s32[8]{0:T(128)S(1)} %get-tuple-element.116.low_ref, s32[8]{0:T(128)S(1)} %get-tuple-element.115.high_ref, s32[1]{0:T(128)} %bitcast.3.place_ref, bf16[3,288,2048]{2,1,0:T(8,128)(2,1)S(1)} %bitcast.180, s32[2048,128]{1,0:T(8,128)S(1)} %broadcast_in_dim.25.kid_ref, ...), custom_call_target="tpu_custom_call" | custom-call | flops 6710886400 | bytes 4718592 | tf_op jit(solution)/shard_map/attend/pallas_call | solution.py:102
  188.3 7.9 add_convert_fusion.3
  196.6 23.3 %attend.2 = (bf16[4,288,512]{2,1,0:T(8,128)(2,1)S(1)}, f32[8,2048]{1,0:T(8,128)S(1)}) custom-call(s32[8]{0:T(128)S(1)} %get-tuple-element.246.low_ref, s32[8]{0:T(128)S(1)} %get-tuple-element.247.high_ref, s32[1]{0:T(128)} %bitcast.3.place_ref, bf16[3,288,2048]{2,1,0:T(8,128)(2,1)S(1)} %bitcast.182, s32[2048,128]{1,0:T(8,128)S(1)} %broadcast_in_dim.22.kid_ref, ...), custom_call_target="tpu_custom_call" | custom-call | flops 6710886400 | bytes 4718592 | tf_op jit(solution)/shard_map/attend/pallas_call | solution.py:102
  228.0 3.6 collective-permute-done.11
  231.6 7.9 collective-permute-done.10
  239.5 5.6 fusion.192
  248.9 16.0 %add_convert_fusion = (bf16[1024,2304]{1,0:T(8,128)(2,1)}, bf16[1024,2304]{1,0:T(8,128)(2,1)}) fusion(f32[2304]{0:T(1024)S(1)} %pad_maximum_fusion.19, bf16[1152,2304]{1,0:T(8,128)(2,1)} %all-gather.14.cloned.1.call-done, f32[1024,1152]{1,0:T(8,128)} %copy-done.22, f32[1152]{0:T(1024)S(1)} %add.430, f32[1152]{0:T(1024)S(1)} %mul.396, ...), kind=kOutput, calls=%fused_computation.11 | convolution fusion | flops 5481824256 | bytes 19490816 | tf_op jit(solution)/shard_map/dot_general | solution.py:278
  264.9 16.0 %add_convert_fusion.1 = (bf16[1024,2304]{1,0:T(8,128)(2,1)}, bf16[1024,2304]{1,0:T(8,128)(2,1)}) fusion(f32[2304]{0:T(1024)S(1)} %pad_maximum_fusion.18, bf16[1152,2304]{1,0:T(8,128)(2,1)} %all-gather.12.cloned.1.call-done, f32[1024,1152]{1,0:T(8,128)} %copy-done.22, f32[1152]{0:T(1024)S(1)} %add.430, f32[1152]{0:T(1024)S(1)} %mul.396, ...), kind=kOutput, calls=%fused_computation.12 | convolution fusion | flops 5481824256 | bytes 19490816 | tf_op jit(solution)/shard_map/dot_general | solution.py:278
  280.9 17.9 %fusion = bf16[1152,4608]{1,0:T(8,128)(2,1)} fusion(bf16[1024,1152]{1,0:T(8,128)(2,1)} %bitcast.209, bf16[1024,2304]{1,0:T(8,128)(2,1)S(1)} %copy-done.29, bf16[1024,2304]{1,0:T(8,128)(2,1)} %get-tuple-element.121), kind=kOutput, calls=%fused_computation.2 | convolution fusion | flops 10895818752 | bytes 22413312 | tf_op jit(solution)/shard_map/dot_general | solution.py:278
  301.1 6.2 convert_reduce_fusion.7
  307.3 51.3 %collective-permute-done.12 = bf16[1152,1152]{1,0:T(8,128)(2,1)S(1)} collective-permute-done((bf16[1152,1152]{1,0:T(8,128)(2,1)}, bf16[1152,1152]{1,0:T(8,128)(2,1)S(1)}, u32[]{:S(2)}, u32[]{:S(2)}) %collective-permute-start.12) | collective-permute-done | bytes 2654240 | tf_op jit(solution)/shard_map/ppermute | solution.py:299
  358.7 6.1 convert_reduce_fusion.6
  364.9 4.8 convert_reduce_fusion.5
  369.8 8.0 fusion.36
  377.7 7.1 convert_reduce_fusion.4
  384.8 12.0 %multiply_reduce_fusion = (bf16[1152]{0:T(1024)(128)(2,1)S(1)}, f32[1024]{0:T(1024)S(1)}, f32[1024]{0:T(1024)S(1)}, bf16[1152]{0:T(1024)(128)(2,1)S(1)}, f32[1024,1152]{1,0:T(8,128)S(1)}) fusion(f32[1024,1152]{1,0:T(8,128)} %copy-done.22, f32[1024]{0:T(1024)S(1)} %add_rsqrt_fusion.1, f32[1024]{0:T(1024)S(1)} %broadcast_multiply_fusion.4, ...), kind=kOutput, calls=%fused_computation.90 | convolution fusion | flops 5457047552 | bytes 24208384 | tf_op jit(solution)/shard_map/dot_general | solution.py:278
  396.9 4.1 convert_reduce_fusion.8
  408.5 4.5 convolution_convert_fusion.2
  413.3 19.4 %convolution_convert_fusion = bf16[1152,4608]{1,0:T(8,128)(2,1)} fusion(bf16[1024,1152]{1,0:T(8,128)(2,1)} %get-tuple-element.239, bf16[1024,1152]{1,0:T(8,128)(2,1)} %get-tuple-element.241, bf16[1024,1152]{1,0:T(8,128)(2,1)} %copy-done.79, bf16[1024,1152]{1,0:T(8,128)(2,1)} %copy-done.78, f32[1024,1152]{1,0:T(8,128)} %copy-done.22, f32[1152]{0:T(1024)S(1)} %add.430, ...), kind=kOutput, calls=%fused_computation | convolution fusion | flops 10920591360 | bytes 24790016 | tf_op jit(solution)/shard_map/dot_general | solution.py:278
  432.7 6.2 pad_maximum_fusion.2
  444.8 9.1 %pad_maximum_fusion = bf16[1024,4608]{1,0:T(8,128)(2,1)} fusion(bf16[1024,2304]{1,0:T(8,128)(2,1)} %get-tuple-element.123, bf16[1024,2304]{1,0:T(8,128)(2,1)} %get-tuple-element.121), kind=kLoop, calls=%fused_computation.3 | loop fusion | flops 18874368 | bytes 18874368 | tf_op jit(solution)/shard_map/concatenate | solution.py:403
  470.6 48.8 %attend_back.2 = bf16[3,288,2048]{2,1,0:T(8,128)(2,1)} custom-call(s32[8]{0:T(128)} %copy-done.10, s32[8]{0:T(128)} %copy-done.11, s32[1]{0:T(128)} %bitcast.3.place_ref, bf16[3,288,2048]{2,1,0:T(8,128)(2,1)} %bitcast.183, bf16[4,288,512]{2,1,0:T(8,128)(2,1)} %copy-done.3, f32[8,2048]{1,0:T(8,128)} %copy-done.15, s32[2048,128]{1,0:T(8,128)} %copy-done.5, ...), custom_call_target="tpu_custom_call" | custom-call | flops 16777216000 | bytes 9437184 | tf_op jit(solution)/shard_map/attend_back/pallas_call | solution.py:215
  519.4 4.6 convolution_convert_fusion.10
  529.4 7.1 fusion.28
  546.5 3.6 collective-permute-done.19.rest_3_
  551.1 44.1 %attend_back.3 = bf16[3,288,2048]{2,1,0:T(8,128)(2,1)} custom-call(s32[8]{0:T(128)} %copy-done.9, s32[8]{0:T(128)} %copy-done.8, s32[1]{0:T(128)} %bitcast.3.place_ref, bf16[3,288,2048]{2,1,0:T(8,128)(2,1)} %bitcast.181, bf16[4,288,512]{2,1,0:T(8,128)(2,1)} %copy-done.2, f32[8,2048]{1,0:T(8,128)} %copy-done.14, s32[2048,128]{1,0:T(8,128)} %copy-done.4, ...), custom_call_target="tpu_custom_call" | custom-call | flops 16777216000 | bytes 9437184 | tf_op jit(solution)/shard_map/attend_back/pallas_call | solution.py:215
  597.9 15.0 %collective-permute-done.42 = bf16[144,1152]{1,0:T(8,128)(2,1)S(1)} collective-permute-done((bf16[144,1152]{1,0:T(8,128)(2,1)S(1)}, bf16[144,1152]{1,0:T(8,128)(2,1)S(1)}, u32[]{:S(2)}, u32[]{:S(2)}) %collective-permute-start.42) | collective-permute-done | bytes 331808 | tf_op jit(solution)/shard_map/ppermute | solution.py:299
  617.9 12.1 %add_convert_fusion.5 = (bf16[1152,864]{1,0:T(8,128)(2,1)}, bf16[1152]{0:T(1024)(128)(2,1)S(1)}) fusion(f32[864]{0:T(1024)S(1)} %add.452, f32[1152]{0:T(1024)S(1)} %copy-done.61, f32[1152]{0:T(1024)S(1)} %copy-done.50, bf16[8,144,864]{2,1,0:T(8,128)(2,1)} %slice.367, f32[1152,864]{1,0:T(8,128)} %fusion.28, bf16[864,2048]{1,0:T(8,128)(2,1)} %bitcast.197, ...), kind=kOutput, calls=%fused_computation.102 | convolution fusion | flops 4103699456 | bytes 16235136 | tf_op jit(solution)/shard_map/dot_general | solution.py:278
  633.6 4.6 convolution_convert_fusion.3
  648.5 4.4 convolution_convert_fusion.6
  653.0 15.3 %collective-permute-done.25 = bf16[512,1152]{1,0:T(8,128)(2,1)} collective-permute-done((bf16[512,1152]{1,0:T(8,128)(2,1)}, bf16[512,1152]{1,0:T(8,128)(2,1)}, u32[]{:S(2)}, u32[]{:S(2)}) %collective-permute-start.25) | collective-permute-done | bytes 1179680 | tf_op jit(solution)/shard_map/ppermute | solution.py:299
  668.8 8.2 %fusion.147 = f32[1024,1152]{1,0:T(8,128)} fusion(bf16[1152,1152]{1,0:T(8,128)(2,1)} %all-gather.8.cloned.1.call-done, bf16[1024,4608]{1,0:T(8,128)(2,1)} %pad_maximum_fusion), kind=kOutput, calls=%fused_computation.205 | convolution fusion | flops 2717908992 | bytes 9732096 | tf_op jit(solution)/shard_map/dot_general | solution.py:278
  677.0 15.8 %collective-permute-done.24 = bf16[512,1152]{1,0:T(8,128)(2,1)} collective-permute-done((bf16[512,1152]{1,0:T(8,128)(2,1)}, bf16[512,1152]{1,0:T(8,128)(2,1)}, u32[]{:S(2)}, u32[]{:S(2)}) %collective-permute-start.24) | collective-permute-done | bytes 1179680 | tf_op jit(solution)/shard_map/ppermute | solution.py:299
  697.4 20.8 %collective-permute-done.20 = bf16[512,1152]{1,0:T(8,128)(2,1)S(1)} collective-permute-done((bf16[512,1152]{1,0:T(8,128)(2,1)}, bf16[512,1152]{1,0:T(8,128)(2,1)S(1)}, u32[]{:S(2)}, u32[]{:S(2)}) %collective-permute-start.20) | collective-permute-done | bytes 1179680 | tf_op jit(solution)/shard_map/ppermute | solution.py:299
  728.0 8.3 %fusion.139 = f32[1024,1152]{1,0:T(8,128)} fusion(bf16[1152,1152]{1,0:T(8,128)(2,1)} %all-gather.16.cloned.1.call-done, bf16[1024,4608]{1,0:T(8,128)(2,1)} %pad_maximum_fusion), kind=kOutput, calls=%fused_computation.199 | convolution fusion | flops 2717908992 | bytes 9732096 | tf_op jit(solution)/shard_map/dot_general | solution.py:278
  736.3 7.5 fusion.145
  743.9 12.8 %add_add_fusion = f32[1024,1152]{1,0:T(8,128)} fusion(f32[1024,1152]{1,0:T(8,128)} %fusion.139, f32[1024,1152]{1,0:T(8,128)} %fusion.145, f32[1024,1152]{1,0:T(8,128)S(1)} %bitcast.188, f32[1024,1152]{1,0:T(8,128)} %fusion.147, f32[1152]{0:T(1024)S(1)} %add.458, bf16[1152,1152]{1,0:T(8,128)(2,1)} %copy-done.72, bf16[1024,4608]{1,0:T(8,128)(2,1)} %pad_maximum_fusion), kind=kOutput, calls=%fused_computation.85 | convolution fusion | flops 2723807232 | bytes 28611072 | tf_op jit(solution)/shard_map/dot_general | solution.py:278
  756.7 3.8 fusion.61
  766.7 4.6 collective-permute-done.29
  773.3 5.8 collective-permute-done.37
  787.9 4.5 collective-permute-done.28
  (462 shorter events, 178.1 us)
Async XLA Ops:
  7.2 124.6 %all-gather.18.cloned.1.call-start = ((), (), s32[]{:S(2)}) async-start(), calls=%async_computation.12 | async-start | bytes 2451456 | tf_op jit(solution)/shard_map/all_gather | solution.py:333
  15.7 210.3 %all-gather.8.cloned.1.call-start = ((), (), s32[]{:S(2)}) async-start(), calls=%async_computation.4 | async-start | bytes 2985984 | tf_op jit(solution)/shard_map/all_gather | solution.py:356
  16.6 209.4 %all-gather.10.cloned.1.call-start = ((), (), s32[]{:S(2)}) async-start(), calls=%async_computation.5 | async-start | bytes 2985984 | tf_op jit(solution)/shard_map/all_gather | solution.py:361
  17.4 230.6 %all-gather.14.cloned.1.call-start = ((), (), s32[]{:S(2)}) async-start(), calls=%async_computation.7 | async-start | bytes 5971968 | tf_op jit(solution)/shard_map/all_gather | solution.py:356
  19.9 245.0 %all-gather.12.cloned.1.call-start = ((), (), s32[]{:S(2)}) async-start(), calls=%async_computation.6 | async-start | bytes 5971968 | tf_op jit(solution)/shard_map/all_gather | solution.py:356
  21.5 29.2 %collective-permute-start = (bf16[512,1152]{1,0:T(8,128)(2,1)}, bf16[512,1152]{1,0:T(8,128)(2,1)}, u32[]{:S(2)}, u32[]{:S(2)}) collective-permute-start(bf16[512,1152]{1,0:T(8,128)(2,1)} %get-tuple-element.141), channel_id=1, source_target_pairs={{0,1},{1,0},{2,3},{3,2},{4,5},{5,4},{6,7},{7,6},{8,9},{9,8},{10,11... | collective-permute-start | bytes 3538952 | tf_op jit(solution)/shard_map/ppermute | solution.py:299
  23.0 53.0 %collective-permute-start.1 = (bf16[512,1152]{1,0:T(8,128)(2,1)}, bf16[512,1152]{1,0:T(8,128)(2,1)}, u32[]{:S(2)}, u32[]{:S(2)}) collective-permute-start(bf16[512,1152]{1,0:T(8,128)(2,1)} %get-tuple-element.141), channel_id=1, source_target_pairs={{0,2},{1,3},{2,0},{3,1},{4,6},{5,7},{6,4},{7,5},{8,10},{9,11},{10,... | collective-permute-start | bytes 3538952 | tf_op jit(solution)/shard_map/ppermute | solution.py:299
  24.6 51.5 %collective-permute-start.2 = (bf16[512,1152]{1,0:T(8,128)(2,1)}, bf16[512,1152]{1,0:T(8,128)(2,1)}, u32[]{:S(2)}, u32[]{:S(2)}) collective-permute-start(bf16[512,1152]{1,0:T(8,128)(2,1)} %get-tuple-element.141), channel_id=1, source_target_pairs={{0,3},{1,2},{2,1},{3,0},{4,7},{5,6},{6,5},{7,4},{8,11},{9,10},{10,... | collective-permute-start | bytes 3538952 | tf_op jit(solution)/shard_map/ppermute | solution.py:299
  25.9 351.8 %all-gather.16.cloned.1.call-start = ((), (), s32[]{:S(2)}) async-start(), calls=%async_computation.9 | async-start | bytes 2985984 | tf_op jit(solution)/shard_map/all_gather | solution.py:356
  76.1 29.9 %collective-permute-start.5 = (bf16[512,1152]{1,0:T(8,128)(2,1)}, bf16[512,1152]{1,0:T(8,128)(2,1)S(1)}, u32[]{:S(2)}, u32[]{:S(2)}) collective-permute-start(bf16[512,1152]{1,0:T(8,128)(2,1)} %get-tuple-element.62), channel_id=1, source_target_pairs={{0,3},{1,2},{2,1},{3,0},{4,7},{5,6},{6,5},{7,4},{8,11},{9,10},{10,... | collective-permute-start | bytes 3538952 | tf_op jit(solution)/shard_map/ppermute | solution.py:299
  77.6 51.5 %collective-permute-start.4 = (bf16[512,1152]{1,0:T(8,128)(2,1)}, bf16[512,1152]{1,0:T(8,128)(2,1)S(1)}, u32[]{:S(2)}, u32[]{:S(2)}) collective-permute-start(bf16[512,1152]{1,0:T(8,128)(2,1)} %get-tuple-element.62), channel_id=1, source_target_pairs={{0,2},{1,3},{2,0},{3,1},{4,6},{5,7},{6,4},{7,5},{8,10},{9,11},{10,... | collective-permute-start | bytes 3538952 | tf_op jit(solution)/shard_map/ppermute | solution.py:299
  78.8 51.5 %collective-permute-start.3 = (bf16[512,1152]{1,0:T(8,128)(2,1)}, bf16[512,1152]{1,0:T(8,128)(2,1)S(1)}, u32[]{:S(2)}, u32[]{:S(2)}) collective-permute-start(bf16[512,1152]{1,0:T(8,128)(2,1)} %get-tuple-element.62), channel_id=1, source_target_pairs={{0,1},{1,0},{2,3},{3,2},{4,5},{5,4},{6,7},{7,6},{8,9},{9,8},{10,11... | collective-permute-start | bytes 3538952 | tf_op jit(solution)/shard_map/ppermute | solution.py:299
  179.0 45.8 %collective-permute-start.7 = (bf16[288,512]{1,0:T(8,128)(2,1)}, bf16[288,512]{1,0:T(8,128)(2,1)}, u32[]{:S(2)}, u32[]{:S(2)}) collective-permute-start(bf16[288,512]{1,0:T(8,128)(2,1)} %get-tuple-element.180), channel_id=1, source_target_pairs={{0,1},{1,0},{2,3},{3,2},{4,5},{5,4},{6,7},{7,6},{8,9},{9,8},{10,11... | collective-permute-start | bytes 884744 | tf_op jit(solution)/shard_map/ppermute | solution.py:299
  179.9 46.2 %collective-permute-start.8 = (bf16[288,512]{1,0:T(8,128)(2,1)}, bf16[288,512]{1,0:T(8,128)(2,1)}, u32[]{:S(2)}, u32[]{:S(2)}) collective-permute-start(bf16[288,512]{1,0:T(8,128)(2,1)} %get-tuple-element.179), channel_id=1, source_target_pairs={{0,2},{1,3},{2,0},{3,1},{4,6},{5,7},{6,4},{7,5},{8,10},{9,11},{10,... | collective-permute-start | bytes 884744 | tf_op jit(solution)/shard_map/ppermute | solution.py:299
  181.0 45.1 %collective-permute-start.9 = (bf16[288,512]{1,0:T(8,128)(2,1)}, bf16[288,512]{1,0:T(8,128)(2,1)}, u32[]{:S(2)}, u32[]{:S(2)}) collective-permute-start(bf16[288,512]{1,0:T(8,128)(2,1)} %get-tuple-element.178), channel_id=1, source_target_pairs={{0,3},{1,2},{2,1},{3,0},{4,7},{5,6},{6,5},{7,4},{8,11},{9,10},{10,... | collective-permute-start | bytes 884744 | tf_op jit(solution)/shard_map/ppermute | solution.py:299
  223.8 15.8 %collective-permute-start.10 = (bf16[288,512]{1,0:T(8,128)(2,1)}, bf16[288,512]{1,0:T(8,128)(2,1)}, u32[]{:S(2)}, u32[]{:S(2)}) collective-permute-start(bf16[288,512]{1,0:T(8,128)(2,1)} %get-tuple-element.175), channel_id=1, source_target_pairs={{0,2},{1,3},{2,0},{3,1},{4,6},{5,7},{6,4},{7,5},{8,10},{9,11},{10,... | collective-permute-start | bytes 884744 | tf_op jit(solution)/shard_map/ppermute | solution.py:299
  224.8 14.7 %collective-permute-start.6 = (bf16[288,512]{1,0:T(8,128)(2,1)}, bf16[288,512]{1,0:T(8,128)(2,1)S(1)}, u32[]{:S(2)}, u32[]{:S(2)}) collective-permute-start(bf16[288,512]{1,0:T(8,128)(2,1)} %get-tuple-element.176), channel_id=1, source_target_pairs={{0,1},{1,0},{2,3},{3,2},{4,5},{5,4},{6,7},{7,6},{8,9},{9,8},{10,11... | collective-permute-start | bytes 884744 | tf_op jit(solution)/shard_map/ppermute | solution.py:299
  248.8 192.9 %reduce-scatter.7.cloned.1.call-start = ((), (), s32[]{:S(2)}) async-start(), calls=%async_computation.8 | async-start | bytes 11943936 | tf_op jit(solution)/shard_map/reduce_scatter | solution.py:422
  298.8 299.0 %reduce-scatter.9.cloned.1.call-start = ((), (), s32[]{:S(2)}) async-start(), calls=%async_computation.10 | async-start | bytes 11943936 | tf_op jit(solution)/shard_map/reduce_scatter | solution.py:447
  298.8 59.8 %collective-permute-start.12 = (bf16[1152,1152]{1,0:T(8,128)(2,1)}, bf16[1152,1152]{1,0:T(8,128)(2,1)S(1)}, u32[]{:S(2)}, u32[]{:S(2)}) collective-permute-start(bf16[1152,1152]{1,0:T(8,128)(2,1)} %all-gather.8.cloned.1.call-done), channel_id=1, source_target_pairs={{0,1},{1,0},{2,3},{3,2},{4,5},{5,4},{6,7},{7,6},{8,9},{9,8},{10,11... | collective-permute-start | bytes 7962632 | tf_op jit(solution)/shard_map/ppermute | solution.py:299
  299.9 65.0 %collective-permute-start.13 = (bf16[1152,1152]{1,0:T(8,128)(2,1)}, bf16[1152,1152]{1,0:T(8,128)(2,1)S(1)}, u32[]{:S(2)}, u32[]{:S(2)}) collective-permute-start(bf16[1152,1152]{1,0:T(8,128)(2,1)} %all-gather.8.cloned.1.call-done), channel_id=1, source_target_pairs={{0,2},{1,3},{2,0},{3,1},{4,6},{5,7},{6,4},{7,5},{8,10},{9,11},{10,... | collective-permute-start | bytes 7962632 | tf_op jit(solution)/shard_map/ppermute | solution.py:299
  402.4 39.3 %collective-permute-start.14 = (bf16[288,512]{1,0:T(8,128)(2,1)}, bf16[288,512]{1,0:T(8,128)(2,1)S(1)}, u32[]{:S(2)}, u32[]{:S(2)}) collective-permute-start(bf16[288,512]{1,0:T(8,128)(2,1)} %convolution_convert_fusion.17), channel_id=1, source_target_pairs={{0,1},{1,0},{2,3},{3,2},{4,5},{5,4},{6,7},{7,6},{8,9},{9,8},{10,11... | collective-permute-start | bytes 884744 | tf_op jit(solution)/shard_map/ppermute | solution.py:299
  404.6 37.1 %collective-permute-start.15 = (bf16[288,512]{1,0:T(8,128)(2,1)}, bf16[288,512]{1,0:T(8,128)(2,1)}, u32[]{:S(2)}, u32[]{:S(2)}) collective-permute-start(bf16[288,512]{1,0:T(8,128)(2,1)} %convolution_convert_fusion.16), channel_id=1, source_target_pairs={{0,2},{1,3},{2,0},{3,1},{4,6},{5,7},{6,4},{7,5},{8,10},{9,11},{10,... | collective-permute-start | bytes 884744 | tf_op jit(solution)/shard_map/ppermute | solution.py:299
  407.1 34.6 %collective-permute-start.16 = (bf16[288,512]{1,0:T(8,128)(2,1)}, bf16[288,512]{1,0:T(8,128)(2,1)}, u32[]{:S(2)}, u32[]{:S(2)}) collective-permute-start(bf16[288,512]{1,0:T(8,128)(2,1)} %convolution_convert_fusion.15), channel_id=1, source_target_pairs={{0,3},{1,2},{2,1},{3,0},{4,7},{5,6},{6,5},{7,4},{8,11},{9,10},{10,... | collective-permute-start | bytes 884744 | tf_op jit(solution)/shard_map/ppermute | solution.py:299
  442.4 210.5 %reduce-scatter.11.cloned.1.call-start = ((), (), s32[]{:S(2)}) async-start(), calls=%async_computation.11 | async-start | bytes 2985984 | tf_op jit(solution)/shard_map/reduce_scatter | solution.py:468
  457.3 86.5 %collective-permute-start.17 = (bf16[288,512]{1,0:T(8,128)(2,1)}, bf16[288,512]{1,0:T(8,128)(2,1)}, u32[]{:S(2)}, u32[]{:S(2)}) collective-permute-start(bf16[288,512]{1,0:T(8,128)(2,1)} %convolution_convert_fusion.13), channel_id=1, source_target_pairs={{0,1},{1,0},{2,3},{3,2},{4,5},{5,4},{6,7},{7,6},{8,9},{9,8},{10,11... | collective-permute-start | bytes 884744 | tf_op jit(solution)/shard_map/ppermute | solution.py:299
  460.6 84.5 %collective-permute-start.18 = (bf16[288,512]{1,0:T(8,128)(2,1)}, bf16[288,512]{1,0:T(8,128)(2,1)}, u32[]{:S(2)}, u32[]{:S(2)}) collective-permute-start(bf16[288,512]{1,0:T(8,128)(2,1)} %convolution_convert_fusion.12), channel_id=1, source_target_pairs={{0,2},{1,3},{2,0},{3,1},{4,6},{5,7},{6,4},{7,5},{8,10},{9,11},{10,... | collective-permute-start | bytes 884744 | tf_op jit(solution)/shard_map/ppermute | solution.py:299
  467.1 72.1 %collective-permute-start.40 = (bf16[144,1152]{1,0:T(8,128)(2,1)}, bf16[144,1152]{1,0:T(8,128)(2,1)S(1)}, u32[]{:S(2)}, u32[]{:S(2)}) collective-permute-start(bf16[144,1152]{1,0:T(8,128)(2,1)} %get-tuple-element.148), channel_id=1, source_target_pairs={{0,3},{1,2},{2,1},{3,0},{4,7},{5,6},{6,5},{7,4},{8,11},{9,10},{10,... | collective-permute-start | bytes 995336 | tf_op jit(solution)/shard_map/ppermute | solution.py:299
  468.5 71.9 %collective-permute-start.39 = (bf16[144,1152]{1,0:T(8,128)(2,1)}, bf16[144,1152]{1,0:T(8,128)(2,1)S(1)}, u32[]{:S(2)}, u32[]{:S(2)}) collective-permute-start(bf16[144,1152]{1,0:T(8,128)(2,1)} %get-tuple-element.149), channel_id=1, source_target_pairs={{0,2},{1,3},{2,0},{3,1},{4,6},{5,7},{6,4},{7,5},{8,10},{9,11},{10,... | collective-permute-start | bytes 995336 | tf_op jit(solution)/shard_map/ppermute | solution.py:299
  469.1 73.0 %collective-permute-start.38 = (bf16[144,1152]{1,0:T(8,128)(2,1)S(1)}, bf16[144,1152]{1,0:T(8,128)(2,1)S(1)}, u32[]{:S(2)}, u32[]{:S(2)}) collective-permute-start(bf16[144,1152]{1,0:T(8,128)(2,1)S(1)} %get-tuple-element.147), channel_id=1, source_target_pairs={{0,1},{1,0},{2,3},{3,2},{4,5},{5,4},{6,7},{7,6},{8,9},{9,8},{10,11... | collective-permute-start | bytes 995336 | tf_op jit(solution)/shard_map/ppermute | solution.py:299
  540.3 157.0 %collective-permute-start.22 = (bf16[512,1152]{1,0:T(8,128)(2,1)}, bf16[512,1152]{1,0:T(8,128)(2,1)}, u32[]{:S(2)}, u32[]{:S(2)}) collective-permute-start(bf16[512,1152]{1,0:T(8,128)(2,1)} %convolution_convert_fusion.7), channel_id=1, source_target_pairs={{0,3},{1,2},{2,1},{3,0},{4,7},{5,6},{6,5},{7,4},{8,11},{9,10},{10,... | collective-permute-start | bytes 3538952 | tf_op jit(solution)/shard_map/ppermute | solution.py:299
  542.1 155.2 %collective-permute-start.21 = (bf16[512,1152]{1,0:T(8,128)(2,1)}, bf16[512,1152]{1,0:T(8,128)(2,1)}, u32[]{:S(2)}, u32[]{:S(2)}) collective-permute-start(bf16[512,1152]{1,0:T(8,128)(2,1)} %convolution_convert_fusion.8), channel_id=1, source_target_pairs={{0,2},{1,3},{2,0},{3,1},{4,6},{5,7},{6,4},{7,5},{8,10},{9,11},{10,... | collective-permute-start | bytes 3538952 | tf_op jit(solution)/shard_map/ppermute | solution.py:299
  543.8 54.0 %collective-permute-start.43 = (bf16[144,1152]{1,0:T(8,128)(2,1)S(1)}, bf16[144,1152]{1,0:T(8,128)(2,1)S(1)}, u32[]{:S(2)}, u32[]{:S(2)}) collective-permute-start(bf16[144,1152]{1,0:T(8,128)(2,1)S(1)} %add_convert_fusion.6), channel_id=1, source_target_pairs={{0,3},{1,2},{2,1},{3,0},{4,7},{5,6},{6,5},{7,4},{8,11},{9,10},{10,... | collective-permute-start | bytes 995336 | tf_op jit(solution)/shard_map/ppermute | solution.py:299
  545.1 67.8 %collective-permute-start.42 = (bf16[144,1152]{1,0:T(8,128)(2,1)S(1)}, bf16[144,1152]{1,0:T(8,128)(2,1)S(1)}, u32[]{:S(2)}, u32[]{:S(2)}) collective-permute-start(bf16[144,1152]{1,0:T(8,128)(2,1)S(1)} %add_convert_fusion.6), channel_id=1, source_target_pairs={{0,2},{1,3},{2,0},{3,1},{4,6},{5,7},{6,4},{7,5},{8,10},{9,11},{10,... | collective-permute-start | bytes 995336 | tf_op jit(solution)/shard_map/ppermute | solution.py:299
  550.8 62.1 %collective-permute-start.41 = (bf16[144,1152]{1,0:T(8,128)(2,1)S(1)}, bf16[144,1152]{1,0:T(8,128)(2,1)}, u32[]{:S(2)}, u32[]{:S(2)}) collective-permute-start(bf16[144,1152]{1,0:T(8,128)(2,1)S(1)} %add_convert_fusion.6), channel_id=1, source_target_pairs={{0,1},{1,0},{2,3},{3,2},{4,5},{5,4},{6,7},{7,6},{8,9},{9,8},{10,11... | collective-permute-start | bytes 995336 | tf_op jit(solution)/shard_map/ppermute | solution.py:299
  597.8 184.9 %reduce-scatter.13.cloned.1.call-start = ((), (), s32[]{:S(2)}) async-start(), calls=%async_computation.13 | async-start | bytes 2451456
  638.2 30.1 %collective-permute-start.25 = (bf16[512,1152]{1,0:T(8,128)(2,1)}, bf16[512,1152]{1,0:T(8,128)(2,1)}, u32[]{:S(2)}, u32[]{:S(2)}) collective-permute-start(bf16[512,1152]{1,0:T(8,128)(2,1)} %convolution_convert_fusion.3), channel_id=1, source_target_pairs={{0,3},{1,2},{2,1},{3,0},{4,7},{5,6},{6,5},{7,4},{8,11},{9,10},{10,... | collective-permute-start | bytes 3538952 | tf_op jit(solution)/shard_map/ppermute | solution.py:299
  642.4 50.3 %collective-permute-start.24 = (bf16[512,1152]{1,0:T(8,128)(2,1)}, bf16[512,1152]{1,0:T(8,128)(2,1)}, u32[]{:S(2)}, u32[]{:S(2)}) collective-permute-start(bf16[512,1152]{1,0:T(8,128)(2,1)} %convolution_convert_fusion.4), channel_id=1, source_target_pairs={{0,2},{1,3},{2,0},{3,1},{4,6},{5,7},{6,4},{7,5},{8,10},{9,11},{10,... | collective-permute-start | bytes 3538952 | tf_op jit(solution)/shard_map/ppermute | solution.py:299
  645.5 48.9 %collective-permute-start.23 = (bf16[512,1152]{1,0:T(8,128)(2,1)}, bf16[512,1152]{1,0:T(8,128)(2,1)}, u32[]{:S(2)}, u32[]{:S(2)}) collective-permute-start(bf16[512,1152]{1,0:T(8,128)(2,1)} %convolution_convert_fusion.5), channel_id=1, source_target_pairs={{0,1},{1,0},{2,3},{3,2},{4,5},{5,4},{6,7},{7,6},{8,9},{9,8},{10,11... | collective-permute-start | bytes 3538952 | tf_op jit(solution)/shard_map/ppermute | solution.py:299
  668.3 49.9 %collective-permute-start.20 = (bf16[512,1152]{1,0:T(8,128)(2,1)}, bf16[512,1152]{1,0:T(8,128)(2,1)S(1)}, u32[]{:S(2)}, u32[]{:S(2)}) collective-permute-start(bf16[512,1152]{1,0:T(8,128)(2,1)} %convolution_convert_fusion.9), channel_id=1, source_target_pairs={{0,1},{1,0},{2,3},{3,2},{4,5},{5,4},{6,7},{7,6},{8,9},{9,8},{10,11... | collective-permute-start | bytes 3538952 | tf_op jit(solution)/shard_map/ppermute | solution.py:299
  692.7 72.6 %collective-permute-start.31 = (bf16[144,1152]{1,0:T(8,128)(2,1)S(1)}, bf16[144,1152]{1,0:T(8,128)(2,1)S(1)}, u32[]{:S(2)}, u32[]{:S(2)}) collective-permute-start(bf16[144,1152]{1,0:T(8,128)(2,1)S(1)} %copy-done.62), channel_id=1, source_target_pairs={{0,3},{1,2},{2,1},{3,0},{4,7},{5,6},{6,5},{7,4},{8,11},{9,10},{10,... | collective-permute-start | bytes 995336 | tf_op jit(solution)/shard_map/ppermute | solution.py:299
  694.3 72.3 %collective-permute-start.30 = (bf16[144,1152]{1,0:T(8,128)(2,1)S(1)}, bf16[144,1152]{1,0:T(8,128)(2,1)}, u32[]{:S(2)}, u32[]{:S(2)}) collective-permute-start(bf16[144,1152]{1,0:T(8,128)(2,1)S(1)} %copy-done.62), channel_id=1, source_target_pairs={{0,2},{1,3},{2,0},{3,1},{4,6},{5,7},{6,4},{7,5},{8,10},{9,11},{10,... | collective-permute-start | bytes 995336 | tf_op jit(solution)/shard_map/ppermute | solution.py:299
  724.4 36.1 %collective-permute-start.34 = (bf16[144,1152]{1,0:T(8,128)(2,1)S(1)}, bf16[144,1152]{1,0:T(8,128)(2,1)S(1)}, u32[]{:S(2)}, u32[]{:S(2)}) collective-permute-start(bf16[144,1152]{1,0:T(8,128)(2,1)S(1)} %get-tuple-element.155), channel_id=1, source_target_pairs={{0,3},{1,2},{2,1},{3,0},{4,7},{5,6},{6,5},{7,4},{8,11},{9,10},{10,... | collective-permute-start | bytes 995336 | tf_op jit(solution)/shard_map/ppermute | solution.py:299
  725.5 36.4 %collective-permute-start.33 = (bf16[144,1152]{1,0:T(8,128)(2,1)S(1)}, bf16[144,1152]{1,0:T(8,128)(2,1)S(1)}, u32[]{:S(2)}, u32[]{:S(2)}) collective-permute-start(bf16[144,1152]{1,0:T(8,128)(2,1)S(1)} %get-tuple-element.156), channel_id=1, source_target_pairs={{0,2},{1,3},{2,0},{3,1},{4,6},{5,7},{6,4},{7,5},{8,10},{9,11},{10,... | collective-permute-start | bytes 995336 | tf_op jit(solution)/shard_map/ppermute | solution.py:299
  727.2 34.7 %collective-permute-start.32 = (bf16[144,1152]{1,0:T(8,128)(2,1)S(1)}, bf16[144,1152]{1,0:T(8,128)(2,1)S(1)}, u32[]{:S(2)}, u32[]{:S(2)}) collective-permute-start(bf16[144,1152]{1,0:T(8,128)(2,1)S(1)} %get-tuple-element.154), channel_id=1, source_target_pairs={{0,1},{1,0},{2,3},{3,2},{4,5},{5,4},{6,7},{7,6},{8,9},{9,8},{10,11... | collective-permute-start | bytes 995336 | tf_op jit(solution)/shard_map/ppermute | solution.py:299
  763.1 15.9 %collective-permute-start.37 = (bf16[144,1152]{1,0:T(8,128)(2,1)S(1)}, bf16[144,1152]{1,0:T(8,128)(2,1)S(1)}, u32[]{:S(2)}, u32[]{:S(2)}) collective-permute-start(bf16[144,1152]{1,0:T(8,128)(2,1)S(1)} %add_convert_fusion.7), channel_id=1, source_target_pairs={{0,3},{1,2},{2,1},{3,0},{4,7},{5,6},{6,5},{7,4},{8,11},{9,10},{10,... | collective-permute-start | bytes 995336 | tf_op jit(solution)/shard_map/ppermute | solution.py:299
  764.5 14.5 %collective-permute-start.36 = (bf16[144,1152]{1,0:T(8,128)(2,1)S(1)}, bf16[144,1152]{1,0:T(8,128)(2,1)S(1)}, u32[]{:S(2)}, u32[]{:S(2)}) collective-permute-start(bf16[144,1152]{1,0:T(8,128)(2,1)S(1)} %add_convert_fusion.7), channel_id=1, source_target_pairs={{0,2},{1,3},{2,0},{3,1},{4,6},{5,7},{6,4},{7,5},{8,10},{9,11},{10,... | collective-permute-start | bytes 995336 | tf_op jit(solution)/shard_map/ppermute | solution.py:299
  765.3 17.0 %collective-permute-start.35 = (bf16[144,1152]{1,0:T(8,128)(2,1)S(1)}, bf16[144,1152]{1,0:T(8,128)(2,1)S(1)}, u32[]{:S(2)}, u32[]{:S(2)}) collective-permute-start(bf16[144,1152]{1,0:T(8,128)(2,1)S(1)} %add_convert_fusion.7), channel_id=1, source_target_pairs={{0,1},{1,0},{2,3},{3,2},{4,5},{5,4},{6,7},{7,6},{8,9},{9,8},{10,11... | collective-permute-start | bytes 995336 | tf_op jit(solution)/shard_map/ppermute | solution.py:299
  (97 other events, 1761.2 us)
Sparse Core Ops, SparseCore 0:
  15.8 30.9 all-gather.17
  49.0 32.9 all-gather.7
  83.6 33.0 all-gather.9
  118.8 54.4 all-gather.13
  175.4 55.2 all-gather.11
  248.9 34.5 all-gather.15
  298.9 108.8 reduce-scatter.6
  441.9 106.0 reduce-scatter.8
  597.9 32.9 reduce-scatter.10
  723.3 34.1 reduce-scatter.12

commit v6 on v5

--- a/solution.py
+++ b/solution.py
@@ -447,7 +447,7 @@
     up_raw = lax.psum_scatter(grad_up, "rows", scatter_dimension=0, tiled=True)
     down_share = exchange_sum([slab_of(down_raw, hop) for hop in range(seq_count)]).astype(bf16)
     down_pieces = all_pieces(down_share)
-    normed_grad, sum_grad, grad_in = None, 0.0, []
+    normed_grad, sum_grad, grad_in, grad_packs = None, 0.0, [], []
     early_grads = [
         jnp.sum(grad_attn.astype(f32), axis=0),
         jnp.sum(grad_mlp_input * normed2, axis=0),
@@ -474,7 +474,12 @@
             partial.append(piece.astype(bf16))
         grad_in.append(partial)
         after = partial
-        term = with_layout_constraint(contract(normed_rows[row], grad_pack, 0, 1), Layout(major_to_minor=(0, 1)))
+        grad_packs.append(grad_pack)
+
+    held = lax.optimization_barrier((*grad_packs, *grad_in[-1]))
+    grad_packs, grad_in[-1] = held[:count], list(held[count:])
+    for row in range(count):
+        term = with_layout_constraint(contract(normed_rows[row], grad_packs[row], 0, 1), Layout(major_to_minor=(0, 1)))
         normed_grad = term if normed_grad is None else normed_grad + term
 
     def placed(value):
@@ -494,12 +499,15 @@
     heads_grad, output_share = held[:2]
     for row in range(count):
         grad_in[row][0] = held[2 + row]
-    gelu_late, output_share, up_raw, heads_grad = lax.optimization_barrier((gelu_out, output_share, up_raw, heads_grad))
+    held = lax.optimization_barrier((gelu_out, output_share, up_raw, heads_grad, *down_pieces))
+    gelu_late, output_share, up_raw, heads_grad = held[:4]
+    down_pieces = held[4:]
     total = resid
     for hop in range(seq_count):
         total = total + contract(slab_of(gelu_late, hop), downs[hop], 1, 1)
     activations = total + down_off
     up_share = exchange_sum([slab_of(up_raw, hop) for hop in range(seq_count)]).astype(bf16)
+    up_pieces = all_pieces(up_share)
 
     heads_share = lax.psum_scatter(heads_grad, "rows", scatter_dimension=0, tiled=False)
     normed1, inverse1 = norm_parts(tokens_own)
@@ -539,7 +547,7 @@
         vectors[4],
         vectors[5],
         vectors[6],
-        slabs(all_pieces(up_share)),
+        slabs(up_pieces),
         vectors[8],
         slabs(down_pieces).T,
         vectors[7],

time: 819 us -> 803 us (0.980)
  waiting for transfers between devices: 244 us -> 230 us
    ppermute x44, waiting for transfers between devices: 243 us -> 229 us  [swap(): return lax.ppermute(value, 'seq', [(i, i ^ hop) for i in range(seq_count)])]
    dot_general x36, matrix products: 238 us -> 230 us  [contract(): lax.dot_general(left, right, (((left_axis,), (right_axis,)), ((), ())), p...]
where the time goes in v6:
time: 803 us; the launch traced here: 795 us
  waiting for transfers between devices  230 us (29%)
  matrix products  230 us (29%)
  Pallas kernels  137 us (17%)
  other arithmetic  86.9 us (11%)
  starting transfers between devices  50.3 us (6%)
  local copies, waits for them, and re-layouts  44.5 us (6%)
  between operations  16.1 us (2%)
    dot_general x36, matrix products, contract(): lax.dot_general(left, right, (((left_axis,), (right_axis,)), ((), ())), p...  230 us
    ppermute x44, waiting for transfers between devices, swap(): return lax.ppermute(value, 'seq', [(i, i ^ hop) for i in range(seq_count)])  229 us
    pallas_call x2, Pallas kernels, attend_back(): pl.pallas_call(functools.partial(attend_back_kernel, count=count, block=b...  93 us
    ppermute x44, starting transfers between devices, swap(): return lax.ppermute(value, 'seq', [(i, i ^ hop) for i in range(seq_count)])  49.9 us
    pallas_call x2, Pallas kernels, attend(): pl.pallas_call(functools.partial(attend_kernel, count=count, block=block,...  44 us
    convert_element_type x6, other arithmetic, per_device(): piece.astype(bf16)  17.5 us
  transfers between devices with their start and end apart: 54, of which 17 were waited for; matrix products, arithmetic and copies ran while one was open for 42% of the time, Pallas kernels for 17%

profile of v6, /device:TPU:8, one launch (start us, length us, event | category | flops | bytes accessed | tf_op | source)
XLA Modules:
  0.0 795.0 jit_solution(16545771292303807494)
XLA Ops:
  7.3 6.2 concatenate.103
  28.0 22.7 %collective-permute-done = bf16[512,1152]{1,0:T(8,128)(2,1)} collective-permute-done((bf16[512,1152]{1,0:T(8,128)(2,1)}, bf16[512,1152]{1,0:T(8,128)(2,1)}, u32[]{:S(2)}, u32[]{:S(2)}) %collective-permute-start) | collective-permute-done | bytes 1179680 | tf_op jit(solution)/shard_map/ppermute | solution.py:299
  50.7 25.4 %collective-permute-done.1 = bf16[512,1152]{1,0:T(8,128)(2,1)} collective-permute-done((bf16[512,1152]{1,0:T(8,128)(2,1)}, bf16[512,1152]{1,0:T(8,128)(2,1)}, u32[]{:S(2)}, u32[]{:S(2)}) %collective-permute-start.1) | collective-permute-done | bytes 1179680 | tf_op jit(solution)/shard_map/ppermute | solution.py:299
  88.3 17.7 %collective-permute-done.5 = bf16[512,1152]{1,0:T(8,128)(2,1)S(1)} collective-permute-done((bf16[512,1152]{1,0:T(8,128)(2,1)}, bf16[512,1152]{1,0:T(8,128)(2,1)S(1)}, u32[]{:S(2)}, u32[]{:S(2)}) %collective-permute-start.5) | collective-permute-done | bytes 1179680 | tf_op jit(solution)/shard_map/ppermute | solution.py:299
  106.2 22.9 %collective-permute-done.4 = bf16[512,1152]{1,0:T(8,128)(2,1)S(1)} collective-permute-done((bf16[512,1152]{1,0:T(8,128)(2,1)}, bf16[512,1152]{1,0:T(8,128)(2,1)S(1)}, u32[]{:S(2)}, u32[]{:S(2)}) %collective-permute-start.4) | collective-permute-done | bytes 1179680 | tf_op jit(solution)/shard_map/ppermute | solution.py:299
  144.6 4.3 fusion.100
  148.9 7.9 add_convert_fusion.2
  157.2 20.7 %attend.3 = (bf16[4,288,512]{2,1,0:T(8,128)(2,1)S(1)}, f32[8,2048]{1,0:T(8,128)S(1)}) custom-call(s32[8]{0:T(128)S(1)} %get-tuple-element.136.low_ref, s32[8]{0:T(128)S(1)} %get-tuple-element.135.high_ref, s32[1]{0:T(128)} %bitcast.3.place_ref, bf16[3,288,2048]{2,1,0:T(8,128)(2,1)S(1)} %bitcast.180, s32[2048,128]{1,0:T(8,128)S(1)} %broadcast_in_dim.25.kid_ref, ...), custom_call_target="tpu_custom_call" | custom-call | flops 6710886400 | bytes 4718592 | tf_op jit(solution)/shard_map/attend/pallas_call | solution.py:102
  188.3 7.9 add_convert_fusion.3
  196.6 23.3 %attend.2 = (bf16[4,288,512]{2,1,0:T(8,128)(2,1)S(1)}, f32[8,2048]{1,0:T(8,128)S(1)}) custom-call(s32[8]{0:T(128)S(1)} %get-tuple-element.266.low_ref, s32[8]{0:T(128)S(1)} %get-tuple-element.267.high_ref, s32[1]{0:T(128)} %bitcast.3.place_ref, bf16[3,288,2048]{2,1,0:T(8,128)(2,1)S(1)} %bitcast.182, s32[2048,128]{1,0:T(8,128)S(1)} %broadcast_in_dim.22.kid_ref, ...), custom_call_target="tpu_custom_call" | custom-call | flops 6710886400 | bytes 4718592 | tf_op jit(solution)/shard_map/attend/pallas_call | solution.py:102
  228.0 3.6 collective-permute-done.11
  231.6 7.9 collective-permute-done.10
  239.5 5.6 fusion.192
  248.8 16.0 %add_convert_fusion = (bf16[1024,2304]{1,0:T(8,128)(2,1)}, bf16[1024,2304]{1,0:T(8,128)(2,1)}) fusion(f32[2304]{0:T(1024)S(1)} %pad_maximum_fusion.19, bf16[1152,2304]{1,0:T(8,128)(2,1)} %all-gather.14.cloned.1.call-done, f32[1024,1152]{1,0:T(8,128)} %copy-done.20, f32[1152]{0:T(1024)S(1)} %add.430, f32[1152]{0:T(1024)S(1)} %mul.396, ...), kind=kOutput, calls=%fused_computation.11 | convolution fusion | flops 5481824256 | bytes 19490816 | tf_op jit(solution)/shard_map/dot_general | solution.py:278
  264.8 15.9 %add_convert_fusion.1 = (bf16[1024,2304]{1,0:T(8,128)(2,1)}, bf16[1024,2304]{1,0:T(8,128)(2,1)}) fusion(f32[2304]{0:T(1024)S(1)} %pad_maximum_fusion.18, bf16[1152,2304]{1,0:T(8,128)(2,1)} %all-gather.12.cloned.1.call-done, f32[1024,1152]{1,0:T(8,128)} %copy-done.20, f32[1152]{0:T(1024)S(1)} %add.430, f32[1152]{0:T(1024)S(1)} %mul.396, ...), kind=kOutput, calls=%fused_computation.12 | convolution fusion | flops 5481824256 | bytes 19490816 | tf_op jit(solution)/shard_map/dot_general | solution.py:278
  280.8 17.9 %fusion = bf16[1152,4608]{1,0:T(8,128)(2,1)} fusion(bf16[1024,1152]{1,0:T(8,128)(2,1)} %bitcast.209, bf16[1024,2304]{1,0:T(8,128)(2,1)S(1)} %copy-done.27, bf16[1024,2304]{1,0:T(8,128)(2,1)} %get-tuple-element.141), kind=kOutput, calls=%fused_computation.2 | convolution fusion | flops 10895818752 | bytes 22413312 | tf_op jit(solution)/shard_map/dot_general | solution.py:278
  301.0 6.2 convert_reduce_fusion.7
  307.2 51.4 %collective-permute-done.12 = bf16[1152,1152]{1,0:T(8,128)(2,1)S(1)} collective-permute-done((bf16[1152,1152]{1,0:T(8,128)(2,1)}, bf16[1152,1152]{1,0:T(8,128)(2,1)S(1)}, u32[]{:S(2)}, u32[]{:S(2)}) %collective-permute-start.12) | collective-permute-done | bytes 2654240 | tf_op jit(solution)/shard_map/ppermute | solution.py:299
  358.6 6.1 convert_reduce_fusion.6
  364.8 4.8 convert_reduce_fusion.5
  369.7 8.0 %fusion.36 = f32[1024,1152]{1,0:T(8,128)} fusion(bf16[1152,2304]{1,0:T(8,128)(2,1)S(1)} %bitcast.249, bf16[1024,1152]{1,0:T(8,128)(2,1)S(1)} %get-tuple-element.263, bf16[1024,1152]{1,0:T(8,128)(2,1)S(1)} %get-tuple-element.265), kind=kOutput, calls=%fused_computation.54 | convolution fusion | flops 5445255168 | bytes 14745600 | tf_op jit(solution)/shard_map/dot_general | solution.py:278
  377.7 7.1 convert_reduce_fusion.4
  384.7 12.0 %multiply_reduce_fusion = (bf16[1152]{0:T(1024)(128)(2,1)S(1)}, f32[1024]{0:T(1024)S(1)}, f32[1024]{0:T(1024)S(1)}, bf16[1152]{0:T(1024)(128)(2,1)S(1)}, f32[1024,1152]{1,0:T(8,128)S(1)}) fusion(f32[1024,1152]{1,0:T(8,128)} %copy-done.20, f32[1024]{0:T(1024)S(1)} %add_rsqrt_fusion.1, f32[1024]{0:T(1024)S(1)} %broadcast_multiply_fusion.4, ...), kind=kOutput, calls=%fused_computation.90 | convolution fusion | flops 5457047552 | bytes 24208384 | tf_op jit(solution)/shard_map/dot_general | solution.py:278
  396.8 4.2 convert_reduce_fusion.8
  408.5 4.5 convolution_convert_fusion.2
  413.3 19.4 %convolution_convert_fusion = bf16[1152,4608]{1,0:T(8,128)(2,1)} fusion(bf16[1024,1152]{1,0:T(8,128)(2,1)} %get-tuple-element.259, bf16[1024,1152]{1,0:T(8,128)(2,1)} %get-tuple-element.261, bf16[1024,1152]{1,0:T(8,128)(2,1)} %copy-done.81, bf16[1024,1152]{1,0:T(8,128)(2,1)} %copy-done.80, f32[1024,1152]{1,0:T(8,128)} %copy-done.20, f32[1152]{0:T(1024)S(1)} %add.430, ...), kind=kOutput, calls=%fused_computation | convolution fusion | flops 10920591360 | bytes 24790016 | tf_op jit(solution)/shard_map/dot_general | solution.py:278
  432.7 6.0 pad_maximum_fusion.2
  444.6 9.1 %pad_maximum_fusion = bf16[1024,4608]{1,0:T(8,128)(2,1)} fusion(bf16[1024,2304]{1,0:T(8,128)(2,1)} %get-tuple-element.143, bf16[1024,2304]{1,0:T(8,128)(2,1)} %get-tuple-element.141), kind=kLoop, calls=%fused_computation.3 | loop fusion | flops 18874368 | bytes 18874368 | tf_op jit(solution)/shard_map/concatenate | solution.py:403
  470.4 48.5 %attend_back.2 = bf16[3,288,2048]{2,1,0:T(8,128)(2,1)} custom-call(s32[8]{0:T(128)} %copy-done.10, s32[8]{0:T(128)} %copy-done.11, s32[1]{0:T(128)} %bitcast.3.place_ref, bf16[3,288,2048]{2,1,0:T(8,128)(2,1)} %bitcast.183, bf16[4,288,512]{2,1,0:T(8,128)(2,1)} %copy-done.3, f32[8,2048]{1,0:T(8,128)} %copy-done.15, s32[2048,128]{1,0:T(8,128)} %copy-done.5, ...), custom_call_target="tpu_custom_call" | custom-call | flops 16777216000 | bytes 9437184 | tf_op jit(solution)/shard_map/attend_back/pallas_call | solution.py:215
  518.9 4.6 convolution_convert_fusion.10
  538.7 3.5 collective-permute-done.19.rest_3_
  543.3 44.5 %attend_back.3 = bf16[3,288,2048]{2,1,0:T(8,128)(2,1)} custom-call(s32[8]{0:T(128)} %copy-done.9, s32[8]{0:T(128)} %copy-done.8, s32[1]{0:T(128)} %bitcast.3.place_ref, bf16[3,288,2048]{2,1,0:T(8,128)(2,1)} %bitcast.181, bf16[4,288,512]{2,1,0:T(8,128)(2,1)} %copy-done.2, f32[8,2048]{1,0:T(8,128)} %copy-done.14, s32[2048,128]{1,0:T(8,128)} %copy-done.4, ...), custom_call_target="tpu_custom_call" | custom-call | flops 16777216000 | bytes 9437184 | tf_op jit(solution)/shard_map/attend_back/pallas_call | solution.py:215
  590.3 14.8 %collective-permute-done.24 = bf16[144,1152]{1,0:T(8,128)(2,1)S(1)} collective-permute-done((bf16[144,1152]{1,0:T(8,128)(2,1)S(1)}, bf16[144,1152]{1,0:T(8,128)(2,1)S(1)}, u32[]{:S(2)}, u32[]{:S(2)}) %collective-permute-start.24) | collective-permute-done | bytes 331808 | tf_op jit(solution)/shard_map/ppermute | solution.py:299
  608.8 4.5 convolution_convert_fusion.6
  613.3 4.7 convolution_convert_fusion.5
  626.8 7.1 fusion.28
  634.0 8.9 %add_convert_fusion.5 = (bf16[1152,864]{1,0:T(8,128)(2,1)}, bf16[1152]{0:T(1024)(128)(2,1)S(1)}) fusion(f32[864]{0:T(1024)S(1)} %add.452, f32[1152]{0:T(1024)S(1)} %copy-done.63, f32[1152]{0:T(1024)S(1)} %copy-done.52, bf16[8,144,864]{2,1,0:T(8,128)(2,1)S(1)} %copy-done.37, f32[1152,864]{1,0:T(8,128)} %fusion.28, bf16[864,2048]{1,0:T(8,128)(2,1)S(1)} %bitcast.206, ...), kind=kOutput, calls=%fused_computation.102 | convolution fusion | flops 4103699456 | bytes 16235136 | tf_op jit(solution)/shard_map/dot_general | solution.py:278
  653.9 8.2 %fusion.147 = f32[1024,1152]{1,0:T(8,128)} fusion(bf16[1152,1152]{1,0:T(8,128)(2,1)} %all-gather.8.cloned.1.call-done, bf16[1024,4608]{1,0:T(8,128)(2,1)} %pad_maximum_fusion), kind=kOutput, calls=%fused_computation.205 | convolution fusion | flops 2717908992 | bytes 9732096 | tf_op jit(solution)/shard_map/dot_general | solution.py:278
  662.0 15.6 %collective-permute-done.30 = bf16[512,1152]{1,0:T(8,128)(2,1)} collective-permute-done((bf16[512,1152]{1,0:T(8,128)(2,1)}, bf16[512,1152]{1,0:T(8,128)(2,1)}, u32[]{:S(2)}, u32[]{:S(2)}) %collective-permute-start.30) | collective-permute-done | bytes 1179680 | tf_op jit(solution)/shard_map/ppermute | solution.py:299
  682.3 20.9 %collective-permute-done.26 = bf16[512,1152]{1,0:T(8,128)(2,1)S(1)} collective-permute-done((bf16[512,1152]{1,0:T(8,128)(2,1)}, bf16[512,1152]{1,0:T(8,128)(2,1)S(1)}, u32[]{:S(2)}, u32[]{:S(2)}) %collective-permute-start.26) | collective-permute-done | bytes 1179680 | tf_op jit(solution)/shard_map/ppermute | solution.py:299
  712.9 6.7 fusion.61
  719.6 8.3 %fusion.139 = f32[1024,1152]{1,0:T(8,128)} fusion(bf16[1152,1152]{1,0:T(8,128)(2,1)S(1)} %copy-done.71, bf16[1024,4608]{1,0:T(8,128)(2,1)} %pad_maximum_fusion), kind=kOutput, calls=%fused_computation.199 | convolution fusion | flops 2717908992 | bytes 9732096 | tf_op jit(solution)/shard_map/dot_general | solution.py:278
  727.9 5.2 fusion.145
  733.1 10.2 %add_add_fusion = f32[1024,1152]{1,0:T(8,128)} fusion(f32[1024,1152]{1,0:T(8,128)} %fusion.139, f32[1024,1152]{1,0:T(8,128)} %fusion.145, f32[1024,1152]{1,0:T(8,128)S(1)} %bitcast.188, f32[1024,1152]{1,0:T(8,128)} %fusion.147, f32[1152]{0:T(1024)S(1)} %add.461, bf16[1152,1152]{1,0:T(8,128)(2,1)} %copy-done.74, bf16[1024,4608]{1,0:T(8,128)(2,1)S(1)} %bitcast.190), kind=kOutput, calls=%fused_computation.85 | convolution fusion | flops 2723807232 | bytes 28614656 | tf_op jit(solution)/shard_map/dot_general | solution.py:278
  751.0 4.8 collective-permute-done.35
  758.0 5.5 collective-permute-done.43
  763.5 3.2 collective-permute-done.41
  772.2 4.2 collective-permute-done.34
  (468 shorter events, 180.4 us)
Async XLA Ops:
  7.2 124.6 %all-gather.18.cloned.1.call-start = ((), (), s32[]{:S(2)}) async-start(), calls=%async_computation.12 | async-start | bytes 2451456 | tf_op jit(solution)/shard_map/all_gather | solution.py:333
  15.7 210.3 %all-gather.8.cloned.1.call-start = ((), (), s32[]{:S(2)}) async-start(), calls=%async_computation.4 | async-start | bytes 2985984 | tf_op jit(solution)/shard_map/all_gather | solution.py:356
  16.6 209.4 %all-gather.10.cloned.1.call-start = ((), (), s32[]{:S(2)}) async-start(), calls=%async_computation.5 | async-start | bytes 2985984 | tf_op jit(solution)/shard_map/all_gather | solution.py:361
  17.4 230.6 %all-gather.14.cloned.1.call-start = ((), (), s32[]{:S(2)}) async-start(), calls=%async_computation.7 | async-start | bytes 5971968 | tf_op jit(solution)/shard_map/all_gather | solution.py:356
  19.9 244.9 %all-gather.12.cloned.1.call-start = ((), (), s32[]{:S(2)}) async-start(), calls=%async_computation.6 | async-start | bytes 5971968 | tf_op jit(solution)/shard_map/all_gather | solution.py:356
  21.5 29.2 %collective-permute-start = (bf16[512,1152]{1,0:T(8,128)(2,1)}, bf16[512,1152]{1,0:T(8,128)(2,1)}, u32[]{:S(2)}, u32[]{:S(2)}) collective-permute-start(bf16[512,1152]{1,0:T(8,128)(2,1)} %get-tuple-element.161), channel_id=1, source_target_pairs={{0,1},{1,0},{2,3},{3,2},{4,5},{5,4},{6,7},{7,6},{8,9},{9,8},{10,11... | collective-permute-start | bytes 3538952 | tf_op jit(solution)/shard_map/ppermute | solution.py:299
  23.0 53.0 %collective-permute-start.1 = (bf16[512,1152]{1,0:T(8,128)(2,1)}, bf16[512,1152]{1,0:T(8,128)(2,1)}, u32[]{:S(2)}, u32[]{:S(2)}) collective-permute-start(bf16[512,1152]{1,0:T(8,128)(2,1)} %get-tuple-element.161), channel_id=1, source_target_pairs={{0,2},{1,3},{2,0},{3,1},{4,6},{5,7},{6,4},{7,5},{8,10},{9,11},{10,... | collective-permute-start | bytes 3538952 | tf_op jit(solution)/shard_map/ppermute | solution.py:299
  24.6 51.5 %collective-permute-start.2 = (bf16[512,1152]{1,0:T(8,128)(2,1)}, bf16[512,1152]{1,0:T(8,128)(2,1)}, u32[]{:S(2)}, u32[]{:S(2)}) collective-permute-start(bf16[512,1152]{1,0:T(8,128)(2,1)} %get-tuple-element.161), channel_id=1, source_target_pairs={{0,3},{1,2},{2,1},{3,0},{4,7},{5,6},{6,5},{7,4},{8,11},{9,10},{10,... | collective-permute-start | bytes 3538952 | tf_op jit(solution)/shard_map/ppermute | solution.py:299
  25.9 351.7 %all-gather.16.cloned.1.call-start = ((), (), s32[]{:S(2)}) async-start(), calls=%async_computation.9 | async-start | bytes 2985984 | tf_op jit(solution)/shard_map/all_gather | solution.py:356
  76.1 29.9 %collective-permute-start.5 = (bf16[512,1152]{1,0:T(8,128)(2,1)}, bf16[512,1152]{1,0:T(8,128)(2,1)S(1)}, u32[]{:S(2)}, u32[]{:S(2)}) collective-permute-start(bf16[512,1152]{1,0:T(8,128)(2,1)} %get-tuple-element.72), channel_id=1, source_target_pairs={{0,3},{1,2},{2,1},{3,0},{4,7},{5,6},{6,5},{7,4},{8,11},{9,10},{10,... | collective-permute-start | bytes 3538952 | tf_op jit(solution)/shard_map/ppermute | solution.py:299
  77.6 51.5 %collective-permute-start.4 = (bf16[512,1152]{1,0:T(8,128)(2,1)}, bf16[512,1152]{1,0:T(8,128)(2,1)S(1)}, u32[]{:S(2)}, u32[]{:S(2)}) collective-permute-start(bf16[512,1152]{1,0:T(8,128)(2,1)} %get-tuple-element.72), channel_id=1, source_target_pairs={{0,2},{1,3},{2,0},{3,1},{4,6},{5,7},{6,4},{7,5},{8,10},{9,11},{10,... | collective-permute-start | bytes 3538952 | tf_op jit(solution)/shard_map/ppermute | solution.py:299
  78.8 51.5 %collective-permute-start.3 = (bf16[512,1152]{1,0:T(8,128)(2,1)}, bf16[512,1152]{1,0:T(8,128)(2,1)S(1)}, u32[]{:S(2)}, u32[]{:S(2)}) collective-permute-start(bf16[512,1152]{1,0:T(8,128)(2,1)} %get-tuple-element.72), channel_id=1, source_target_pairs={{0,1},{1,0},{2,3},{3,2},{4,5},{5,4},{6,7},{7,6},{8,9},{9,8},{10,11... | collective-permute-start | bytes 3538952 | tf_op jit(solution)/shard_map/ppermute | solution.py:299
  179.0 45.8 %collective-permute-start.7 = (bf16[288,512]{1,0:T(8,128)(2,1)}, bf16[288,512]{1,0:T(8,128)(2,1)}, u32[]{:S(2)}, u32[]{:S(2)}) collective-permute-start(bf16[288,512]{1,0:T(8,128)(2,1)} %get-tuple-element.200), channel_id=1, source_target_pairs={{0,1},{1,0},{2,3},{3,2},{4,5},{5,4},{6,7},{7,6},{8,9},{9,8},{10,11... | collective-permute-start | bytes 884744 | tf_op jit(solution)/shard_map/ppermute | solution.py:299
  179.9 46.1 %collective-permute-start.8 = (bf16[288,512]{1,0:T(8,128)(2,1)}, bf16[288,512]{1,0:T(8,128)(2,1)}, u32[]{:S(2)}, u32[]{:S(2)}) collective-permute-start(bf16[288,512]{1,0:T(8,128)(2,1)} %get-tuple-element.199), channel_id=1, source_target_pairs={{0,2},{1,3},{2,0},{3,1},{4,6},{5,7},{6,4},{7,5},{8,10},{9,11},{10,... | collective-permute-start | bytes 884744 | tf_op jit(solution)/shard_map/ppermute | solution.py:299
  181.0 45.0 %collective-permute-start.9 = (bf16[288,512]{1,0:T(8,128)(2,1)}, bf16[288,512]{1,0:T(8,128)(2,1)}, u32[]{:S(2)}, u32[]{:S(2)}) collective-permute-start(bf16[288,512]{1,0:T(8,128)(2,1)} %get-tuple-element.198), channel_id=1, source_target_pairs={{0,3},{1,2},{2,1},{3,0},{4,7},{5,6},{6,5},{7,4},{8,11},{9,10},{10,... | collective-permute-start | bytes 884744 | tf_op jit(solution)/shard_map/ppermute | solution.py:299
  223.7 15.8 %collective-permute-start.10 = (bf16[288,512]{1,0:T(8,128)(2,1)}, bf16[288,512]{1,0:T(8,128)(2,1)}, u32[]{:S(2)}, u32[]{:S(2)}) collective-permute-start(bf16[288,512]{1,0:T(8,128)(2,1)} %get-tuple-element.195), channel_id=1, source_target_pairs={{0,2},{1,3},{2,0},{3,1},{4,6},{5,7},{6,4},{7,5},{8,10},{9,11},{10,... | collective-permute-start | bytes 884744 | tf_op jit(solution)/shard_map/ppermute | solution.py:299
  224.8 14.7 %collective-permute-start.6 = (bf16[288,512]{1,0:T(8,128)(2,1)}, bf16[288,512]{1,0:T(8,128)(2,1)S(1)}, u32[]{:S(2)}, u32[]{:S(2)}) collective-permute-start(bf16[288,512]{1,0:T(8,128)(2,1)} %get-tuple-element.196), channel_id=1, source_target_pairs={{0,1},{1,0},{2,3},{3,2},{4,5},{5,4},{6,7},{7,6},{8,9},{9,8},{10,11... | collective-permute-start | bytes 884744 | tf_op jit(solution)/shard_map/ppermute | solution.py:299
  248.8 192.8 %reduce-scatter.7.cloned.1.call-start = ((), (), s32[]{:S(2)}) async-start(), calls=%async_computation.8 | async-start | bytes 11943936 | tf_op jit(solution)/shard_map/reduce_scatter | solution.py:422
  298.7 307.4 %reduce-scatter.9.cloned.1.call-start = ((), (), s32[]{:S(2)}) async-start(), calls=%async_computation.10 | async-start | bytes 11943936 | tf_op jit(solution)/shard_map/reduce_scatter | solution.py:447
  298.7 59.9 %collective-permute-start.12 = (bf16[1152,1152]{1,0:T(8,128)(2,1)}, bf16[1152,1152]{1,0:T(8,128)(2,1)S(1)}, u32[]{:S(2)}, u32[]{:S(2)}) collective-permute-start(bf16[1152,1152]{1,0:T(8,128)(2,1)} %all-gather.8.cloned.1.call-done), channel_id=1, source_target_pairs={{0,1},{1,0},{2,3},{3,2},{4,5},{5,4},{6,7},{7,6},{8,9},{9,8},{10,11... | collective-permute-start | bytes 7962632 | tf_op jit(solution)/shard_map/ppermute | solution.py:299
  299.8 65.0 %collective-permute-start.13 = (bf16[1152,1152]{1,0:T(8,128)(2,1)}, bf16[1152,1152]{1,0:T(8,128)(2,1)S(1)}, u32[]{:S(2)}, u32[]{:S(2)}) collective-permute-start(bf16[1152,1152]{1,0:T(8,128)(2,1)} %all-gather.8.cloned.1.call-done), channel_id=1, source_target_pairs={{0,2},{1,3},{2,0},{3,1},{4,6},{5,7},{6,4},{7,5},{8,10},{9,11},{10,... | collective-permute-start | bytes 7962632 | tf_op jit(solution)/shard_map/ppermute | solution.py:299
  402.4 39.1 %collective-permute-start.14 = (bf16[288,512]{1,0:T(8,128)(2,1)}, bf16[288,512]{1,0:T(8,128)(2,1)S(1)}, u32[]{:S(2)}, u32[]{:S(2)}) collective-permute-start(bf16[288,512]{1,0:T(8,128)(2,1)} %convolution_convert_fusion.17), channel_id=1, source_target_pairs={{0,1},{1,0},{2,3},{3,2},{4,5},{5,4},{6,7},{7,6},{8,9},{9,8},{10,11... | collective-permute-start | bytes 884744 | tf_op jit(solution)/shard_map/ppermute | solution.py:299
  404.6 36.9 %collective-permute-start.15 = (bf16[288,512]{1,0:T(8,128)(2,1)}, bf16[288,512]{1,0:T(8,128)(2,1)}, u32[]{:S(2)}, u32[]{:S(2)}) collective-permute-start(bf16[288,512]{1,0:T(8,128)(2,1)} %convolution_convert_fusion.16), channel_id=1, source_target_pairs={{0,2},{1,3},{2,0},{3,1},{4,6},{5,7},{6,4},{7,5},{8,10},{9,11},{10,... | collective-permute-start | bytes 884744 | tf_op jit(solution)/shard_map/ppermute | solution.py:299
  407.1 34.4 %collective-permute-start.16 = (bf16[288,512]{1,0:T(8,128)(2,1)}, bf16[288,512]{1,0:T(8,128)(2,1)}, u32[]{:S(2)}, u32[]{:S(2)}) collective-permute-start(bf16[288,512]{1,0:T(8,128)(2,1)} %convolution_convert_fusion.15), channel_id=1, source_target_pairs={{0,3},{1,2},{2,1},{3,0},{4,7},{5,6},{6,5},{7,4},{8,11},{9,10},{10,... | collective-permute-start | bytes 884744 | tf_op jit(solution)/shard_map/ppermute | solution.py:299
  442.2 208.6 %reduce-scatter.11.cloned.1.call-start = ((), (), s32[]{:S(2)}) async-start(), calls=%async_computation.11 | async-start | bytes 2985984 | tf_op jit(solution)/shard_map/reduce_scatter | solution.py:468
  457.1 78.9 %collective-permute-start.17 = (bf16[288,512]{1,0:T(8,128)(2,1)}, bf16[288,512]{1,0:T(8,128)(2,1)}, u32[]{:S(2)}, u32[]{:S(2)}) collective-permute-start(bf16[288,512]{1,0:T(8,128)(2,1)} %convolution_convert_fusion.13), channel_id=1, source_target_pairs={{0,1},{1,0},{2,3},{3,2},{4,5},{5,4},{6,7},{7,6},{8,9},{9,8},{10,11... | collective-permute-start | bytes 884744 | tf_op jit(solution)/shard_map/ppermute | solution.py:299
  460.4 76.9 %collective-permute-start.18 = (bf16[288,512]{1,0:T(8,128)(2,1)}, bf16[288,512]{1,0:T(8,128)(2,1)}, u32[]{:S(2)}, u32[]{:S(2)}) collective-permute-start(bf16[288,512]{1,0:T(8,128)(2,1)} %convolution_convert_fusion.12), channel_id=1, source_target_pairs={{0,2},{1,3},{2,0},{3,1},{4,6},{5,7},{6,4},{7,5},{8,10},{9,11},{10,... | collective-permute-start | bytes 884744 | tf_op jit(solution)/shard_map/ppermute | solution.py:299
  466.9 64.4 %collective-permute-start.22 = (bf16[144,1152]{1,0:T(8,128)(2,1)}, bf16[144,1152]{1,0:T(8,128)(2,1)S(1)}, u32[]{:S(2)}, u32[]{:S(2)}) collective-permute-start(bf16[144,1152]{1,0:T(8,128)(2,1)} %get-tuple-element.175), channel_id=1, source_target_pairs={{0,3},{1,2},{2,1},{3,0},{4,7},{5,6},{6,5},{7,4},{8,11},{9,10},{10,... | collective-permute-start | bytes 995336 | tf_op jit(solution)/shard_map/ppermute | solution.py:299
  468.3 64.2 %collective-permute-start.21 = (bf16[144,1152]{1,0:T(8,128)(2,1)}, bf16[144,1152]{1,0:T(8,128)(2,1)S(1)}, u32[]{:S(2)}, u32[]{:S(2)}) collective-permute-start(bf16[144,1152]{1,0:T(8,128)(2,1)} %get-tuple-element.176), channel_id=1, source_target_pairs={{0,2},{1,3},{2,0},{3,1},{4,6},{5,7},{6,4},{7,5},{8,10},{9,11},{10,... | collective-permute-start | bytes 995336 | tf_op jit(solution)/shard_map/ppermute | solution.py:299
  468.9 65.3 %collective-permute-start.20 = (bf16[144,1152]{1,0:T(8,128)(2,1)S(1)}, bf16[144,1152]{1,0:T(8,128)(2,1)S(1)}, u32[]{:S(2)}, u32[]{:S(2)}) collective-permute-start(bf16[144,1152]{1,0:T(8,128)(2,1)S(1)} %get-tuple-element.174), channel_id=1, source_target_pairs={{0,1},{1,0},{2,3},{3,2},{4,5},{5,4},{6,7},{7,6},{8,9},{9,8},{10,11... | collective-permute-start | bytes 995336 | tf_op jit(solution)/shard_map/ppermute | solution.py:299
  532.5 149.8 %collective-permute-start.28 = (bf16[512,1152]{1,0:T(8,128)(2,1)}, bf16[512,1152]{1,0:T(8,128)(2,1)}, u32[]{:S(2)}, u32[]{:S(2)}) collective-permute-start(bf16[512,1152]{1,0:T(8,128)(2,1)} %convolution_convert_fusion.7), channel_id=1, source_target_pairs={{0,3},{1,2},{2,1},{3,0},{4,7},{5,6},{6,5},{7,4},{8,11},{9,10},{10,... | collective-permute-start | bytes 3538952 | tf_op jit(solution)/shard_map/ppermute | solution.py:299
  534.3 148.1 %collective-permute-start.27 = (bf16[512,1152]{1,0:T(8,128)(2,1)}, bf16[512,1152]{1,0:T(8,128)(2,1)}, u32[]{:S(2)}, u32[]{:S(2)}) collective-permute-start(bf16[512,1152]{1,0:T(8,128)(2,1)} %convolution_convert_fusion.8), channel_id=1, source_target_pairs={{0,2},{1,3},{2,0},{3,1},{4,6},{5,7},{6,4},{7,5},{8,10},{9,11},{10,... | collective-permute-start | bytes 3538952 | tf_op jit(solution)/shard_map/ppermute | solution.py:299
  536.0 54.3 %collective-permute-start.25 = (bf16[144,1152]{1,0:T(8,128)(2,1)S(1)}, bf16[144,1152]{1,0:T(8,128)(2,1)S(1)}, u32[]{:S(2)}, u32[]{:S(2)}) collective-permute-start(bf16[144,1152]{1,0:T(8,128)(2,1)S(1)} %add_convert_fusion.7), channel_id=1, source_target_pairs={{0,3},{1,2},{2,1},{3,0},{4,7},{5,6},{6,5},{7,4},{8,11},{9,10},{10,... | collective-permute-start | bytes 995336 | tf_op jit(solution)/shard_map/ppermute | solution.py:299
  537.3 67.7 %collective-permute-start.24 = (bf16[144,1152]{1,0:T(8,128)(2,1)S(1)}, bf16[144,1152]{1,0:T(8,128)(2,1)S(1)}, u32[]{:S(2)}, u32[]{:S(2)}) collective-permute-start(bf16[144,1152]{1,0:T(8,128)(2,1)S(1)} %add_convert_fusion.7), channel_id=1, source_target_pairs={{0,2},{1,3},{2,0},{3,1},{4,6},{5,7},{6,4},{7,5},{8,10},{9,11},{10,... | collective-permute-start | bytes 995336 | tf_op jit(solution)/shard_map/ppermute | solution.py:299
  542.9 62.1 %collective-permute-start.23 = (bf16[144,1152]{1,0:T(8,128)(2,1)S(1)}, bf16[144,1152]{1,0:T(8,128)(2,1)S(1)}, u32[]{:S(2)}, u32[]{:S(2)}) collective-permute-start(bf16[144,1152]{1,0:T(8,128)(2,1)S(1)} %add_convert_fusion.7), channel_id=1, source_target_pairs={{0,1},{1,0},{2,3},{3,2},{4,5},{5,4},{6,7},{7,6},{8,9},{9,8},{10,11... | collective-permute-start | bytes 995336 | tf_op jit(solution)/shard_map/ppermute | solution.py:299
  613.3 153.8 %reduce-scatter.13.cloned.1.call-start = ((), (), s32[]{:S(2)}) async-start(), calls=%async_computation.13 | async-start | bytes 2451456
  623.2 30.1 %collective-permute-start.31 = (bf16[512,1152]{1,0:T(8,128)(2,1)}, bf16[512,1152]{1,0:T(8,128)(2,1)}, u32[]{:S(2)}, u32[]{:S(2)}) collective-permute-start(bf16[512,1152]{1,0:T(8,128)(2,1)} %convolution_convert_fusion.3), channel_id=1, source_target_pairs={{0,3},{1,2},{2,1},{3,0},{4,7},{5,6},{6,5},{7,4},{8,11},{9,10},{10,... | collective-permute-start | bytes 3538952 | tf_op jit(solution)/shard_map/ppermute | solution.py:299
  624.9 52.7 %collective-permute-start.30 = (bf16[512,1152]{1,0:T(8,128)(2,1)}, bf16[512,1152]{1,0:T(8,128)(2,1)}, u32[]{:S(2)}, u32[]{:S(2)}) collective-permute-start(bf16[512,1152]{1,0:T(8,128)(2,1)} %convolution_convert_fusion.4), channel_id=1, source_target_pairs={{0,2},{1,3},{2,0},{3,1},{4,6},{5,7},{6,4},{7,5},{8,10},{9,11},{10,... | collective-permute-start | bytes 3538952 | tf_op jit(solution)/shard_map/ppermute | solution.py:299
  625.2 54.1 %collective-permute-start.29 = (bf16[512,1152]{1,0:T(8,128)(2,1)}, bf16[512,1152]{1,0:T(8,128)(2,1)}, u32[]{:S(2)}, u32[]{:S(2)}) collective-permute-start(bf16[512,1152]{1,0:T(8,128)(2,1)} %convolution_convert_fusion.5), channel_id=1, source_target_pairs={{0,1},{1,0},{2,3},{3,2},{4,5},{5,4},{6,7},{7,6},{8,9},{9,8},{10,11... | collective-permute-start | bytes 3538952 | tf_op jit(solution)/shard_map/ppermute | solution.py:299
  653.3 49.9 %collective-permute-start.26 = (bf16[512,1152]{1,0:T(8,128)(2,1)}, bf16[512,1152]{1,0:T(8,128)(2,1)S(1)}, u32[]{:S(2)}, u32[]{:S(2)}) collective-permute-start(bf16[512,1152]{1,0:T(8,128)(2,1)} %convolution_convert_fusion.9), channel_id=1, source_target_pairs={{0,1},{1,0},{2,3},{3,2},{4,5},{5,4},{6,7},{7,6},{8,9},{9,8},{10,11... | collective-permute-start | bytes 3538952 | tf_op jit(solution)/shard_map/ppermute | solution.py:299
  677.6 72.0 %collective-permute-start.37 = (bf16[144,1152]{1,0:T(8,128)(2,1)}, bf16[144,1152]{1,0:T(8,128)(2,1)}, u32[]{:S(2)}, u32[]{:S(2)}) collective-permute-start(bf16[144,1152]{1,0:T(8,128)(2,1)} %reduce-scatter.11.cloned.1.call-done), channel_id=1, source_target_pairs={{0,3},{1,2},{2,1},{3,0},{4,7},{5,6},{6,5},{7,4},{8,11},{9,10},{10,... | collective-permute-start | bytes 995336 | tf_op jit(solution)/shard_map/ppermute | solution.py:299
  679.3 71.7 %collective-permute-start.36 = (bf16[144,1152]{1,0:T(8,128)(2,1)}, bf16[144,1152]{1,0:T(8,128)(2,1)}, u32[]{:S(2)}, u32[]{:S(2)}) collective-permute-start(bf16[144,1152]{1,0:T(8,128)(2,1)} %reduce-scatter.11.cloned.1.call-done), channel_id=1, source_target_pairs={{0,2},{1,3},{2,0},{3,1},{4,6},{5,7},{6,4},{7,5},{8,10},{9,11},{10,... | collective-permute-start | bytes 995336 | tf_op jit(solution)/shard_map/ppermute | solution.py:299
  709.3 35.6 %collective-permute-start.40 = (bf16[144,1152]{1,0:T(8,128)(2,1)S(1)}, bf16[144,1152]{1,0:T(8,128)(2,1)S(1)}, u32[]{:S(2)}, u32[]{:S(2)}) collective-permute-start(bf16[144,1152]{1,0:T(8,128)(2,1)S(1)} %get-tuple-element.168), channel_id=1, source_target_pairs={{0,3},{1,2},{2,1},{3,0},{4,7},{5,6},{6,5},{7,4},{8,11},{9,10},{10,... | collective-permute-start | bytes 995336 | tf_op jit(solution)/shard_map/ppermute | solution.py:299
  710.5 35.8 %collective-permute-start.39 = (bf16[144,1152]{1,0:T(8,128)(2,1)S(1)}, bf16[144,1152]{1,0:T(8,128)(2,1)S(1)}, u32[]{:S(2)}, u32[]{:S(2)}) collective-permute-start(bf16[144,1152]{1,0:T(8,128)(2,1)S(1)} %get-tuple-element.169), channel_id=1, source_target_pairs={{0,2},{1,3},{2,0},{3,1},{4,6},{5,7},{6,4},{7,5},{8,10},{9,11},{10,... | collective-permute-start | bytes 995336 | tf_op jit(solution)/shard_map/ppermute | solution.py:299
  712.2 34.1 %collective-permute-start.38 = (bf16[144,1152]{1,0:T(8,128)(2,1)S(1)}, bf16[144,1152]{1,0:T(8,128)(2,1)S(1)}, u32[]{:S(2)}, u32[]{:S(2)}) collective-permute-start(bf16[144,1152]{1,0:T(8,128)(2,1)S(1)} %get-tuple-element.167), channel_id=1, source_target_pairs={{0,1},{1,0},{2,3},{3,2},{4,5},{5,4},{6,7},{7,6},{8,9},{9,8},{10,11... | collective-permute-start | bytes 995336 | tf_op jit(solution)/shard_map/ppermute | solution.py:299
  747.4 16.1 %collective-permute-start.43 = (bf16[144,1152]{1,0:T(8,128)(2,1)S(1)}, bf16[144,1152]{1,0:T(8,128)(2,1)S(1)}, u32[]{:S(2)}, u32[]{:S(2)}) collective-permute-start(bf16[144,1152]{1,0:T(8,128)(2,1)S(1)} %add_convert_fusion.6), channel_id=1, source_target_pairs={{0,3},{1,2},{2,1},{3,0},{4,7},{5,6},{6,5},{7,4},{8,11},{9,10},{10,... | collective-permute-start | bytes 995336 | tf_op jit(solution)/shard_map/ppermute | solution.py:299
  748.8 14.7 %collective-permute-start.42 = (bf16[144,1152]{1,0:T(8,128)(2,1)S(1)}, bf16[144,1152]{1,0:T(8,128)(2,1)S(1)}, u32[]{:S(2)}, u32[]{:S(2)}) collective-permute-start(bf16[144,1152]{1,0:T(8,128)(2,1)S(1)} %add_convert_fusion.6), channel_id=1, source_target_pairs={{0,2},{1,3},{2,0},{3,1},{4,6},{5,7},{6,4},{7,5},{8,10},{9,11},{10,... | collective-permute-start | bytes 995336 | tf_op jit(solution)/shard_map/ppermute | solution.py:299
  749.7 17.0 %collective-permute-start.41 = (bf16[144,1152]{1,0:T(8,128)(2,1)S(1)}, bf16[144,1152]{1,0:T(8,128)(2,1)S(1)}, u32[]{:S(2)}, u32[]{:S(2)}) collective-permute-start(bf16[144,1152]{1,0:T(8,128)(2,1)S(1)} %add_convert_fusion.6), channel_id=1, source_target_pairs={{0,1},{1,0},{2,3},{3,2},{4,5},{5,4},{6,7},{7,6},{8,9},{9,8},{10,11... | collective-permute-start | bytes 995336 | tf_op jit(solution)/shard_map/ppermute | solution.py:299
  (100 other events, 1749.9 us)
Sparse Core Ops, SparseCore 0:
  15.8 30.9 all-gather.17
  49.0 32.9 all-gather.7
  83.6 33.0 all-gather.9
  118.8 54.4 all-gather.13
  175.4 55.2 all-gather.11
  248.9 34.5 all-gather.15
  298.8 108.8 reduce-scatter.6
  441.7 105.9 reduce-scatter.8
  613.4 32.7 reduce-scatter.10
  708.2 34.0 reduce-scatter.12
